TPU v7x, 256 devices: a whole 4x4x8 slice. The times are simulated.
256 devices in a mesh: row: 32 (over x_hi, z, core), col: 8 (over x_lo, y).
Axes of the slice: x: 4 (x_hi: 2, x_lo: 2; x = x_hi * 2 + x_lo), y: 4, z: 8, core: 2. Of those that a mesh axis runs over, the one named last changes fastest.
Arguments:
- occupied_waves: bfloat16 [1024, 32768], P('row', 'col'), may hold values from -6 to 6
- virtual_waves: bfloat16 [512, 32768], P('row', 'col'), may hold values from -6 to 6
- occupied_decay: float32 [1024], replicated, may hold values from 0.02 to 1
- virtual_decay: float32 [512], replicated, may hold values from 0.02 to 1
Outputs:
- spectrum_real: float32 [1024, 32, 1024], P('row', 'col')
- spectrum_imaginary: float32 [1024, 32, 1024], P('row', 'col')
All inputs are finite; a program needn't handle non-finite values.
Results may differ from a plain program's by a relative error of at most 0.0041.
Values may be sent and summed in bfloat16 or wider, within the bound.
No kernel may reach another device: no remote copies, remote signals or barrier semaphores. Data moves between devices by JAX's collectives and lax.ppermute only.
A program may use at most 64 MiB of HBM per device.

v0:
```python
import math

import jax
import jax.numpy as jnp
import numpy as np
from jax import lax
from jax.experimental import pallas as pl
from jax.experimental.pallas import tpu as pltpu
from jax.sharding import Mesh, PartitionSpec as P


NOCC = 1024
NVIR = 512
NGRID = 32768
POLAR_FACTOR = -1.0 / math.sqrt(NOCC * NVIR)
NORMAL = 1.0 / math.sqrt(NGRID)
Z = ("z2", "z1", "z0")
Y = ("y1", "y0")
ROW = ("xh", *Z, "c")
COL = ("xl", *Y)
FINE = ROW + COL
LAST = ("z1", "xl", "y0", "z2", "xh", "y1")
BF16 = jnp.bfloat16
F32 = jnp.float32
LIMIT = 16 * 1024 * 1024


def split_table(table):
    high = table.astype(np.float32).astype(jnp.bfloat16)
    low = (table - high.astype(np.float64)).astype(np.float32).astype(jnp.bfloat16)
    return high, low


def rotation(phase):
    cosine, sine = np.cos(phase), np.sin(phase)
    return np.array([[cosine, sine], [-sine, cosine]])


def c_table():
    kc = np.arange(32).reshape(8, 4)
    turn = rotation(2 * np.pi * (kc[..., None] * np.arange(32) % 32) / 32)[:, 0]
    full = np.einsum("pjic,bd->ijpbdc", turn, np.eye(8))
    return split_table(full.reshape(512, 256))


def a_table():
    ka = np.arange(32)
    turn = rotation(2 * np.pi * (ka[:, None] * ka[None, :] % 32) / 32)
    turn = turn.reshape(2, 2, 8, 4, 8, 4)
    full = np.einsum("pqghck,bd->ghpbkcqd", turn, np.eye(8))
    return split_table(full.reshape(512, 512))


def b_table():
    kb = np.arange(32)
    turn = rotation(2 * np.pi * (kb[:, None] * kb[None, :] % 32) / 32) * NORMAL
    turn = turn.reshape(2, 2, 32, 4, 8)
    full = np.einsum("pqkBb,hj->Bhqbpjk", turn, np.eye(4))
    return split_table(full.reshape(256, 256))


def dot(a, b):
    return lax.dot_general(a, b, (((1,), (0,)), ((), ())), preferred_element_type=F32)


def prepare_kernel(place_ref, occ_decay_ref, vir_decay_ref, occ_ref, vir_ref, out_ref):
    row = place_ref[0]

    def column(decay_ref, count):
        index = lax.broadcasted_iota(jnp.int32, (count, 128), 0)
        out = jnp.zeros((count, 128), F32)
        for i in range(count):
            out = jnp.where(index == i, decay_ref[row * count + i], out)
        return out

    def scaled_tiles(ref, decay):
        tiles = [ref[:, 128 * t : 128 * (t + 1)].astype(F32) * decay for t in range(8)]
        return [
            [
                jnp.concatenate(
                    [tiles[4 * t + u][:, 32 * kind : 32 * (kind + 1)] for u in range(4)], axis=1
                )
                for kind in range(4)
            ]
            for t in range(2)
        ]

    occ = scaled_tiles(occ_ref, column(occ_decay_ref, 32))
    vir = scaled_tiles(vir_ref, column(vir_decay_ref, 16))
    for xl in range(2):
        for y1 in range(2):
            for t in range(2):
                for kind in range(4):
                    group = 2 * xl + y1
                    piece = jnp.concatenate(
                        [
                            occ[t][kind][8 * group : 8 * (group + 1)],
                            vir[t][kind][8 * y1 : 8 * (y1 + 1)],
                        ],
                        axis=0,
                    )
                    out_ref[4 * xl + 2 * y1 + t, kind] = piece.astype(BF16)


def prepare(place, occ_decay, vir_decay, occ, vir):
    smem = pl.BlockSpec(memory_space=pltpu.SMEM)
    return pl.pallas_call(
        prepare_kernel,
        grid=(1,),
        out_shape=jax.ShapeDtypeStruct((8, 4, 16, 128), BF16),
        in_specs=[
            smem,
            smem,
            smem,
            pl.BlockSpec((32, 1024), lambda i: (0, 0)),
            pl.BlockSpec((16, 1024), lambda i: (0, 0)),
        ],
        out_specs=pl.BlockSpec((8, 4, 16, 128), lambda i: (0, 0, 0, 0)),
        name="prepare",
    )(place, occ_decay, vir_decay, occ, vir)


def pack_kernel(occ_ref, vir_ref, rows_ref, out_ref):
    for p in range(32):
        out_ref[p, 0:32, :] = occ_ref[:, 128 * p : 128 * (p + 1)]
        out_ref[p, 32:48, :] = vir_ref[:, 128 * p : 128 * (p + 1)]
        out_ref[p, 48:64, :] = rows_ref[0, p % 4]


def pack(occ, vir, rows):
    vmem = pl.BlockSpec(memory_space=pltpu.VMEM)
    return pl.pallas_call(
        pack_kernel,
        out_shape=jax.ShapeDtypeStruct((32, 64, 128), BF16),
        in_specs=[vmem] * 3,
        out_specs=vmem,
        compiler_params=pltpu.CompilerParams(vmem_limit_bytes=LIMIT),
        name="pack",
    )(occ, vir, rows)


def polar_kernel(place_ref, *refs):
    points, near, far = refs[:4], refs[4:8], refs[8:10]
    high_ref, low_ref, out_ref, polar_ref, occ_ref, vir_ref = refs[10:]
    core, z0, xl, y = place_ref[0], place_ref[1], place_ref[2], place_ref[3]
    for step in range(4):
        chunk = lax.rem(y + 4 - step, 4)
        y1, y0 = lax.div(chunk, 2), lax.rem(chunk, 2)
        lanes = pl.ds(pl.multiple_of(128 * y0, 128), 128)

        def rows(group):
            return pl.ds(pl.multiple_of(256 * group, 256), 256)

        occ_ref[rows(2 * xl + y1), lanes] = near[step][:256]
        occ_ref[rows(2 * (1 - xl) + y1), lanes] = far[step // 2][
            256 * (step % 2) : 256 * (step % 2 + 1)
        ]
        vir_ref[rows(y1), lanes] = near[step][256:]
    for k, ref in enumerate(points):
        place = 2 * (z0 if k < 2 else 1 - z0) + (core if k % 2 == 0 else 1 - core)
        green_occ = dot(ref[:1024].T, occ_ref[...])
        green_vir = dot(ref[1024:].T, vir_ref[...])
        polar_ref[pl.ds(pl.multiple_of(128 * place, 128), 128), :] = (
            green_occ * green_vir * POLAR_FACTOR
        )
    for half in range(2):
        polar = polar_ref[256 * half : 256 * (half + 1), :]
        polar_high = polar.astype(BF16)
        polar_low = (polar - polar_high.astype(F32)).astype(BF16)
        spectrum = (
            dot(high_ref[...], polar_high)
            + dot(high_ref[...], polar_low)
            + dot(low_ref[...], polar_high)
        )
        for m in range(8):
            pieces = [spectrum[128 * i : 128 * (i + 1), 32 * m : 32 * (m + 1)] for i in range(4)]
            message = jnp.concatenate(pieces, axis=1).astype(BF16)
            out_ref[m, :, half] = message.reshape(8, 16, 128)


def polar_messages(place, *arrays):
    high, low = c_table()
    vmem = pl.BlockSpec(memory_space=pltpu.VMEM)
    return pl.pallas_call(
        polar_kernel,
        out_shape=jax.ShapeDtypeStruct((8, 8, 2, 16, 128), BF16),
        in_specs=[pl.BlockSpec(memory_space=pltpu.SMEM)] + [vmem] * 12,
        out_specs=vmem,
        scratch_shapes=[
            pltpu.VMEM((512, 256), F32),
            pltpu.VMEM((1024, 256), BF16),
            pltpu.VMEM((512, 256), BF16),
        ],
        compiler_params=pltpu.CompilerParams(vmem_limit_bytes=LIMIT),
        name="polar",
    )(place, *arrays, high, low)


def finish_kernel(x_ref, a_high_ref, a_low_ref, b_high_ref, b_low_ref, real_ref, imag_ref):
    planes = []
    for block in range(4):
        zb, half = divmod(block, 2)
        x = jnp.concatenate(
            [x_ref[2 * k + zb, :, half].reshape(128, 128) for k in range(4)], axis=0
        )
        planes.append(dot(a_high_ref[...], x) + dot(a_low_ref[...], x))
    for g in range(8):
        z = jnp.concatenate([plane[64 * g : 64 * (g + 1)] for plane in planes], axis=0).T
        z_high = z.astype(BF16)
        z_low = (z - z_high.astype(F32)).astype(BF16)
        out = (
            dot(z_high, b_high_ref[...])
            + dot(z_high, b_low_ref[...])
            + dot(z_low, b_high_ref[...])
        )
        for i in range(4):
            real_ref[:, i, 128 * g : 128 * (g + 1)] = out[32 * i : 32 * (i + 1), :128]
            imag_ref[:, i, 128 * g : 128 * (g + 1)] = out[32 * i : 32 * (i + 1), 128:]


def finish(x):
    vmem = pl.BlockSpec(memory_space=pltpu.VMEM)
    shape = jax.ShapeDtypeStruct((32, 4, 1024), F32)
    return pl.pallas_call(
        finish_kernel,
        out_shape=(shape, shape),
        in_specs=[vmem] * 5,
        out_specs=(vmem, vmem),
        compiler_params=pltpu.CompilerParams(vmem_limit_bytes=LIMIT),
        name="finish",
    )(x, *a_table(), *b_table())


def join_kernel(first_ref, second_ref, out_ref):
    out_ref[:256] = first_ref[:256]
    out_ref[256:] = second_ref[:256]


def join(first, second):
    vmem = pl.BlockSpec(memory_space=pltpu.VMEM)
    return pl.pallas_call(
        join_kernel,
        out_shape=jax.ShapeDtypeStruct((512, 128), BF16),
        in_specs=[vmem, vmem],
        out_specs=vmem,
        compiler_params=pltpu.CompilerParams(vmem_limit_bytes=LIMIT),
        name="join",
    )(first, second)


def fence(x):
    anywhere = pl.BlockSpec(memory_space=pl.ANY)
    return pl.pallas_call(
        lambda in_ref, out_ref: None,
        out_shape=jax.ShapeDtypeStruct(x.shape, x.dtype),
        in_specs=[anywhere],
        out_specs=anywhere,
        input_output_aliases={0: 0},
        compiler_params=pltpu.CompilerParams(vmem_limit_bytes=LIMIT),
        name="fence",
    )(x)


def shift(x, axes, count, by):
    return lax.ppermute(x, axes, [(i, (i + by) % count) for i in range(count)])


def swap(x, axis):
    return lax.ppermute(x, axis, [(0, 1), (1, 0)])


def body(occ, vir, occ_decay, vir_decay):
    row = lax.axis_index(ROW).astype(jnp.int32).reshape(1)
    place = jnp.stack([lax.axis_index(a).astype(jnp.int32) for a in ("c", "z0", "xl", Y)])
    scattered = lax.all_to_all(prepare(row, occ_decay, vir_decay, occ, vir), COL, 0, 0, tiled=True)
    arrived = lax.all_to_all(pack(occ, vir, scattered), ROW, 0, 0, tiled=True)

    near = jnp.concatenate(
        [arrived[:, 48:56].reshape(256, 128), arrived[:, 56:].reshape(256, 128)], axis=0
    )
    near = [near]
    for by in (1, 2, 3):
        near.append(shift(near[0], Y, 4, by))
    up = join(near[0], near[1])
    up = shift(up, ("xh", "xl"), 4, 1)
    down = join(near[2], near[3])
    down = shift(down, ("xh", "xl"), 4, -1)

    def by_group(part, count):
        part = part.reshape(32, count, 8, 128)
        return jnp.transpose(part, (1, 0, 2, 3)).reshape(256 * count, 128)

    own = jnp.concatenate([by_group(arrived[:, :32], 4), by_group(arrived[:, 32:48], 2)], axis=0)
    across = swap(own, "z0")
    beside = swap(own, "c")
    beside = fence(beside)
    opposite = swap(across, "c")
    points = (own, beside, across, opposite)
    messages = polar_messages(place, *points, *near, up, down)

    names = ("xh", "z2", "z1", *COL)
    bits = messages.reshape(2, 2, 2, 2, 2, 2, 32, 128)
    sent = jnp.transpose(bits, (*(names.index(a) for a in LAST), 6, 7)).reshape(64, 32, 128)
    received = lax.all_to_all(sent, LAST, 0, 0, tiled=True).reshape(bits.shape)
    received = jnp.transpose(received, (*(LAST.index(a) for a in names), 6, 7))
    return finish(received.reshape(8, 8, 2, 16, 128))


def solution(mesh):
    fine = Mesh(mesh.devices.reshape((2,) * len(FINE)), FINE)
    return jax.shard_map(
        body,
        mesh=fine,
        in_specs=(P(ROW, COL), P(ROW, COL), P(), P()),
        out_specs=(P(ROW, COL, None), P(ROW, COL, None)),
        check_vma=False,
    )
```

profile of v0, /device:TPU:32, one launch (start us, length us, event | category | flops | bytes accessed | tf_op | source)
XLA Modules:
  0.0 104.9 jit_solution(14316859433900838449)
XLA Ops:
  0.6 0.0 copy-start.3
  0.7 1.7 %prepare.1 = bf16[8,4,16,128]{3,2,1,0:T(8,128)(2,1)} custom-call(s32[1]{0:T(128)} %bitcast.4.place_ref, f32[1024]{0:T(1024)} %occ_decay_ref.1, f32[512]{0:T(512)} %vir_decay_ref.1, bf16[32,4096]{1,0:T(8,128)(2,1)} %occ_ref.3, bf16[16,4096]{1,0:T(8,128)(2,1)} %vir_ref.3), custom_call_target="tpu_custom_call" | custom-call | tf_op jit(solution)/shard_map/prepare/pallas_call | solution.py:107
  2.4 0.0 copy-start
  2.4 12.1 %all_to_all.15.rows_ref = bf16[8,4,16,128]{3,2,1,0:T(8,128)(2,1)S(1)} all-to-all(bf16[8,4,16,128]{3,2,1,0:T(8,128)(2,1)} %prepare.1), channel_id=1, replica_groups=mesh['xh'=2,'z2'=2,'z1'=2,'z0'=2,'c'=2,'xl'=2,'y1'=2,'y0'=2] {'xl','y1',..., dimensions={0} | all-to-all | bytes 262144 | tf_op jit(solution)/shard_map/all_to_all | solution.py:275
  14.5 0.0 copy-done.3
  14.5 0.0 copy-done
  14.5 0.1 pack.1
  14.6 29.9 %all_to_all.16 = bf16[32,64,128]{2,1,0:T(8,128)(2,1)S(1)} all-to-all(bf16[32,64,128]{2,1,0:T(8,128)(2,1)S(1)} %pack.1), channel_id=1, replica_groups=mesh['xh'=2,'z2'=2,'z1'=2,'z0'=2,'c'=2,'xl'=2,'y1'=2,'y0'=2] {'xh','z2',..., dimensions={0} | all-to-all | bytes 1048576 | tf_op jit(solution)/shard_map/all_to_all | solution.py:276
  44.7 1.0 collective-permute-start.1
  45.7 0.0 collective-permute-start
  45.7 8.9 %collective-permute-done.1.refs_2_ = bf16[1536,128]{1,0:T(8,128)(2,1)S(1)} collective-permute-done((bf16[1536,128]{1,0:T(8,128)(2,1)S(1)}, bf16[1536,128]{1,0:T(8,128)(2,1)S(1)}, u32[]{:S(2)}, u32[]{:S(2)}) %collective-permute-start.1) | collective-permute-done | bytes 393248 | tf_op jit(solution)/shard_map/ppermute | solution.py:269
  54.5 0.0 collective-permute-start.2
  54.6 1.2 %collective-permute-start.5 = (bf16[512,128]{1,0:T(8,128)(2,1)S(1)}, bf16[512,128]{1,0:T(8,128)(2,1)S(1)}, u32[]{:S(2)}, u32[]{:S(2)}) collective-permute-start(bf16[512,128]{1,0:T(8,128)(2,1)S(1)} %pad_maximum_fusion.1.first_ref.refs_4_), channel_id=1, source_target_pairs={{0,3},{1,0},{2,1},{3,2},{4,7},{5,4},{6,5},{7,6},{8,11},{9,8},{10,9... | collective-permute-start | bytes 393224 | tf_op jit(solution)/shard_map/ppermute | solution.py:265
  55.8 1.5 %collective-permute-start.4 = (bf16[512,128]{1,0:T(8,128)(2,1)S(1)}, bf16[512,128]{1,0:T(8,128)(2,1)S(1)}, u32[]{:S(2)}, u32[]{:S(2)}) collective-permute-start(bf16[512,128]{1,0:T(8,128)(2,1)S(1)} %pad_maximum_fusion.1.first_ref.refs_4_), channel_id=1, source_target_pairs={{0,2},{1,3},{2,0},{3,1},{4,6},{5,7},{6,4},{7,5},{8,10},{9,11},{10,... | collective-permute-start | bytes 393224 | tf_op jit(solution)/shard_map/ppermute | solution.py:265
  57.2 0.0 collective-permute-start.3
  57.2 3.8 %collective-permute-done.5.second_ref.refs_7_ = bf16[512,128]{1,0:T(8,128)(2,1)S(1)} collective-permute-done((bf16[512,128]{1,0:T(8,128)(2,1)S(1)}, bf16[512,128]{1,0:T(8,128)(2,1)S(1)}, u32[]{:S(2)}, u32[]{:S(2)}) %collective-permute-start.5) | collective-permute-done | bytes 131104 | tf_op jit(solution)/shard_map/ppermute | solution.py:265
  61.0 2.6 %collective-permute-done.4.first_ref.refs_6_ = bf16[512,128]{1,0:T(8,128)(2,1)S(1)} collective-permute-done((bf16[512,128]{1,0:T(8,128)(2,1)S(1)}, bf16[512,128]{1,0:T(8,128)(2,1)S(1)}, u32[]{:S(2)}, u32[]{:S(2)}) %collective-permute-start.4) | collective-permute-done | bytes 131104 | tf_op jit(solution)/shard_map/ppermute | solution.py:265
  63.7 0.1 collective-permute-start.7
  63.7 2.0 %collective-permute-done.3.second_ref.refs_5_ = bf16[512,128]{1,0:T(8,128)(2,1)S(1)} collective-permute-done((bf16[512,128]{1,0:T(8,128)(2,1)S(1)}, bf16[512,128]{1,0:T(8,128)(2,1)S(1)}, u32[]{:S(2)}, u32[]{:S(2)}) %collective-permute-start.3) | collective-permute-done | bytes 131104 | tf_op jit(solution)/shard_map/ppermute | solution.py:265
  65.7 0.4 collective-permute-start.6
  66.1 0.1 pad_add_fusion.place_ref
  66.2 0.0 copy-start.4
  66.2 0.0 copy-start.5
  66.2 0.0 collective-permute-done.in_ref
  66.2 2.5 %collective-permute-done.7.refs_9_ = bf16[512,128]{1,0:T(8,128)(2,1)S(1)} collective-permute-done((bf16[512,128]{1,0:T(8,128)(2,1)S(1)}, bf16[512,128]{1,0:T(8,128)(2,1)S(1)}, u32[]{:S(2)}, u32[]{:S(2)}) %collective-permute-start.7) | collective-permute-done | bytes 131104 | tf_op jit(solution)/shard_map/ppermute | solution.py:265
  68.7 3.7 %collective-permute-done.6.refs_8_ = bf16[512,128]{1,0:T(8,128)(2,1)S(1)} collective-permute-done((bf16[512,128]{1,0:T(8,128)(2,1)S(1)}, bf16[512,128]{1,0:T(8,128)(2,1)S(1)}, u32[]{:S(2)}, u32[]{:S(2)}) %collective-permute-start.6) | collective-permute-done | bytes 131104 | tf_op jit(solution)/shard_map/ppermute | solution.py:265
  72.4 0.0 collective-permute-done.2.refs_3_
  72.4 0.0 copy-done.4
  72.4 0.0 copy-done.5
  72.4 2.3 %polar.1 = bf16[8,8,2,16,128]{4,3,2,1,0:T(8,128)(2,1)S(1)} custom-call(s32[4]{0:T(128)S(1)} %pad_add_fusion.place_ref, bf16[1536,128]{1,0:T(8,128)(2,1)S(1)} %pad_maximum_fusion.refs_0_, bf16[1536,128]{1,0:T(8,128)(2,1)S(1)} %fence.1.refs_1_, bf16[1536,128]{1,0:T(8,128)(2,1)S(1)} %collective-permute-done.1.refs_2_, ...), custom_call_target="tpu_custom_call" | custom-call | tf_op jit(solution)/shard_map/polar/pallas_call | solution.py:184
  74.8 0.1 copy.17
  74.8 0.0 copy-start.6
  74.8 0.0 copy-start.7
  74.8 25.5 %all_to_all.17 = bf16[64,32,128]{2,1,0:T(8,128)(2,1)S(1)} all-to-all(bf16[64,32,128]{2,1,0:T(8,128)(2,1)S(1)} %bitcast.29), channel_id=1, replica_groups=mesh['xh'=2,'z2'=2,'z1'=2,'z0'=2,'c'=2,'xl'=2,'y1'=2,'y0'=2] {'z1','xl',..., dimensions={0} | all-to-all | bytes 1048576 | tf_op jit(solution)/shard_map/all_to_all | solution.py:304
  100.4 0.0 copy-start.1
  100.4 0.0 copy-start.2
  100.4 0.0 copy-done.6
  100.4 0.0 copy-done.7
  100.4 1.0 copy-done.1
  101.4 0.2 copy-done.2
  101.6 3.3 %finish.1 = (f32[32,4,1024]{2,1,0:T(4,128)}, f32[32,4,1024]{2,1,0:T(4,128)}) custom-call(bf16[8,8,2,16,128]{4,3,2,1,0:T(8,128)(2,1)S(1)} %bitcast.27, bf16[512,512]{1,0:T(8,128)(2,1)S(1)} %copy-done.2, bf16[512,512]{1,0:T(8,128)(2,1)S(1)} %copy-done.1, bf16[256,256]{1,0:T(8,128)(2,1)S(1)} %copy-done.7, bf16[256,256]{1,0:T(8,128)(2,1)S(1)} %copy-done.6), custom_call_target="tpu_custom_call" | custom-call | tf_op jit(solution)/shard_map/finish/pallas_call | solution.py:224
  (11 shorter events, 0.2 us)
Async XLA Ops:
  0.6 13.8 %copy-start.3 = (bf16[16,4096]{1,0:T(8,128)(2,1)S(1)}, bf16[16,4096]{1,0:T(8,128)(2,1)}, u32[]{:S(2)}) copy-start(bf16[16,4096]{1,0:T(8,128)(2,1)} %vir_ref.3) | copy-start | bytes 393220
  2.4 12.1 %copy-start = (bf16[32,4096]{1,0:T(8,128)(2,1)S(1)}, bf16[32,4096]{1,0:T(8,128)(2,1)}, u32[]{:S(2)}) copy-start(bf16[32,4096]{1,0:T(8,128)(2,1)} %occ_ref.3) | copy-start | bytes 786436
  44.7 9.9 %collective-permute-start.1 = (bf16[1536,128]{1,0:T(8,128)(2,1)S(1)}, bf16[1536,128]{1,0:T(8,128)(2,1)S(1)}, u32[]{:S(2)}, u32[]{:S(2)}) collective-permute-start(bf16[1536,128]{1,0:T(8,128)(2,1)S(1)} %pad_maximum_fusion.refs_0_), channel_id=1, source_target_pairs={{0,16},{16,0},{1,17},{17,1},{2,18},{18,2},{3,19},{19,3},{4,20},{20... | collective-permute-start | bytes 1179656 | tf_op jit(solution)/shard_map/ppermute | solution.py:269
  45.7 20.5 %collective-permute-start = (bf16[1536,128]{1,0:T(8,128)(2,1)S(1)}, bf16[1536,128]{1,0:T(8,128)(2,1)S(1)}, u32[]{:S(2)}, u32[]{:S(2)}) collective-permute-start(bf16[1536,128]{1,0:T(8,128)(2,1)S(1)} %pad_maximum_fusion.refs_0_), channel_id=1, source_target_pairs={{0,8},{8,0},{1,9},{9,1},{2,10},{10,2},{3,11},{11,3},{4,12},{12,4},... | collective-permute-start | bytes 1179656 | tf_op jit(solution)/shard_map/ppermute | solution.py:269
  54.5 17.9 %collective-permute-start.2 = (bf16[1536,128]{1,0:T(8,128)(2,1)S(1)}, bf16[1536,128]{1,0:T(8,128)(2,1)S(1)}, u32[]{:S(2)}, u32[]{:S(2)}) collective-permute-start(bf16[1536,128]{1,0:T(8,128)(2,1)S(1)} %collective-permute-done.1.refs_2_), channel_id=1, source_target_pairs={{0,8},{8,0},{1,9},{9,1},{2,10},{10,2},{3,11},{11,3},{4,12},{12,4},... | collective-permute-start | bytes 1179656 | tf_op jit(solution)/shard_map/ppermute | solution.py:269
  54.6 6.4 %collective-permute-start.5 = (bf16[512,128]{1,0:T(8,128)(2,1)S(1)}, bf16[512,128]{1,0:T(8,128)(2,1)S(1)}, u32[]{:S(2)}, u32[]{:S(2)}) collective-permute-start(bf16[512,128]{1,0:T(8,128)(2,1)S(1)} %pad_maximum_fusion.1.first_ref.refs_4_), channel_id=1, source_target_pairs={{0,3},{1,0},{2,1},{3,2},{4,7},{5,4},{6,5},{7,6},{8,11},{9,8},{10,9... | collective-permute-start | bytes 393224 | tf_op jit(solution)/shard_map/ppermute | solution.py:265
  55.8 7.9 %collective-permute-start.4 = (bf16[512,128]{1,0:T(8,128)(2,1)S(1)}, bf16[512,128]{1,0:T(8,128)(2,1)S(1)}, u32[]{:S(2)}, u32[]{:S(2)}) collective-permute-start(bf16[512,128]{1,0:T(8,128)(2,1)S(1)} %pad_maximum_fusion.1.first_ref.refs_4_), channel_id=1, source_target_pairs={{0,2},{1,3},{2,0},{3,1},{4,6},{5,7},{6,4},{7,5},{8,10},{9,11},{10,... | collective-permute-start | bytes 393224 | tf_op jit(solution)/shard_map/ppermute | solution.py:265
  57.2 8.5 %collective-permute-start.3 = (bf16[512,128]{1,0:T(8,128)(2,1)S(1)}, bf16[512,128]{1,0:T(8,128)(2,1)S(1)}, u32[]{:S(2)}, u32[]{:S(2)}) collective-permute-start(bf16[512,128]{1,0:T(8,128)(2,1)S(1)} %pad_maximum_fusion.1.first_ref.refs_4_), channel_id=1, source_target_pairs={{0,1},{1,2},{2,3},{3,0},{4,5},{5,6},{6,7},{7,4},{8,9},{9,10},{10,1... | collective-permute-start | bytes 393224 | tf_op jit(solution)/shard_map/ppermute | solution.py:265
  63.7 5.0 %collective-permute-start.7 = (bf16[512,128]{1,0:T(8,128)(2,1)S(1)}, bf16[512,128]{1,0:T(8,128)(2,1)S(1)}, u32[]{:S(2)}, u32[]{:S(2)}) collective-permute-start(bf16[512,128]{1,0:T(8,128)(2,1)S(1)} %join.3), channel_id=1, source_target_pairs={{0,132},{4,0},{128,4},{132,128},{1,133},{5,1},{129,5},{133,129},{2... | collective-permute-start | bytes 393224 | tf_op jit(solution)/shard_map/ppermute | solution.py:265
  65.7 6.7 %collective-permute-start.6 = (bf16[512,128]{1,0:T(8,128)(2,1)S(1)}, bf16[512,128]{1,0:T(8,128)(2,1)S(1)}, u32[]{:S(2)}, u32[]{:S(2)}) collective-permute-start(bf16[512,128]{1,0:T(8,128)(2,1)S(1)} %join.2), channel_id=1, source_target_pairs={{0,4},{4,128},{128,132},{132,0},{1,5},{5,129},{129,133},{133,1},{2... | collective-permute-start | bytes 393224 | tf_op jit(solution)/shard_map/ppermute | solution.py:265
  66.2 6.2 %copy-start.4 = (bf16[512,256]{1,0:T(8,128)(2,1)S(1)}, bf16[512,256]{1,0:T(8,128)(2,1)}, u32[]{:S(2)}) copy-start(bf16[512,256]{1,0:T(8,128)(2,1)} %constant.51.clone.refs_11_) | copy-start | bytes 786436
  66.2 6.3 %copy-start.5 = (bf16[512,256]{1,0:T(8,128)(2,1)S(1)}, bf16[512,256]{1,0:T(8,128)(2,1)}, u32[]{:S(2)}) copy-start(bf16[512,256]{1,0:T(8,128)(2,1)} %constant.50.clone.refs_10_) | copy-start | bytes 786436
  74.8 25.6 %copy-start.6 = (bf16[256,256]{1,0:T(8,128)(2,1)S(1)}, bf16[256,256]{1,0:T(8,128)(2,1)}, u32[]{:S(2)}) copy-start(bf16[256,256]{1,0:T(8,128)(2,1)} %constant.55.clone.b_low_ref) | copy-start | bytes 393220
  74.8 25.6 %copy-start.7 = (bf16[256,256]{1,0:T(8,128)(2,1)S(1)}, bf16[256,256]{1,0:T(8,128)(2,1)}, u32[]{:S(2)}) copy-start(bf16[256,256]{1,0:T(8,128)(2,1)} %constant.54.clone.b_high_ref) | copy-start | bytes 393220
  100.4 1.0 copy-start.1
  100.4 1.2 %copy-start.2 = (bf16[512,512]{1,0:T(8,128)(2,1)S(1)}, bf16[512,512]{1,0:T(8,128)(2,1)}, u32[]{:S(2)}) copy-start(bf16[512,512]{1,0:T(8,128)(2,1)} %constant.52.clone.a_high_ref) | copy-start | bytes 1572868
where the time goes:
time: 105 us
  blocking collectives  67.5 us (64%)
  waiting for transfers between devices  23.5 us (22%)
  Pallas kernels  7.47 us (7%)
  starting transfers between devices  4.14 us (4%)
  local copies, waits for them, and re-layouts  1.37 us (1%)
    all_to_all x1, blocking collectives, body(): arrived = lax.all_to_all(pack(occ, vir, scattered), ROW, 0, 0, tiled=True)  29.9 us
    all_to_all x1, blocking collectives, body(): received = lax.all_to_all(sent, LAST, 0, 0, tiled=True).reshape(bits.shape)  25.5 us
    ppermute x5, waiting for transfers between devices, shift(): return lax.ppermute(x, axes, [(i, (i + by) % count) for i in range(count)])  14.6 us
    all_to_all x1, blocking collectives, body(): lax.all_to_all(prepare(row, occ_decay, vir_decay, occ, vir), COL, 0, 0, t...  12.1 us
    ppermute x3, waiting for transfers between devices, swap(): return lax.ppermute(x, axis, [(0, 1), (1, 0)])  8.86 us
    pallas_call x1, Pallas kernels, finish(): pl.pallas_call(finish_kernel, out_shape=(shape, shape), in_specs=[vmem] *...  3.35 us
    ppermute x5, starting transfers between devices, shift(): return lax.ppermute(x, axes, [(i, (i + by) % count) for i in range(count)])  3.12 us
    pallas_call x1, Pallas kernels, polar_messages(): pl.pallas_call(polar_kernel, out_shape=jax.ShapeDtypeStruct((8, 8, 2, 16,...  2.31 us
  transfers between devices with their start and end apart: 8, of which 6 were waited for; matrix products, arithmetic and copies ran while one was open for 0% of the time, Pallas kernels for 0%

commit v1 on v0

--- a/solution.py
+++ b/solution.py
@@ -25,6 +25,15 @@
 LIMIT = 16 * 1024 * 1024
 
 
+def place_in_last(m, j):
+    bits = dict(zip(("xh", "z2", "z1"), ((m >> 2) & 1, (m >> 1) & 1, m & 1)))
+    bits.update(zip(COL, ((j >> 2) & 1, (j >> 1) & 1, j & 1)))
+    place = 0
+    for axis in LAST:
+        place = 2 * place + bits[axis]
+    return place
+
+
 def split_table(table):
     high = table.astype(np.float32).astype(jnp.bfloat16)
     low = (table - high.astype(np.float64)).astype(np.float32).astype(jnp.bfloat16)
@@ -87,19 +96,19 @@
 
     occ = scaled_tiles(occ_ref, column(occ_decay_ref, 32))
     vir = scaled_tiles(vir_ref, column(vir_decay_ref, 16))
-    for xl in range(2):
-        for y1 in range(2):
-            for t in range(2):
-                for kind in range(4):
-                    group = 2 * xl + y1
-                    piece = jnp.concatenate(
-                        [
-                            occ[t][kind][8 * group : 8 * (group + 1)],
-                            vir[t][kind][8 * y1 : 8 * (y1 + 1)],
-                        ],
-                        axis=0,
-                    )
-                    out_ref[4 * xl + 2 * y1 + t, kind] = piece.astype(BF16)
+    for y1 in range(2):
+        for t in range(2):
+            for kind in range(4):
+                piece = jnp.concatenate(
+                    [
+                        occ[t][kind][8 * y1 : 8 * (y1 + 1)],
+                        occ[t][kind][8 * (2 + y1) : 8 * (3 + y1)],
+                        vir[t][kind][8 * y1 : 8 * (y1 + 1)],
+                    ],
+                    axis=0,
+                ).astype(BF16)
+                for xl in range(2):
+                    out_ref[4 * xl + 2 * y1 + t, kind] = piece
 
 
 def prepare(place, occ_decay, vir_decay, occ, vir):
@@ -107,7 +116,7 @@
     return pl.pallas_call(
         prepare_kernel,
         grid=(1,),
-        out_shape=jax.ShapeDtypeStruct((8, 4, 16, 128), BF16),
+        out_shape=jax.ShapeDtypeStruct((8, 4, 24, 128), BF16),
         in_specs=[
             smem,
             smem,
@@ -115,7 +124,7 @@
             pl.BlockSpec((32, 1024), lambda i: (0, 0)),
             pl.BlockSpec((16, 1024), lambda i: (0, 0)),
         ],
-        out_specs=pl.BlockSpec((8, 4, 16, 128), lambda i: (0, 0, 0, 0)),
+        out_specs=pl.BlockSpec((8, 4, 24, 128), lambda i: (0, 0, 0, 0)),
         name="prepare",
     )(place, occ_decay, vir_decay, occ, vir)
 
@@ -124,14 +133,14 @@
     for p in range(32):
         out_ref[p, 0:32, :] = occ_ref[:, 128 * p : 128 * (p + 1)]
         out_ref[p, 32:48, :] = vir_ref[:, 128 * p : 128 * (p + 1)]
-        out_ref[p, 48:64, :] = rows_ref[0, p % 4]
+        out_ref[p, 48:72, :] = rows_ref[0, p % 4]
 
 
 def pack(occ, vir, rows):
     vmem = pl.BlockSpec(memory_space=pltpu.VMEM)
     return pl.pallas_call(
         pack_kernel,
-        out_shape=jax.ShapeDtypeStruct((32, 64, 128), BF16),
+        out_shape=jax.ShapeDtypeStruct((32, 72, 128), BF16),
         in_specs=[vmem] * 3,
         out_specs=vmem,
         compiler_params=pltpu.CompilerParams(vmem_limit_bytes=LIMIT),
@@ -139,10 +148,10 @@
     )(occ, vir, rows)
 
 
-def polar_kernel(place_ref, *refs):
-    points, near, far = refs[:4], refs[4:8], refs[8:10]
-    high_ref, low_ref, out_ref, polar_ref, occ_ref, vir_ref = refs[10:]
-    core, z0, xl, y = place_ref[0], place_ref[1], place_ref[2], place_ref[3]
+def polar_kernel(core_ref, z0_ref, y_ref, *refs):
+    points, near, (high_ref, low_ref) = refs[:4], refs[4:8], refs[8:10]
+    out_ref, polar_ref, occ_ref, vir_ref = refs[-4:]
+    core, z0, y = core_ref[0], z0_ref[0], y_ref[0]
     for step in range(4):
         chunk = lax.rem(y + 4 - step, 4)
         y1, y0 = lax.div(chunk, 2), lax.rem(chunk, 2)
@@ -151,11 +160,9 @@
         def rows(group):
             return pl.ds(pl.multiple_of(256 * group, 256), 256)
 
-        occ_ref[rows(2 * xl + y1), lanes] = near[step][:256]
-        occ_ref[rows(2 * (1 - xl) + y1), lanes] = far[step // 2][
-            256 * (step % 2) : 256 * (step % 2 + 1)
-        ]
-        vir_ref[rows(y1), lanes] = near[step][256:]
+        occ_ref[rows(y1), lanes] = near[step][:256]
+        occ_ref[rows(2 + y1), lanes] = near[step][256:512]
+        vir_ref[rows(y1), lanes] = near[step][512:]
     for k, ref in enumerate(points):
         place = 2 * (z0 if k < 2 else 1 - z0) + (core if k % 2 == 0 else 1 - core)
         green_occ = dot(ref[:1024].T, occ_ref[...])
@@ -175,16 +182,16 @@
         for m in range(8):
             pieces = [spectrum[128 * i : 128 * (i + 1), 32 * m : 32 * (m + 1)] for i in range(4)]
             message = jnp.concatenate(pieces, axis=1).astype(BF16)
-            out_ref[m, :, half] = message.reshape(8, 16, 128)
-
-
-def polar_messages(place, *arrays):
-    high, low = c_table()
+            for j in range(8):
+                out_ref[place_in_last(m, j), half] = message[16 * j : 16 * (j + 1)]
+
+
+def polar_messages(*arrays):
     vmem = pl.BlockSpec(memory_space=pltpu.VMEM)
     return pl.pallas_call(
         polar_kernel,
-        out_shape=jax.ShapeDtypeStruct((8, 8, 2, 16, 128), BF16),
-        in_specs=[pl.BlockSpec(memory_space=pltpu.SMEM)] + [vmem] * 12,
+        out_shape=jax.ShapeDtypeStruct((64, 2, 16, 128), BF16),
+        in_specs=[pl.BlockSpec(memory_space=pltpu.SMEM)] * 3 + [vmem] * 10,
         out_specs=vmem,
         scratch_shapes=[
             pltpu.VMEM((512, 256), F32),
@@ -193,17 +200,19 @@
         ],
         compiler_params=pltpu.CompilerParams(vmem_limit_bytes=LIMIT),
         name="polar",
-    )(place, *arrays, high, low)
-
-
-def finish_kernel(x_ref, a_high_ref, a_low_ref, b_high_ref, b_low_ref, real_ref, imag_ref):
+    )(*arrays)
+
+
+def finish_kernel(x_ref, a_high_ref, a_low_ref, b_high_ref, b_low_ref, *refs):
+    outs, parts, sems = refs[:2], refs[2:4], refs[4]
     planes = []
     for block in range(4):
         zb, half = divmod(block, 2)
         x = jnp.concatenate(
-            [x_ref[2 * k + zb, :, half].reshape(128, 128) for k in range(4)], axis=0
+            [x_ref[place_in_last(2 * k + zb, j), half] for k in range(4) for j in range(8)], axis=0
         )
         planes.append(dot(a_high_ref[...], x) + dot(a_low_ref[...], x))
+    copies = []
     for g in range(8):
         z = jnp.concatenate([plane[64 * g : 64 * (g + 1)] for plane in planes], axis=0).T
         z_high = z.astype(BF16)
@@ -213,39 +222,57 @@
             + dot(z_high, b_low_ref[...])
             + dot(z_low, b_high_ref[...])
         )
-        for i in range(4):
-            real_ref[:, i, 128 * g : 128 * (g + 1)] = out[32 * i : 32 * (i + 1), :128]
-            imag_ref[:, i, 128 * g : 128 * (g + 1)] = out[32 * i : 32 * (i + 1), 128:]
-
-
-def finish(x):
+        for which in range(2):
+            for i in range(4):
+                parts[which][:, i, 128 * g : 128 * (g + 1)] = out[
+                    32 * i : 32 * (i + 1), 128 * which : 128 * (which + 1)
+                ]
+            if g % 2 == 1:
+                lanes = pl.ds(128 * (g - 1), 256)
+                copy = pltpu.make_async_copy(
+                    parts[which].at[:, :, lanes], outs[which].at[:, :, lanes], sems.at[which, g // 2]
+                )
+                copy.start()
+                copies.append(copy)
+    for copy in copies:
+        copy.wait()
+
+
+def finish(x, *tables):
     vmem = pl.BlockSpec(memory_space=pltpu.VMEM)
+    hbm = pl.BlockSpec(memory_space=pl.ANY)
     shape = jax.ShapeDtypeStruct((32, 4, 1024), F32)
     return pl.pallas_call(
         finish_kernel,
         out_shape=(shape, shape),
         in_specs=[vmem] * 5,
-        out_specs=(vmem, vmem),
+        out_specs=(hbm, hbm),
+        scratch_shapes=[
+            pltpu.VMEM((32, 4, 1024), F32),
+            pltpu.VMEM((32, 4, 1024), F32),
+            pltpu.SemaphoreType.DMA((2, 4)),
+        ],
         compiler_params=pltpu.CompilerParams(vmem_limit_bytes=LIMIT),
         name="finish",
-    )(x, *a_table(), *b_table())
-
-
-def join_kernel(first_ref, second_ref, out_ref):
-    out_ref[:256] = first_ref[:256]
-    out_ref[256:] = second_ref[:256]
-
-
-def join(first, second):
+    )(x, *tables)
+
+
+def carry_kernel(*refs):
+    count = len(refs) // 2
+    for in_ref, out_ref in zip(refs[:count], refs[count:]):
+        out_ref[...] = in_ref[...]
+
+
+def carry(*arrays):
     vmem = pl.BlockSpec(memory_space=pltpu.VMEM)
     return pl.pallas_call(
-        join_kernel,
-        out_shape=jax.ShapeDtypeStruct((512, 128), BF16),
-        in_specs=[vmem, vmem],
-        out_specs=vmem,
-        compiler_params=pltpu.CompilerParams(vmem_limit_bytes=LIMIT),
-        name="join",
-    )(first, second)
+        carry_kernel,
+        out_shape=[jax.ShapeDtypeStruct(a.shape, a.dtype) for a in arrays],
+        in_specs=[vmem] * len(arrays),
+        out_specs=[vmem] * len(arrays),
+        compiler_params=pltpu.CompilerParams(vmem_limit_bytes=LIMIT),
+        name="carry",
+    )(*arrays)
 
 
 def fence(x):
@@ -271,39 +298,29 @@
 
 def body(occ, vir, occ_decay, vir_decay):
     row = lax.axis_index(ROW).astype(jnp.int32).reshape(1)
-    place = jnp.stack([lax.axis_index(a).astype(jnp.int32) for a in ("c", "z0", "xl", Y)])
+    place = [lax.axis_index(a).astype(jnp.int32).reshape(1) for a in ("c", "z0", Y)]
     scattered = lax.all_to_all(prepare(row, occ_decay, vir_decay, occ, vir), COL, 0, 0, tiled=True)
     arrived = lax.all_to_all(pack(occ, vir, scattered), ROW, 0, 0, tiled=True)
 
-    near = jnp.concatenate(
-        [arrived[:, 48:56].reshape(256, 128), arrived[:, 56:].reshape(256, 128)], axis=0
-    )
+    def by_group(part, count):
+        part = part.reshape(32, count, 8, 128)
+        return jnp.transpose(part, (1, 0, 2, 3)).reshape(256 * count, 128)
+
+    near = jnp.concatenate([by_group(arrived[:, 48:64], 2), by_group(arrived[:, 64:], 1)], axis=0)
     near = [near]
     for by in (1, 2, 3):
         near.append(shift(near[0], Y, 4, by))
-    up = join(near[0], near[1])
-    up = shift(up, ("xh", "xl"), 4, 1)
-    down = join(near[2], near[3])
-    down = shift(down, ("xh", "xl"), 4, -1)
-
-    def by_group(part, count):
-        part = part.reshape(32, count, 8, 128)
-        return jnp.transpose(part, (1, 0, 2, 3)).reshape(256 * count, 128)
-
     own = jnp.concatenate([by_group(arrived[:, :32], 4), by_group(arrived[:, 32:48], 2)], axis=0)
     across = swap(own, "z0")
     beside = swap(own, "c")
     beside = fence(beside)
     opposite = swap(across, "c")
     points = (own, beside, across, opposite)
-    messages = polar_messages(place, *points, *near, up, down)
-
-    names = ("xh", "z2", "z1", *COL)
-    bits = messages.reshape(2, 2, 2, 2, 2, 2, 32, 128)
-    sent = jnp.transpose(bits, (*(names.index(a) for a in LAST), 6, 7)).reshape(64, 32, 128)
-    received = lax.all_to_all(sent, LAST, 0, 0, tiled=True).reshape(bits.shape)
-    received = jnp.transpose(received, (*(LAST.index(a) for a in names), 6, 7))
-    return finish(received.reshape(8, 8, 2, 16, 128))
+    messages = polar_messages(*place, *points, *near, *c_table())
+
+    received = lax.all_to_all(messages, LAST, 0, 0, tiled=True)
+    tables = carry(*a_table(), *b_table())
+    return finish(received, *tables)
 
 
 def solution(mesh):

time: 105 us -> 103 us (0.981)
  blocking collectives: 67.5 us -> 43.8 us
  waiting for transfers between devices: 23.5 us -> 41.1 us
  starting transfers between devices: 4.14 us -> 9.26 us
  local copies, waits for them, and re-layouts: 1.37 us -> 0.15 us
    all_to_all x1 -> x0, blocking collectives: 25.5 us -> none  [body(): received = lax.all_to_all(sent, LAST, 0, 0, tiled=True).reshape(bits.shape)]
    all_to_all x0 -> x1, waiting for transfers between devices: none -> 20.6 us  [body(): received = lax.all_to_all(messages, LAST, 0, 0, tiled=True)]
    all_to_all x0 -> x1, starting transfers between devices: none -> 6.02 us  [body(): received = lax.all_to_all(messages, LAST, 0, 0, tiled=True)]
    ppermute x5 -> x3, waiting for transfers between devices: 14.6 us -> 11.3 us  [shift(): return lax.ppermute(x, axes, [(i, (i + by) % count) for i in range(count)])]
    all_to_all x1, blocking collectives: 29.9 us -> 31.3 us  [body(): arrived = lax.all_to_all(pack(occ, vir, scattered), ROW, 0, 0, tiled=True)]
    unnamed x16, local copies, waits for them, and re-layouts: 1.15 us -> 0.04 us
    ppermute x5 -> x3, starting transfers between devices: 3.12 us -> 2.48 us  [shift(): return lax.ppermute(x, axes, [(i, (i + by) % count) for i in range(count)])]
    pallas_call x4 -> x3, Pallas kernels: 2.41 us -> 2.74 us  [the longest x1 2.56 us: polar_messages(): pl.pallas_call(polar_kernel, out_shape=jax.ShapeDtypeStruct((64, 2, 16, 1...]
  transfers between devices with their start and end apart: 8 -> 7, of which waited for: 6 -> 5; matrix products, arithmetic and copies ran while one was open for 0% -> 0% of each run, Pallas kernels for 0% -> 0%
where the time goes in v1:
time: 103 us
  blocking collectives  43.8 us (43%)
  waiting for transfers between devices  41.1 us (40%)
  starting transfers between devices  9.26 us (9%)
  Pallas kernels  7.58 us (7%)
    all_to_all x1, blocking collectives, body(): arrived = lax.all_to_all(pack(occ, vir, scattered), ROW, 0, 0, tiled=True)  31.3 us
    all_to_all x1, waiting for transfers between devices, body(): received = lax.all_to_all(messages, LAST, 0, 0, tiled=True)  20.6 us
    all_to_all x1, blocking collectives, body(): lax.all_to_all(prepare(row, occ_decay, vir_decay, occ, vir), COL, 0, 0, t...  12.5 us
    ppermute x3, waiting for transfers between devices, shift(): return lax.ppermute(x, axes, [(i, (i + by) % count) for i in range(count)])  11.3 us
    ppermute x3, waiting for transfers between devices, swap(): return lax.ppermute(x, axis, [(0, 1), (1, 0)])  9.18 us
    all_to_all x1, starting transfers between devices, body(): received = lax.all_to_all(messages, LAST, 0, 0, tiled=True)  6.02 us
    pallas_call x1, Pallas kernels, finish(): pl.pallas_call(finish_kernel, out_shape=(shape, shape), in_specs=[vmem] *...  3.14 us
    pallas_call x1, Pallas kernels, polar_messages(): pl.pallas_call(polar_kernel, out_shape=jax.ShapeDtypeStruct((64, 2, 16, 1...  2.56 us
  transfers between devices with their start and end apart: 7, of which 5 were waited for; matrix products, arithmetic and copies ran while one was open for 0% of the time, Pallas kernels for 0%

profile of v1, /device:TPU:32, one launch (start us, length us, event | category | flops | bytes accessed | tf_op | source)
XLA Modules:
  0.0 102.7 jit_solution(10386496317744106604)
XLA Ops:
  0.6 1.7 %prepare.1 = bf16[8,4,24,128]{3,2,1,0:T(8,128)(2,1)} custom-call(s32[1]{0:T(128)} %bitcast.3.place_ref, f32[1024]{0:T(1024)} %occ_decay_ref.1, f32[512]{0:T(512)} %vir_decay_ref.1, bf16[32,4096]{1,0:T(8,128)(2,1)} %occ_ref.3, bf16[16,4096]{1,0:T(8,128)(2,1)} %vir_ref.3), custom_call_target="tpu_custom_call" | custom-call | tf_op jit(solution)/shard_map/prepare/pallas_call | solution.py:116
  2.3 0.0 copy-start
  2.3 0.0 copy-start.3
  2.3 12.5 %all_to_all.15.rows_ref = bf16[8,4,24,128]{3,2,1,0:T(8,128)(2,1)S(1)} all-to-all(bf16[8,4,24,128]{3,2,1,0:T(8,128)(2,1)} %prepare.1), channel_id=1, replica_groups=mesh['xh'=2,'z2'=2,'z1'=2,'z0'=2,'c'=2,'xl'=2,'y1'=2,'y0'=2] {'xl','y1',..., dimensions={0} | all-to-all | bytes 393216 | tf_op jit(solution)/shard_map/all_to_all | solution.py:302
  14.8 0.0 copy-done
  14.8 0.0 copy-done.3
  14.8 0.1 pack.1
  14.9 31.3 %all_to_all.16 = bf16[32,72,128]{2,1,0:T(8,128)(2,1)S(1)} all-to-all(bf16[32,72,128]{2,1,0:T(8,128)(2,1)S(1)} %pack.1), channel_id=1, replica_groups=mesh['xh'=2,'z2'=2,'z1'=2,'z0'=2,'c'=2,'xl'=2,'y1'=2,'y0'=2] {'xh','z2',..., dimensions={0} | all-to-all | bytes 1179648 | tf_op jit(solution)/shard_map/all_to_all | solution.py:303
  46.4 0.8 collective-permute-start.1
  47.2 0.0 collective-permute-start
  47.2 9.2 %collective-permute-done.1.refs_2_ = bf16[1536,128]{1,0:T(8,128)(2,1)S(1)} collective-permute-done((bf16[1536,128]{1,0:T(8,128)(2,1)S(1)}, bf16[1536,128]{1,0:T(8,128)(2,1)S(1)}, u32[]{:S(2)}, u32[]{:S(2)}) %collective-permute-start.1) | collective-permute-done | bytes 393248 | tf_op jit(solution)/shard_map/ppermute | solution.py:296
  56.3 0.0 collective-permute-start.2
  56.4 1.0 collective-permute-start.5
  57.4 1.5 %collective-permute-start.4 = (bf16[768,128]{1,0:T(8,128)(2,1)S(1)}, bf16[768,128]{1,0:T(8,128)(2,1)S(1)}, u32[]{:S(2)}, u32[]{:S(2)}) collective-permute-start(bf16[768,128]{1,0:T(8,128)(2,1)S(1)} %pad_maximum_fusion.1.refs_4_), channel_id=1, source_target_pairs={{0,2},{1,3},{2,0},{3,1},{4,6},{5,7},{6,4},{7,5},{8,10},{9,11},{10,... | collective-permute-start | bytes 589832 | tf_op jit(solution)/shard_map/ppermute | solution.py:292
  58.9 0.0 collective-permute-start.3
  58.9 0.0 copy-start.4
  58.9 0.0 copy-start.5
  58.9 0.0 collective-permute-done.in_ref
  58.9 5.3 %collective-permute-done.5.refs_7_ = bf16[768,128]{1,0:T(8,128)(2,1)S(1)} collective-permute-done((bf16[768,128]{1,0:T(8,128)(2,1)S(1)}, bf16[768,128]{1,0:T(8,128)(2,1)S(1)}, u32[]{:S(2)}, u32[]{:S(2)}) %collective-permute-start.5) | collective-permute-done | bytes 196640 | tf_op jit(solution)/shard_map/ppermute | solution.py:292
  64.2 2.5 %collective-permute-done.4.refs_6_ = bf16[768,128]{1,0:T(8,128)(2,1)S(1)} collective-permute-done((bf16[768,128]{1,0:T(8,128)(2,1)S(1)}, bf16[768,128]{1,0:T(8,128)(2,1)S(1)}, u32[]{:S(2)}, u32[]{:S(2)}) %collective-permute-start.4) | collective-permute-done | bytes 196640 | tf_op jit(solution)/shard_map/ppermute | solution.py:292
  66.7 3.4 %collective-permute-done.3.refs_5_ = bf16[768,128]{1,0:T(8,128)(2,1)S(1)} collective-permute-done((bf16[768,128]{1,0:T(8,128)(2,1)S(1)}, bf16[768,128]{1,0:T(8,128)(2,1)S(1)}, u32[]{:S(2)}, u32[]{:S(2)}) %collective-permute-start.3) | collective-permute-done | bytes 196640 | tf_op jit(solution)/shard_map/ppermute | solution.py:292
  70.1 0.0 collective-permute-done.2.refs_3_
  70.1 0.0 copy-done.4
  70.1 0.0 copy-done.5
  70.1 0.0 copy-start.6
  70.2 0.0 copy-start.7
  70.2 2.6 %polar.1 = bf16[64,2,16,128]{3,2,1,0:T(8,128)(2,1)} custom-call(s32[1]{0:T(128)} %bitcast.core_ref, s32[1]{0:T(128)} %bitcast.1.z0_ref, s32[1]{0:T(128)} %bitcast.2.y_ref, bf16[1536,128]{1,0:T(8,128)(2,1)S(1)} %pad_maximum_fusion.refs_0_, bf16[1536,128]{1,0:T(8,128)(2,1)S(1)} %fence.1.refs_1_, bf16[1536,128]{1,0:T(8,128)(2,1)S(1)} %collective-permute-done.1.refs_2_, ...), custom_call_target="tpu_custom_call" | custom-call | tf_op jit(solution)/shard_map/polar/pallas_call | solution.py:191
  72.7 0.0 copy-start.1
  72.7 0.0 copy-start.2
  72.7 6.0 %all-to-all-start.2 = ((bf16[64,2,16,128]{3,2,1,0:T(8,128)(2,1)}), bf16[64,2,16,128]{3,2,1,0:T(8,128)(2,1)S(1)}, u32[]{:S(2)}, u32[]{:S(2)}) async-start(bf16[64,2,16,128]{3,2,1,0:T(8,128)(2,1)} %polar.1), calls=%async_computation.2 | async-start | bytes 1048576 | tf_op jit(solution)/shard_map/all_to_all | solution.py:321
  78.8 0.0 copy-done.6
  78.8 0.0 copy-done.7
  78.8 0.0 copy-done.1
  78.8 0.0 copy-done.2
  78.8 0.1 carry.1
  78.9 20.6 %all-to-all-done.2.x_ref = bf16[64,2,16,128]{3,2,1,0:T(8,128)(2,1)S(1)} async-done(((bf16[64,2,16,128]{3,2,1,0:T(8,128)(2,1)}), bf16[64,2,16,128]{3,2,1,0:T(8,128)(2,1)S(1)}, u32[]{:S(2)}, u32[]{:S(2)}) %all-to-all-start.2) | async-done | bytes 524320 | tf_op jit(solution)/shard_map/all_to_all | solution.py:321
  99.5 3.1 %finish.1 = (f32[32,4,1024]{2,1,0:T(4,128)}, f32[32,4,1024]{2,1,0:T(4,128)}) custom-call(bf16[64,2,16,128]{3,2,1,0:T(8,128)(2,1)S(1)} %all-to-all-done.2.x_ref, bf16[512,512]{1,0:T(8,128)(2,1)S(1)} %get-tuple-element.6.a_high_ref, bf16[512,512]{1,0:T(8,128)(2,1)S(1)} %get-tuple-element.7.a_low_ref, bf16[256,256]{1,0:T(8,128)(2,1)S(1)} %get-tuple-element.8.b_high_ref, ...), custom_call_target="tpu_custom_call" | custom-call | tf_op jit(solution)/shard_map/finish/pallas_call | solution.py:245
  (9 shorter events, 0.2 us)
Async XLA Ops:
  2.3 12.5 %copy-start = (bf16[32,4096]{1,0:T(8,128)(2,1)S(1)}, bf16[32,4096]{1,0:T(8,128)(2,1)}, u32[]{:S(2)}) copy-start(bf16[32,4096]{1,0:T(8,128)(2,1)} %occ_ref.3) | copy-start | bytes 786436
  2.3 12.5 %copy-start.3 = (bf16[16,4096]{1,0:T(8,128)(2,1)S(1)}, bf16[16,4096]{1,0:T(8,128)(2,1)}, u32[]{:S(2)}) copy-start(bf16[16,4096]{1,0:T(8,128)(2,1)} %vir_ref.3) | copy-start | bytes 393220
  46.4 9.9 %collective-permute-start.1 = (bf16[1536,128]{1,0:T(8,128)(2,1)S(1)}, bf16[1536,128]{1,0:T(8,128)(2,1)S(1)}, u32[]{:S(2)}, u32[]{:S(2)}) collective-permute-start(bf16[1536,128]{1,0:T(8,128)(2,1)S(1)} %pad_maximum_fusion.refs_0_), channel_id=1, source_target_pairs={{0,16},{16,0},{1,17},{17,1},{2,18},{18,2},{3,19},{19,3},{4,20},{20... | collective-permute-start | bytes 1179656 | tf_op jit(solution)/shard_map/ppermute | solution.py:296
  47.2 11.7 %collective-permute-start = (bf16[1536,128]{1,0:T(8,128)(2,1)S(1)}, bf16[1536,128]{1,0:T(8,128)(2,1)S(1)}, u32[]{:S(2)}, u32[]{:S(2)}) collective-permute-start(bf16[1536,128]{1,0:T(8,128)(2,1)S(1)} %pad_maximum_fusion.refs_0_), channel_id=1, source_target_pairs={{0,8},{8,0},{1,9},{9,1},{2,10},{10,2},{3,11},{11,3},{4,12},{12,4},... | collective-permute-start | bytes 1179656 | tf_op jit(solution)/shard_map/ppermute | solution.py:296
  56.3 13.8 %collective-permute-start.2 = (bf16[1536,128]{1,0:T(8,128)(2,1)S(1)}, bf16[1536,128]{1,0:T(8,128)(2,1)S(1)}, u32[]{:S(2)}, u32[]{:S(2)}) collective-permute-start(bf16[1536,128]{1,0:T(8,128)(2,1)S(1)} %collective-permute-done.1.refs_2_), channel_id=1, source_target_pairs={{0,8},{8,0},{1,9},{9,1},{2,10},{10,2},{3,11},{11,3},{4,12},{12,4},... | collective-permute-start | bytes 1179656 | tf_op jit(solution)/shard_map/ppermute | solution.py:296
  56.4 7.8 %collective-permute-start.5 = (bf16[768,128]{1,0:T(8,128)(2,1)S(1)}, bf16[768,128]{1,0:T(8,128)(2,1)S(1)}, u32[]{:S(2)}, u32[]{:S(2)}) collective-permute-start(bf16[768,128]{1,0:T(8,128)(2,1)S(1)} %pad_maximum_fusion.1.refs_4_), channel_id=1, source_target_pairs={{0,3},{1,0},{2,1},{3,2},{4,7},{5,4},{6,5},{7,6},{8,11},{9,8},{10,9... | collective-permute-start | bytes 589832 | tf_op jit(solution)/shard_map/ppermute | solution.py:292
  57.4 9.3 %collective-permute-start.4 = (bf16[768,128]{1,0:T(8,128)(2,1)S(1)}, bf16[768,128]{1,0:T(8,128)(2,1)S(1)}, u32[]{:S(2)}, u32[]{:S(2)}) collective-permute-start(bf16[768,128]{1,0:T(8,128)(2,1)S(1)} %pad_maximum_fusion.1.refs_4_), channel_id=1, source_target_pairs={{0,2},{1,3},{2,0},{3,1},{4,6},{5,7},{6,4},{7,5},{8,10},{9,11},{10,... | collective-permute-start | bytes 589832 | tf_op jit(solution)/shard_map/ppermute | solution.py:292
  58.9 11.3 %collective-permute-start.3 = (bf16[768,128]{1,0:T(8,128)(2,1)S(1)}, bf16[768,128]{1,0:T(8,128)(2,1)S(1)}, u32[]{:S(2)}, u32[]{:S(2)}) collective-permute-start(bf16[768,128]{1,0:T(8,128)(2,1)S(1)} %pad_maximum_fusion.1.refs_4_), channel_id=1, source_target_pairs={{0,1},{1,2},{2,3},{3,0},{4,5},{5,6},{6,7},{7,4},{8,9},{9,10},{10,1... | collective-permute-start | bytes 589832 | tf_op jit(solution)/shard_map/ppermute | solution.py:292
  58.9 11.3 %copy-start.4 = (bf16[512,256]{1,0:T(8,128)(2,1)S(1)}, bf16[512,256]{1,0:T(8,128)(2,1)}, u32[]{:S(2)}) copy-start(bf16[512,256]{1,0:T(8,128)(2,1)} %constant.47.clone.refs_9_) | copy-start | bytes 786436
  58.9 11.3 %copy-start.5 = (bf16[512,256]{1,0:T(8,128)(2,1)S(1)}, bf16[512,256]{1,0:T(8,128)(2,1)}, u32[]{:S(2)}) copy-start(bf16[512,256]{1,0:T(8,128)(2,1)} %constant.46.clone.refs_8_) | copy-start | bytes 786436
  70.1 8.6 %copy-start.6 = (bf16[256,256]{1,0:T(8,128)(2,1)S(1)}, bf16[256,256]{1,0:T(8,128)(2,1)}, u32[]{:S(2)}) copy-start(bf16[256,256]{1,0:T(8,128)(2,1)} %constant.51.clone.refs_3_) | copy-start | bytes 393220
  70.2 8.6 %copy-start.7 = (bf16[256,256]{1,0:T(8,128)(2,1)S(1)}, bf16[256,256]{1,0:T(8,128)(2,1)}, u32[]{:S(2)}) copy-start(bf16[256,256]{1,0:T(8,128)(2,1)} %constant.50.clone.refs_2_) | copy-start | bytes 393220
  72.7 6.0 %copy-start.1 = (bf16[512,512]{1,0:T(8,128)(2,1)S(1)}, bf16[512,512]{1,0:T(8,128)(2,1)}, u32[]{:S(2)}) copy-start(bf16[512,512]{1,0:T(8,128)(2,1)} %constant.49.clone.refs_1_) | copy-start | bytes 1572868
  72.7 6.1 %copy-start.2 = (bf16[512,512]{1,0:T(8,128)(2,1)S(1)}, bf16[512,512]{1,0:T(8,128)(2,1)}, u32[]{:S(2)}) copy-start(bf16[512,512]{1,0:T(8,128)(2,1)} %constant.48.clone.refs_0_) | copy-start | bytes 1572868
  72.7 26.8 %all-to-all-start.2 = ((bf16[64,2,16,128]{3,2,1,0:T(8,128)(2,1)}), bf16[64,2,16,128]{3,2,1,0:T(8,128)(2,1)S(1)}, u32[]{:S(2)}, u32[]{:S(2)}) async-start(bf16[64,2,16,128]{3,2,1,0:T(8,128)(2,1)} %polar.1), calls=%async_computation.2 | async-start | bytes 1048576 | tf_op jit(solution)/shard_map/all_to_all | solution.py:321

commit v2 on v1

--- a/solution.py
+++ b/solution.py
@@ -72,8 +72,23 @@
     return lax.dot_general(a, b, (((1,), (0,)), ((), ())), preferred_element_type=F32)
 
 
-def prepare_kernel(place_ref, occ_decay_ref, vir_decay_ref, occ_ref, vir_ref, out_ref):
-    row = place_ref[0]
+def prepare_kernel(row_ref, col_ref, *refs):
+    @pl.when(col_ref[0] == 0)
+    def _():
+        prepare_rows(row_ref[0], *refs)
+
+
+def prepare_rows(
+    row, occ_decay_ref, vir_decay_ref, occ_hbm, vir_hbm, out_hbm, occ_ref, vir_ref, out_ref, sems
+):
+    copies = [
+        pltpu.make_async_copy(occ_hbm.at[:, :1024], occ_ref, sems.at[0]),
+        pltpu.make_async_copy(vir_hbm.at[:, :1024], vir_ref, sems.at[1]),
+    ]
+    for copy in copies:
+        copy.start()
+    for copy in copies:
+        copy.wait()
 
     def column(decay_ref, count):
         index = lax.broadcasted_iota(jnp.int32, (count, 128), 0)
@@ -109,24 +124,27 @@
                 ).astype(BF16)
                 for xl in range(2):
                     out_ref[4 * xl + 2 * y1 + t, kind] = piece
-
-
-def prepare(place, occ_decay, vir_decay, occ, vir):
+    result = pltpu.make_async_copy(out_ref, out_hbm, sems.at[2])
+    result.start()
+    result.wait()
+
+
+def prepare(row, col, occ_decay, vir_decay, occ, vir):
     smem = pl.BlockSpec(memory_space=pltpu.SMEM)
+    hbm = pl.BlockSpec(memory_space=pl.ANY)
     return pl.pallas_call(
         prepare_kernel,
-        grid=(1,),
         out_shape=jax.ShapeDtypeStruct((8, 4, 24, 128), BF16),
-        in_specs=[
-            smem,
-            smem,
-            smem,
-            pl.BlockSpec((32, 1024), lambda i: (0, 0)),
-            pl.BlockSpec((16, 1024), lambda i: (0, 0)),
+        in_specs=[smem] * 4 + [hbm] * 2,
+        out_specs=hbm,
+        scratch_shapes=[
+            pltpu.VMEM((32, 1024), BF16),
+            pltpu.VMEM((16, 1024), BF16),
+            pltpu.VMEM((8, 4, 24, 128), BF16),
+            pltpu.SemaphoreType.DMA((3,)),
         ],
-        out_specs=pl.BlockSpec((8, 4, 24, 128), lambda i: (0, 0, 0, 0)),
         name="prepare",
-    )(place, occ_decay, vir_decay, occ, vir)
+    )(row, col, occ_decay, vir_decay, occ, vir)
 
 
 def pack_kernel(occ_ref, vir_ref, rows_ref, out_ref):
@@ -163,13 +181,14 @@
         occ_ref[rows(y1), lanes] = near[step][:256]
         occ_ref[rows(2 + y1), lanes] = near[step][256:512]
         vir_ref[rows(y1), lanes] = near[step][512:]
-    for k, ref in enumerate(points):
+    occ = jnp.concatenate([ref[:1024].T for ref in points], axis=0)
+    vir = jnp.concatenate([ref[1024:].T for ref in points], axis=0)
+    product = dot(occ, occ_ref[...]) * dot(vir, vir_ref[...]) * POLAR_FACTOR
+    for k in range(4):
         place = 2 * (z0 if k < 2 else 1 - z0) + (core if k % 2 == 0 else 1 - core)
-        green_occ = dot(ref[:1024].T, occ_ref[...])
-        green_vir = dot(ref[1024:].T, vir_ref[...])
-        polar_ref[pl.ds(pl.multiple_of(128 * place, 128), 128), :] = (
-            green_occ * green_vir * POLAR_FACTOR
-        )
+        polar_ref[pl.ds(pl.multiple_of(128 * place, 128), 128), :] = product[
+            128 * k : 128 * (k + 1)
+        ]
     for half in range(2):
         polar = polar_ref[256 * half : 256 * (half + 1), :]
         polar_high = polar.astype(BF16)
@@ -205,16 +224,32 @@
 
 def finish_kernel(x_ref, a_high_ref, a_low_ref, b_high_ref, b_low_ref, *refs):
     outs, parts, sems = refs[:2], refs[2:4], refs[4]
-    planes = []
-    for block in range(4):
-        zb, half = divmod(block, 2)
-        x = jnp.concatenate(
-            [x_ref[place_in_last(2 * k + zb, j), half] for k in range(4) for j in range(8)], axis=0
+    x = jnp.concatenate(
+        [
+            jnp.concatenate(
+                [x_ref[place_in_last(2 * k + block // 2, j), block % 2] for k in range(4) for j in range(8)],
+                axis=0,
+            )
+            for block in range(4)
+        ],
+        axis=1,
+    )
+    planes = dot(a_high_ref[...], x) + dot(a_low_ref[...], x)
+    copies = []
+    for part in range(4):
+        z = jnp.concatenate(
+            [
+                jnp.concatenate(
+                    [
+                        planes[64 * g : 64 * (g + 1), 128 * block : 128 * (block + 1)]
+                        for block in range(4)
+                    ],
+                    axis=0,
+                ).T
+                for g in (2 * part, 2 * part + 1)
+            ],
+            axis=0,
         )
-        planes.append(dot(a_high_ref[...], x) + dot(a_low_ref[...], x))
-    copies = []
-    for g in range(8):
-        z = jnp.concatenate([plane[64 * g : 64 * (g + 1)] for plane in planes], axis=0).T
         z_high = z.astype(BF16)
         z_low = (z - z_high.astype(F32)).astype(BF16)
         out = (
@@ -223,17 +258,18 @@
             + dot(z_low, b_high_ref[...])
         )
         for which in range(2):
-            for i in range(4):
-                parts[which][:, i, 128 * g : 128 * (g + 1)] = out[
-                    32 * i : 32 * (i + 1), 128 * which : 128 * (which + 1)
-                ]
-            if g % 2 == 1:
-                lanes = pl.ds(128 * (g - 1), 256)
-                copy = pltpu.make_async_copy(
-                    parts[which].at[:, :, lanes], outs[which].at[:, :, lanes], sems.at[which, g // 2]
-                )
-                copy.start()
-                copies.append(copy)
+            for g in range(2):
+                for i in range(4):
+                    rows = 128 * g + 32 * i
+                    parts[which][:, i, 128 * (2 * part + g) : 128 * (2 * part + g + 1)] = out[
+                        rows : rows + 32, 128 * which : 128 * (which + 1)
+                    ]
+            lanes = pl.ds(256 * part, 256)
+            copy = pltpu.make_async_copy(
+                parts[which].at[:, :, lanes], outs[which].at[:, :, lanes], sems.at[which, part]
+            )
+            copy.start()
+            copies.append(copy)
     for copy in copies:
         copy.wait()
 
@@ -298,8 +334,9 @@
 
 def body(occ, vir, occ_decay, vir_decay):
     row = lax.axis_index(ROW).astype(jnp.int32).reshape(1)
+    col = lax.axis_index(COL).astype(jnp.int32).reshape(1)
     place = [lax.axis_index(a).astype(jnp.int32).reshape(1) for a in ("c", "z0", Y)]
-    scattered = lax.all_to_all(prepare(row, occ_decay, vir_decay, occ, vir), COL, 0, 0, tiled=True)
+    scattered = lax.all_to_all(prepare(row, col, occ_decay, vir_decay, occ, vir), COL, 0, 0, tiled=True)
     arrived = lax.all_to_all(pack(occ, vir, scattered), ROW, 0, 0, tiled=True)
 
     def by_group(part, count):

time: 103 us -> 102 us (level)
  blocking collectives: 43.8 us -> 42.1 us
    all_to_all x1, blocking collectives: 12.5 us -> 10.8 us  [body(): lax.all_to_all(prepare(row, col, occ_decay, vir_decay, occ, vir), COL, 0,...]
where the time goes in v2:
time: 102 us
  blocking collectives  42.1 us (41%)
  waiting for transfers between devices  41.1 us (40%)
  starting transfers between devices  9.26 us (9%)
  Pallas kernels  8.01 us (8%)
    all_to_all x1, blocking collectives, body(): arrived = lax.all_to_all(pack(occ, vir, scattered), ROW, 0, 0, tiled=True)  31.3 us
    all_to_all x1, waiting for transfers between devices, body(): received = lax.all_to_all(messages, LAST, 0, 0, tiled=True)  20.6 us
    ppermute x3, waiting for transfers between devices, shift(): return lax.ppermute(x, axes, [(i, (i + by) % count) for i in range(count)])  11.3 us
    all_to_all x1, blocking collectives, body(): lax.all_to_all(prepare(row, col, occ_decay, vir_decay, occ, vir), COL, 0,...  10.8 us
    ppermute x3, waiting for transfers between devices, swap(): return lax.ppermute(x, axis, [(0, 1), (1, 0)])  9.18 us
    all_to_all x1, starting transfers between devices, body(): received = lax.all_to_all(messages, LAST, 0, 0, tiled=True)  6.02 us
    pallas_call x1, Pallas kernels, finish(): pl.pallas_call(finish_kernel, out_shape=(shape, shape), in_specs=[vmem] *...  2.76 us
    pallas_call x1, Pallas kernels, polar_messages(): pl.pallas_call(polar_kernel, out_shape=jax.ShapeDtypeStruct((64, 2, 16, 1...  2.6 us
  transfers between devices with their start and end apart: 7, of which 5 were waited for; matrix products, arithmetic and copies ran while one was open for 0% of the time, Pallas kernels for 0%

profile of v2, /device:TPU:32, one launch (start us, length us, event | category | flops | bytes accessed | tf_op | source)
XLA Modules:
  0.0 101.5 jit_solution(5495044285212563461)
XLA Ops:
  0.6 2.5 %prepare.1 = bf16[8,4,24,128]{3,2,1,0:T(8,128)(2,1)} custom-call(s32[1]{0:T(128)} %bitcast.3.row_ref, s32[1]{0:T(128)} %bitcast.4.col_ref, f32[1024]{0:T(1024)} %refs_0_.2, f32[512]{0:T(512)} %refs_1_.2, bf16[32,4096]{1,0:T(8,128)(2,1)} %occ_ref.1, bf16[16,4096]{1,0:T(8,128)(2,1)} %vir_ref.1), custom_call_target="tpu_custom_call" | custom-call | tf_op jit(solution)/shard_map/prepare/pallas_call | solution.py:135
  3.1 0.0 copy-start
  3.1 0.0 copy-start.3
  3.2 10.8 %all_to_all.15.rows_ref = bf16[8,4,24,128]{3,2,1,0:T(8,128)(2,1)S(1)} all-to-all(bf16[8,4,24,128]{3,2,1,0:T(8,128)(2,1)} %prepare.1), channel_id=1, replica_groups=mesh['xh'=2,'z2'=2,'z1'=2,'z0'=2,'c'=2,'xl'=2,'y1'=2,'y0'=2] {'xl','y1',..., dimensions={0} | all-to-all | bytes 393216 | tf_op jit(solution)/shard_map/all_to_all | solution.py:339
  13.9 0.0 copy-done
  13.9 0.0 copy-done.3
  13.9 0.1 pack.1
  14.0 31.3 %all_to_all.16 = bf16[32,72,128]{2,1,0:T(8,128)(2,1)S(1)} all-to-all(bf16[32,72,128]{2,1,0:T(8,128)(2,1)S(1)} %pack.1), channel_id=1, replica_groups=mesh['xh'=2,'z2'=2,'z1'=2,'z0'=2,'c'=2,'xl'=2,'y1'=2,'y0'=2] {'xh','z2',..., dimensions={0} | all-to-all | bytes 1179648 | tf_op jit(solution)/shard_map/all_to_all | solution.py:340
  45.5 0.8 collective-permute-start.1
  46.3 0.0 collective-permute-start
  46.3 9.2 %collective-permute-done.1.refs_2_ = bf16[1536,128]{1,0:T(8,128)(2,1)S(1)} collective-permute-done((bf16[1536,128]{1,0:T(8,128)(2,1)S(1)}, bf16[1536,128]{1,0:T(8,128)(2,1)S(1)}, u32[]{:S(2)}, u32[]{:S(2)}) %collective-permute-start.1) | collective-permute-done | bytes 393248 | tf_op jit(solution)/shard_map/ppermute | solution.py:332
  55.5 0.0 collective-permute-start.2
  55.5 0.0 copy-start.4
  55.5 0.0 copy-start.5
  55.5 1.0 collective-permute-start.5
  56.6 1.5 %collective-permute-start.4 = (bf16[768,128]{1,0:T(8,128)(2,1)S(1)}, bf16[768,128]{1,0:T(8,128)(2,1)S(1)}, u32[]{:S(2)}, u32[]{:S(2)}) collective-permute-start(bf16[768,128]{1,0:T(8,128)(2,1)S(1)} %pad_maximum_fusion.1.refs_4_), channel_id=1, source_target_pairs={{0,2},{1,3},{2,0},{3,1},{4,6},{5,7},{6,4},{7,5},{8,10},{9,11},{10,... | collective-permute-start | bytes 589832 | tf_op jit(solution)/shard_map/ppermute | solution.py:328
  58.0 0.0 collective-permute-start.3
  58.0 0.0 collective-permute-done.in_ref
  58.0 5.4 %collective-permute-done.5.refs_7_ = bf16[768,128]{1,0:T(8,128)(2,1)S(1)} collective-permute-done((bf16[768,128]{1,0:T(8,128)(2,1)S(1)}, bf16[768,128]{1,0:T(8,128)(2,1)S(1)}, u32[]{:S(2)}, u32[]{:S(2)}) %collective-permute-start.5) | collective-permute-done | bytes 196640 | tf_op jit(solution)/shard_map/ppermute | solution.py:328
  63.4 2.5 %collective-permute-done.4.refs_6_ = bf16[768,128]{1,0:T(8,128)(2,1)S(1)} collective-permute-done((bf16[768,128]{1,0:T(8,128)(2,1)S(1)}, bf16[768,128]{1,0:T(8,128)(2,1)S(1)}, u32[]{:S(2)}, u32[]{:S(2)}) %collective-permute-start.4) | collective-permute-done | bytes 196640 | tf_op jit(solution)/shard_map/ppermute | solution.py:328
  65.9 3.4 %collective-permute-done.3.refs_5_ = bf16[768,128]{1,0:T(8,128)(2,1)S(1)} collective-permute-done((bf16[768,128]{1,0:T(8,128)(2,1)S(1)}, bf16[768,128]{1,0:T(8,128)(2,1)S(1)}, u32[]{:S(2)}, u32[]{:S(2)}) %collective-permute-start.3) | collective-permute-done | bytes 196640 | tf_op jit(solution)/shard_map/ppermute | solution.py:328
  69.3 0.0 collective-permute-done.2.refs_3_
  69.3 0.0 copy-done.4
  69.3 0.0 copy-done.5
  69.3 0.0 copy-start.6
  69.3 0.0 copy-start.7
  69.3 2.6 %polar.1 = bf16[64,2,16,128]{3,2,1,0:T(8,128)(2,1)} custom-call(s32[1]{0:T(128)} %bitcast.core_ref, s32[1]{0:T(128)} %bitcast.1.z0_ref, s32[1]{0:T(128)} %bitcast.2.y_ref, bf16[1536,128]{1,0:T(8,128)(2,1)S(1)} %pad_maximum_fusion.refs_0_, bf16[1536,128]{1,0:T(8,128)(2,1)S(1)} %fence.1.refs_1_, bf16[1536,128]{1,0:T(8,128)(2,1)S(1)} %collective-permute-done.1.refs_2_, ...), custom_call_target="tpu_custom_call" | custom-call | tf_op jit(solution)/shard_map/polar/pallas_call | solution.py:210
  71.9 0.0 copy-start.1
  71.9 0.0 copy-start.2
  71.9 6.0 %all-to-all-start.2 = ((bf16[64,2,16,128]{3,2,1,0:T(8,128)(2,1)}), bf16[64,2,16,128]{3,2,1,0:T(8,128)(2,1)S(1)}, u32[]{:S(2)}, u32[]{:S(2)}) async-start(bf16[64,2,16,128]{3,2,1,0:T(8,128)(2,1)} %polar.1), calls=%async_computation.2 | async-start | bytes 1048576 | tf_op jit(solution)/shard_map/all_to_all | solution.py:358
  78.0 0.0 copy-done.6
  78.0 0.0 copy-done.7
  78.0 0.0 copy-done.1
  78.0 0.0 copy-done.2
  78.0 0.1 carry.1
  78.1 20.6 %all-to-all-done.2.x_ref = bf16[64,2,16,128]{3,2,1,0:T(8,128)(2,1)S(1)} async-done(((bf16[64,2,16,128]{3,2,1,0:T(8,128)(2,1)}), bf16[64,2,16,128]{3,2,1,0:T(8,128)(2,1)S(1)}, u32[]{:S(2)}, u32[]{:S(2)}) %all-to-all-start.2) | async-done | bytes 524320 | tf_op jit(solution)/shard_map/all_to_all | solution.py:358
  98.7 2.8 %finish.1 = (f32[32,4,1024]{2,1,0:T(4,128)}, f32[32,4,1024]{2,1,0:T(4,128)}) custom-call(bf16[64,2,16,128]{3,2,1,0:T(8,128)(2,1)S(1)} %all-to-all-done.2.x_ref, bf16[512,512]{1,0:T(8,128)(2,1)S(1)} %get-tuple-element.6.a_high_ref, bf16[512,512]{1,0:T(8,128)(2,1)S(1)} %get-tuple-element.7.a_low_ref, bf16[256,256]{1,0:T(8,128)(2,1)S(1)} %get-tuple-element.8.b_high_ref, ...), custom_call_target="tpu_custom_call" | custom-call | tf_op jit(solution)/shard_map/finish/pallas_call | solution.py:281
  (9 shorter events, 0.2 us)
Async XLA Ops:
  3.1 10.8 %copy-start = (bf16[32,4096]{1,0:T(8,128)(2,1)S(1)}, bf16[32,4096]{1,0:T(8,128)(2,1)}, u32[]{:S(2)}) copy-start(bf16[32,4096]{1,0:T(8,128)(2,1)} %occ_ref.1) | copy-start | bytes 786436
  3.1 10.8 %copy-start.3 = (bf16[16,4096]{1,0:T(8,128)(2,1)S(1)}, bf16[16,4096]{1,0:T(8,128)(2,1)}, u32[]{:S(2)}) copy-start(bf16[16,4096]{1,0:T(8,128)(2,1)} %vir_ref.1) | copy-start | bytes 393220
  45.5 9.9 %collective-permute-start.1 = (bf16[1536,128]{1,0:T(8,128)(2,1)S(1)}, bf16[1536,128]{1,0:T(8,128)(2,1)S(1)}, u32[]{:S(2)}, u32[]{:S(2)}) collective-permute-start(bf16[1536,128]{1,0:T(8,128)(2,1)S(1)} %pad_maximum_fusion.refs_0_), channel_id=1, source_target_pairs={{0,16},{16,0},{1,17},{17,1},{2,18},{18,2},{3,19},{19,3},{4,20},{20... | collective-permute-start | bytes 1179656 | tf_op jit(solution)/shard_map/ppermute | solution.py:332
  46.3 11.7 %collective-permute-start = (bf16[1536,128]{1,0:T(8,128)(2,1)S(1)}, bf16[1536,128]{1,0:T(8,128)(2,1)S(1)}, u32[]{:S(2)}, u32[]{:S(2)}) collective-permute-start(bf16[1536,128]{1,0:T(8,128)(2,1)S(1)} %pad_maximum_fusion.refs_0_), channel_id=1, source_target_pairs={{0,8},{8,0},{1,9},{9,1},{2,10},{10,2},{3,11},{11,3},{4,12},{12,4},... | collective-permute-start | bytes 1179656 | tf_op jit(solution)/shard_map/ppermute | solution.py:332
  55.5 13.8 %collective-permute-start.2 = (bf16[1536,128]{1,0:T(8,128)(2,1)S(1)}, bf16[1536,128]{1,0:T(8,128)(2,1)S(1)}, u32[]{:S(2)}, u32[]{:S(2)}) collective-permute-start(bf16[1536,128]{1,0:T(8,128)(2,1)S(1)} %collective-permute-done.1.refs_2_), channel_id=1, source_target_pairs={{0,8},{8,0},{1,9},{9,1},{2,10},{10,2},{3,11},{11,3},{4,12},{12,4},... | collective-permute-start | bytes 1179656 | tf_op jit(solution)/shard_map/ppermute | solution.py:332
  55.5 13.8 %copy-start.4 = (bf16[512,256]{1,0:T(8,128)(2,1)S(1)}, bf16[512,256]{1,0:T(8,128)(2,1)}, u32[]{:S(2)}) copy-start(bf16[512,256]{1,0:T(8,128)(2,1)} %constant.51.clone.refs_9_) | copy-start | bytes 786436
  55.5 13.8 %copy-start.5 = (bf16[512,256]{1,0:T(8,128)(2,1)S(1)}, bf16[512,256]{1,0:T(8,128)(2,1)}, u32[]{:S(2)}) copy-start(bf16[512,256]{1,0:T(8,128)(2,1)} %constant.50.clone.refs_8_) | copy-start | bytes 786436
  55.5 7.8 %collective-permute-start.5 = (bf16[768,128]{1,0:T(8,128)(2,1)S(1)}, bf16[768,128]{1,0:T(8,128)(2,1)S(1)}, u32[]{:S(2)}, u32[]{:S(2)}) collective-permute-start(bf16[768,128]{1,0:T(8,128)(2,1)S(1)} %pad_maximum_fusion.1.refs_4_), channel_id=1, source_target_pairs={{0,3},{1,0},{2,1},{3,2},{4,7},{5,4},{6,5},{7,6},{8,11},{9,8},{10,9... | collective-permute-start | bytes 589832 | tf_op jit(solution)/shard_map/ppermute | solution.py:328
  56.6 9.3 %collective-permute-start.4 = (bf16[768,128]{1,0:T(8,128)(2,1)S(1)}, bf16[768,128]{1,0:T(8,128)(2,1)S(1)}, u32[]{:S(2)}, u32[]{:S(2)}) collective-permute-start(bf16[768,128]{1,0:T(8,128)(2,1)S(1)} %pad_maximum_fusion.1.refs_4_), channel_id=1, source_target_pairs={{0,2},{1,3},{2,0},{3,1},{4,6},{5,7},{6,4},{7,5},{8,10},{9,11},{10,... | collective-permute-start | bytes 589832 | tf_op jit(solution)/shard_map/ppermute | solution.py:328
  58.0 11.3 %collective-permute-start.3 = (bf16[768,128]{1,0:T(8,128)(2,1)S(1)}, bf16[768,128]{1,0:T(8,128)(2,1)S(1)}, u32[]{:S(2)}, u32[]{:S(2)}) collective-permute-start(bf16[768,128]{1,0:T(8,128)(2,1)S(1)} %pad_maximum_fusion.1.refs_4_), channel_id=1, source_target_pairs={{0,1},{1,2},{2,3},{3,0},{4,5},{5,6},{6,7},{7,4},{8,9},{9,10},{10,1... | collective-permute-start | bytes 589832 | tf_op jit(solution)/shard_map/ppermute | solution.py:328
  69.3 8.7 %copy-start.6 = (bf16[256,256]{1,0:T(8,128)(2,1)S(1)}, bf16[256,256]{1,0:T(8,128)(2,1)}, u32[]{:S(2)}) copy-start(bf16[256,256]{1,0:T(8,128)(2,1)} %constant.55.clone.refs_3_) | copy-start | bytes 393220
  69.3 8.7 %copy-start.7 = (bf16[256,256]{1,0:T(8,128)(2,1)S(1)}, bf16[256,256]{1,0:T(8,128)(2,1)}, u32[]{:S(2)}) copy-start(bf16[256,256]{1,0:T(8,128)(2,1)} %constant.54.clone.refs_2_) | copy-start | bytes 393220
  71.9 6.1 %copy-start.1 = (bf16[512,512]{1,0:T(8,128)(2,1)S(1)}, bf16[512,512]{1,0:T(8,128)(2,1)}, u32[]{:S(2)}) copy-start(bf16[512,512]{1,0:T(8,128)(2,1)} %constant.53.clone.refs_1_) | copy-start | bytes 1572868
  71.9 6.1 %copy-start.2 = (bf16[512,512]{1,0:T(8,128)(2,1)S(1)}, bf16[512,512]{1,0:T(8,128)(2,1)}, u32[]{:S(2)}) copy-start(bf16[512,512]{1,0:T(8,128)(2,1)} %constant.52.clone.refs_0_) | copy-start | bytes 1572868
  71.9 26.8 %all-to-all-start.2 = ((bf16[64,2,16,128]{3,2,1,0:T(8,128)(2,1)}), bf16[64,2,16,128]{3,2,1,0:T(8,128)(2,1)S(1)}, u32[]{:S(2)}, u32[]{:S(2)}) async-start(bf16[64,2,16,128]{3,2,1,0:T(8,128)(2,1)} %polar.1), calls=%async_computation.2 | async-start | bytes 1048576 | tf_op jit(solution)/shard_map/all_to_all | solution.py:358

commit v3 on v2

--- a/solution.py
+++ b/solution.py
@@ -111,19 +111,20 @@
 
     occ = scaled_tiles(occ_ref, column(occ_decay_ref, 32))
     vir = scaled_tiles(vir_ref, column(vir_decay_ref, 16))
-    for y1 in range(2):
-        for t in range(2):
-            for kind in range(4):
-                piece = jnp.concatenate(
-                    [
-                        occ[t][kind][8 * y1 : 8 * (y1 + 1)],
-                        occ[t][kind][8 * (2 + y1) : 8 * (3 + y1)],
-                        vir[t][kind][8 * y1 : 8 * (y1 + 1)],
-                    ],
-                    axis=0,
-                ).astype(BF16)
-                for xl in range(2):
-                    out_ref[4 * xl + 2 * y1 + t, kind] = piece
+    for xl in range(2):
+        for y1 in range(2):
+            for t in range(2):
+                for kind in range(4):
+                    group = 2 * xl + y1
+                    piece = jnp.concatenate(
+                        [
+                            occ[t][kind][8 * group : 8 * (group + 1)],
+                            vir[t][kind][8 * y1 : 8 * (y1 + 1)],
+                        ],
+                        axis=0,
+                    )
+                    peer = 8 * (kind % 2) + 4 * xl + 2 * y1 + t
+                    out_ref[peer, kind // 2] = piece.astype(BF16)
     result = pltpu.make_async_copy(out_ref, out_hbm, sems.at[2])
     result.start()
     result.wait()
@@ -134,42 +135,66 @@
     hbm = pl.BlockSpec(memory_space=pl.ANY)
     return pl.pallas_call(
         prepare_kernel,
-        out_shape=jax.ShapeDtypeStruct((8, 4, 24, 128), BF16),
+        out_shape=jax.ShapeDtypeStruct((16, 2, 16, 128), BF16),
         in_specs=[smem] * 4 + [hbm] * 2,
         out_specs=hbm,
         scratch_shapes=[
             pltpu.VMEM((32, 1024), BF16),
             pltpu.VMEM((16, 1024), BF16),
-            pltpu.VMEM((8, 4, 24, 128), BF16),
+            pltpu.VMEM((16, 2, 16, 128), BF16),
             pltpu.SemaphoreType.DMA((3,)),
         ],
         name="prepare",
     )(row, col, occ_decay, vir_decay, occ, vir)
 
 
-def pack_kernel(occ_ref, vir_ref, rows_ref, out_ref):
-    for p in range(32):
-        out_ref[p, 0:32, :] = occ_ref[:, 128 * p : 128 * (p + 1)]
-        out_ref[p, 32:48, :] = vir_ref[:, 128 * p : 128 * (p + 1)]
-        out_ref[p, 48:72, :] = rows_ref[0, p % 4]
-
-
-def pack(occ, vir, rows):
+def divide_kernel(core_ref, occ_ref, vir_ref, kept_ref, sent_ref):
+    core = core_ref[0]
+    for out_ref, which in ((kept_ref, core), (sent_ref, 1 - core)):
+        for p in range(16):
+            lanes = pl.ds(pl.multiple_of(128 * (2 * p + which), 128), 128)
+            out_ref[p, :32, :] = occ_ref[:, lanes]
+            out_ref[p, 32:, :] = vir_ref[:, lanes]
+
+
+def divide(core, occ, vir):
+    vmem = pl.BlockSpec(memory_space=pltpu.VMEM)
+    shape = jax.ShapeDtypeStruct((16, 48, 128), BF16)
+    return pl.pallas_call(
+        divide_kernel,
+        out_shape=(shape, shape),
+        in_specs=[pl.BlockSpec(memory_space=pltpu.SMEM), vmem, vmem],
+        out_specs=(vmem, vmem),
+        compiler_params=pltpu.CompilerParams(vmem_limit_bytes=LIMIT),
+        name="divide",
+    )(core, occ, vir)
+
+
+def pack_kernel(core_ref, kept_ref, other_ref, rows_ref, out_ref):
+    core = core_ref[0]
+    out_ref[:, pl.ds(pl.multiple_of(48 * core, 16), 48), :] = kept_ref[...]
+    out_ref[:, pl.ds(pl.multiple_of(48 * (1 - core), 16), 48), :] = other_ref[...]
+    for p in range(16):
+        out_ref[p, 96:112, :] = rows_ref[0, p % 2]
+        out_ref[p, 112:128, :] = rows_ref[8, p % 2]
+
+
+def pack(core, kept, other, rows):
     vmem = pl.BlockSpec(memory_space=pltpu.VMEM)
     return pl.pallas_call(
         pack_kernel,
-        out_shape=jax.ShapeDtypeStruct((32, 72, 128), BF16),
-        in_specs=[vmem] * 3,
+        out_shape=jax.ShapeDtypeStruct((16, 128, 128), BF16),
+        in_specs=[pl.BlockSpec(memory_space=pltpu.SMEM)] + [vmem] * 3,
         out_specs=vmem,
         compiler_params=pltpu.CompilerParams(vmem_limit_bytes=LIMIT),
         name="pack",
-    )(occ, vir, rows)
-
-
-def polar_kernel(core_ref, z0_ref, y_ref, *refs):
-    points, near, (high_ref, low_ref) = refs[:4], refs[4:8], refs[8:10]
+    )(core, kept, other, rows)
+
+
+def polar_kernel(core_ref, z0_ref, xl_ref, y_ref, *refs):
+    points, near, far, (high_ref, low_ref) = refs[:4], refs[4:8], refs[8:10], refs[10:12]
     out_ref, polar_ref, occ_ref, vir_ref = refs[-4:]
-    core, z0, y = core_ref[0], z0_ref[0], y_ref[0]
+    core, z0, xl, y = core_ref[0], z0_ref[0], xl_ref[0], y_ref[0]
     for step in range(4):
         chunk = lax.rem(y + 4 - step, 4)
         y1, y0 = lax.div(chunk, 2), lax.rem(chunk, 2)
@@ -178,9 +203,11 @@
         def rows(group):
             return pl.ds(pl.multiple_of(256 * group, 256), 256)
 
-        occ_ref[rows(y1), lanes] = near[step][:256]
-        occ_ref[rows(2 + y1), lanes] = near[step][256:512]
-        vir_ref[rows(y1), lanes] = near[step][512:]
+        occ_ref[rows(2 * xl + y1), lanes] = near[step][:256]
+        occ_ref[rows(2 * (1 - xl) + y1), lanes] = far[step // 2][
+            256 * (step % 2) : 256 * (step % 2 + 1)
+        ]
+        vir_ref[rows(y1), lanes] = near[step][256:]
     occ = jnp.concatenate([ref[:1024].T for ref in points], axis=0)
     vir = jnp.concatenate([ref[1024:].T for ref in points], axis=0)
     product = dot(occ, occ_ref[...]) * dot(vir, vir_ref[...]) * POLAR_FACTOR
@@ -210,7 +237,7 @@
     return pl.pallas_call(
         polar_kernel,
         out_shape=jax.ShapeDtypeStruct((64, 2, 16, 128), BF16),
-        in_specs=[pl.BlockSpec(memory_space=pltpu.SMEM)] * 3 + [vmem] * 10,
+        in_specs=[pl.BlockSpec(memory_space=pltpu.SMEM)] * 4 + [vmem] * 12,
         out_specs=vmem,
         scratch_shapes=[
             pltpu.VMEM((512, 256), F32),
@@ -293,6 +320,23 @@
     )(x, *tables)
 
 
+def join_kernel(first_ref, second_ref, out_ref):
+    out_ref[:256] = first_ref[:256]
+    out_ref[256:] = second_ref[:256]
+
+
+def join(first, second):
+    vmem = pl.BlockSpec(memory_space=pltpu.VMEM)
+    return pl.pallas_call(
+        join_kernel,
+        out_shape=jax.ShapeDtypeStruct((512, 128), BF16),
+        in_specs=[vmem, vmem],
+        out_specs=vmem,
+        compiler_params=pltpu.CompilerParams(vmem_limit_bytes=LIMIT),
+        name="join",
+    )(first, second)
+
+
 def carry_kernel(*refs):
     count = len(refs) // 2
     for in_ref, out_ref in zip(refs[:count], refs[count:]):
@@ -335,25 +379,34 @@
 def body(occ, vir, occ_decay, vir_decay):
     row = lax.axis_index(ROW).astype(jnp.int32).reshape(1)
     col = lax.axis_index(COL).astype(jnp.int32).reshape(1)
-    place = [lax.axis_index(a).astype(jnp.int32).reshape(1) for a in ("c", "z0", Y)]
-    scattered = lax.all_to_all(prepare(row, col, occ_decay, vir_decay, occ, vir), COL, 0, 0, tiled=True)
-    arrived = lax.all_to_all(pack(occ, vir, scattered), ROW, 0, 0, tiled=True)
-
-    def by_group(part, count):
-        part = part.reshape(32, count, 8, 128)
-        return jnp.transpose(part, (1, 0, 2, 3)).reshape(256 * count, 128)
-
-    near = jnp.concatenate([by_group(arrived[:, 48:64], 2), by_group(arrived[:, 64:], 1)], axis=0)
+    place = [lax.axis_index(a).astype(jnp.int32).reshape(1) for a in ("c", "z0", "xl", Y)]
+    scattered = prepare(row, col, occ_decay, vir_decay, occ, vir)
+    scattered = lax.all_to_all(scattered, ("c", *COL), 0, 0, tiled=True)
+    kept, sent = divide(place[0], occ, vir)
+    other = swap(sent, "c")
+    arrived = lax.all_to_all(pack(place[0], kept, other, scattered), ("xh", *Z), 0, 0, tiled=True)
+
+    def by_group(first, count):
+        parts = [arrived[:, start : start + 8 * count] for start in first]
+        parts = jnp.stack([part.reshape(16, count, 8, 128) for part in parts])
+        return jnp.transpose(parts, (2, 0, 1, 3, 4)).reshape(256 * count, 128)
+
+    near = jnp.concatenate([by_group((96, 112), 1), by_group((104, 120), 1)], axis=0)
     near = [near]
     for by in (1, 2, 3):
         near.append(shift(near[0], Y, 4, by))
-    own = jnp.concatenate([by_group(arrived[:, :32], 4), by_group(arrived[:, 32:48], 2)], axis=0)
+    up = join(near[0], near[1])
+    up = shift(up, ("xh", "xl"), 4, 1)
+    down = join(near[2], near[3])
+    down = shift(down, ("xh", "xl"), 4, -1)
+
+    own = jnp.concatenate([by_group((0, 48), 4), by_group((32, 80), 2)], axis=0)
     across = swap(own, "z0")
     beside = swap(own, "c")
     beside = fence(beside)
     opposite = swap(across, "c")
     points = (own, beside, across, opposite)
-    messages = polar_messages(*place, *points, *near, *c_table())
+    messages = polar_messages(*place, *points, *near, up, down, *c_table())
 
     received = lax.all_to_all(messages, LAST, 0, 0, tiled=True)
     tables = carry(*a_table(), *b_table())

time: 102 us -> 102 us (level)
  blocking collectives: 42.1 us -> 37.5 us
  starting transfers between devices: 9.26 us -> 13 us
  local copies, waits for them, and re-layouts: 0.16 us -> 2.01 us
    all_to_all x2, blocking collectives: 42.1 us -> 37.5 us  [the longest x1 27 us: body(): lax.all_to_all(pack(place[0], kept, other, scattered), ('xh', *Z), 0, 0,...]
    ppermute x3 -> x5, starting transfers between devices: 2.48 us -> 5.11 us  [shift(): return lax.ppermute(x, axes, [(i, (i + by) % count) for i in range(count)])]
    unnamed x16, local copies, waits for them, and re-layouts: 0.05 us -> 1.88 us
    ppermute x3 -> x5, waiting for transfers between devices: 11.3 us -> 12.5 us  [shift(): return lax.ppermute(x, axes, [(i, (i + by) % count) for i in range(count)])]
    ppermute x3 -> x4, waiting for transfers between devices: 9.18 us -> 8.14 us  [swap(): return lax.ppermute(x, axis, [(0, 1), (1, 0)])]
    pallas_call x2 -> x5, Pallas kernels: 2.56 us -> 2.62 us  [the longest x1 2.45 us: prepare(): pl.pallas_call(prepare_kernel, out_shape=jax.ShapeDtypeStruct((16, 2, 16,...]
  transfers between devices with their start and end apart: 7 -> 10, of which waited for: 5 -> 7; matrix products, arithmetic and copies ran while one was open for 0% -> 0% of each run, Pallas kernels for 0% -> 3%
where the time goes in v3:
time: 102 us
  waiting for transfers between devices  40.5 us (40%)
  blocking collectives  37.5 us (37%)
  starting transfers between devices  13 us (13%)
  Pallas kernels  8.09 us (8%)
  local copies, waits for them, and re-layouts  2.01 us (2%)
    all_to_all x1, blocking collectives, body(): lax.all_to_all(pack(place[0], kept, other, scattered), ('xh', *Z), 0, 0,...  27 us
    all_to_all x1, waiting for transfers between devices, body(): received = lax.all_to_all(messages, LAST, 0, 0, tiled=True)  19.8 us
    ppermute x5, waiting for transfers between devices, shift(): return lax.ppermute(x, axes, [(i, (i + by) % count) for i in range(count)])  12.5 us
    all_to_all x1, blocking collectives, body(): scattered = lax.all_to_all(scattered, ('c', *COL), 0, 0, tiled=True)  10.4 us
    ppermute x4, waiting for transfers between devices, swap(): return lax.ppermute(x, axis, [(0, 1), (1, 0)])  8.14 us
    all_to_all x1, starting transfers between devices, body(): received = lax.all_to_all(messages, LAST, 0, 0, tiled=True)  6.76 us
    ppermute x5, starting transfers between devices, shift(): return lax.ppermute(x, axes, [(i, (i + by) % count) for i in range(count)])  5.11 us
    pallas_call x1, Pallas kernels, finish(): pl.pallas_call(finish_kernel, out_shape=(shape, shape), in_specs=[vmem] *...  2.76 us
  transfers between devices with their start and end apart: 10, of which 7 were waited for; matrix products, arithmetic and copies ran while one was open for 0% of the time, Pallas kernels for 3%

profile of v3, /device:TPU:32, one launch (start us, length us, event | category | flops | bytes accessed | tf_op | source)
XLA Modules:
  0.0 102.0 jit_solution(17112983325853188769)
XLA Ops:
  0.6 0.0 copy-start
  0.6 0.9 copy-done
  1.6 0.0 copy-start.3
  1.6 0.9 copy-done.3
  2.5 0.1 divide.1
  2.6 0.1 collective-permute-start
  2.7 2.5 %prepare.1 = bf16[16,2,16,128]{3,2,1,0:T(8,128)(2,1)} custom-call(s32[1]{0:T(128)} %bitcast.4.row_ref, s32[1]{0:T(128)} %bitcast.5.col_ref, f32[1024]{0:T(1024)} %refs_0_.2, f32[512]{0:T(512)} %refs_1_.2, bf16[32,4096]{1,0:T(8,128)(2,1)} %refs_2_.2, bf16[16,4096]{1,0:T(8,128)(2,1)} %refs_3_.2), custom_call_target="tpu_custom_call" | custom-call | tf_op jit(solution)/shard_map/prepare/pallas_call | solution.py:136
  5.2 10.4 %all_to_all.15.rows_ref = bf16[16,2,16,128]{3,2,1,0:T(8,128)(2,1)S(1)} all-to-all(bf16[16,2,16,128]{3,2,1,0:T(8,128)(2,1)} %prepare.1), channel_id=1, replica_groups=mesh['xh'=2,'z2'=2,'z1'=2,'z0'=2,'c'=2,'xl'=2,'y1'=2,'y0'=2] {'c','xl','..., dimensions={0} | all-to-all | bytes 262144 | tf_op jit(solution)/shard_map/all_to_all | solution.py:384
  15.6 0.0 collective-permute-done.other_ref
  15.7 27.0 %all_to_all.16 = bf16[16,128,128]{2,1,0:T(8,128)(2,1)S(1)} all-to-all(bf16[16,128,128]{2,1,0:T(8,128)(2,1)S(1)} %pack.1), channel_id=1, replica_groups=mesh['xh'=2,'z2'=2,'z1'=2,'z0'=2,'c'=2,'xl'=2,'y1'=2,'y0'=2] {'xh','z2',..., dimensions={0} | all-to-all | bytes 1048576 | tf_op jit(solution)/shard_map/all_to_all | solution.py:387
  42.9 1.0 %collective-permute-start.2 = (bf16[1536,128]{1,0:T(8,128)(2,1)S(1)}, bf16[1536,128]{1,0:T(8,128)(2,1)S(1)}, u32[]{:S(2)}, u32[]{:S(2)}) collective-permute-start(bf16[1536,128]{1,0:T(8,128)(2,1)S(1)} %pad_maximum_fusion.refs_0_), channel_id=1, source_target_pairs={{0,16},{16,0},{1,17},{17,1},{2,18},{18,2},{3,19},{19,3},{4,20},{20... | collective-permute-start | bytes 1179656 | tf_op jit(solution)/shard_map/ppermute | solution.py:376
  44.0 0.0 collective-permute-start.1
  44.0 8.1 %collective-permute-done.2.refs_2_ = bf16[1536,128]{1,0:T(8,128)(2,1)S(1)} collective-permute-done((bf16[1536,128]{1,0:T(8,128)(2,1)S(1)}, bf16[1536,128]{1,0:T(8,128)(2,1)S(1)}, u32[]{:S(2)}, u32[]{:S(2)}) %collective-permute-start.2) | collective-permute-done | bytes 393248 | tf_op jit(solution)/shard_map/ppermute | solution.py:376
  52.1 0.0 collective-permute-start.3
  52.2 1.0 collective-permute-start.6
  53.2 1.9 %collective-permute-start.5 = (bf16[512,128]{1,0:T(8,128)(2,1)S(1)}, bf16[512,128]{1,0:T(8,128)(2,1)S(1)}, u32[]{:S(2)}, u32[]{:S(2)}) collective-permute-start(bf16[512,128]{1,0:T(8,128)(2,1)S(1)} %pad_maximum_fusion.3.first_ref.refs_4_), channel_id=1, source_target_pairs={{0,2},{1,3},{2,0},{3,1},{4,6},{5,7},{6,4},{7,5},{8,10},{9,11},{10,... | collective-permute-start | bytes 393224 | tf_op jit(solution)/shard_map/ppermute | solution.py:372
  55.1 0.0 collective-permute-start.4
  55.1 3.5 %collective-permute-done.6.second_ref.refs_7_ = bf16[512,128]{1,0:T(8,128)(2,1)S(1)} collective-permute-done((bf16[512,128]{1,0:T(8,128)(2,1)S(1)}, bf16[512,128]{1,0:T(8,128)(2,1)S(1)}, u32[]{:S(2)}, u32[]{:S(2)}) %collective-permute-start.6) | collective-permute-done | bytes 131104 | tf_op jit(solution)/shard_map/ppermute | solution.py:372
  58.6 2.4 %collective-permute-done.5.first_ref.refs_6_ = bf16[512,128]{1,0:T(8,128)(2,1)S(1)} collective-permute-done((bf16[512,128]{1,0:T(8,128)(2,1)S(1)}, bf16[512,128]{1,0:T(8,128)(2,1)S(1)}, u32[]{:S(2)}, u32[]{:S(2)}) %collective-permute-start.5) | collective-permute-done | bytes 131104 | tf_op jit(solution)/shard_map/ppermute | solution.py:372
  61.1 2.0 %collective-permute-start.8 = (bf16[512,128]{1,0:T(8,128)(2,1)S(1)}, bf16[512,128]{1,0:T(8,128)(2,1)S(1)}, u32[]{:S(2)}, u32[]{:S(2)}) collective-permute-start(bf16[512,128]{1,0:T(8,128)(2,1)S(1)} %join.3), channel_id=1, source_target_pairs={{0,132},{4,0},{128,4},{132,128},{1,133},{5,1},{129,5},{133,129},{2... | collective-permute-start | bytes 393224 | tf_op jit(solution)/shard_map/ppermute | solution.py:372
  63.0 0.1 collective-permute-done.4.second_ref.refs_5_
  63.1 0.0 copy-start.4
  63.1 0.0 copy-start.5
  63.2 0.3 collective-permute-start.7
  63.4 0.0 collective-permute-done.1.in_ref
  63.4 2.7 %collective-permute-done.8.refs_9_ = bf16[512,128]{1,0:T(8,128)(2,1)S(1)} collective-permute-done((bf16[512,128]{1,0:T(8,128)(2,1)S(1)}, bf16[512,128]{1,0:T(8,128)(2,1)S(1)}, u32[]{:S(2)}, u32[]{:S(2)}) %collective-permute-start.8) | collective-permute-done | bytes 131104 | tf_op jit(solution)/shard_map/ppermute | solution.py:372
  66.1 3.7 %collective-permute-done.7.refs_8_ = bf16[512,128]{1,0:T(8,128)(2,1)S(1)} collective-permute-done((bf16[512,128]{1,0:T(8,128)(2,1)S(1)}, bf16[512,128]{1,0:T(8,128)(2,1)S(1)}, u32[]{:S(2)}, u32[]{:S(2)}) %collective-permute-start.7) | collective-permute-done | bytes 131104 | tf_op jit(solution)/shard_map/ppermute | solution.py:372
  69.8 0.0 collective-permute-done.3.refs_3_
  69.8 0.0 copy-done.4
  69.8 0.0 copy-done.5
  69.8 0.0 copy-start.6
  69.9 0.0 copy-start.7
  69.9 2.6 %polar.1 = bf16[64,2,16,128]{3,2,1,0:T(8,128)(2,1)} custom-call(s32[1]{0:T(128)} %bitcast.core_ref, s32[1]{0:T(128)} %bitcast.1.z0_ref, s32[1]{0:T(128)} %bitcast.2.xl_ref, s32[1]{0:T(128)} %bitcast.3.y_ref, bf16[1536,128]{1,0:T(8,128)(2,1)S(1)} %pad_maximum_fusion.refs_0_, bf16[1536,128]{1,0:T(8,128)(2,1)S(1)} %fence.1.refs_1_, ...), custom_call_target="tpu_custom_call" | custom-call | tf_op jit(solution)/shard_map/polar/pallas_call | solution.py:237
  72.5 0.0 copy-start.1
  72.5 0.0 copy-start.2
  72.5 6.8 %all-to-all-start.2 = ((bf16[64,2,16,128]{3,2,1,0:T(8,128)(2,1)}), bf16[64,2,16,128]{3,2,1,0:T(8,128)(2,1)S(1)}, u32[]{:S(2)}, u32[]{:S(2)}) async-start(bf16[64,2,16,128]{3,2,1,0:T(8,128)(2,1)} %polar.1), calls=%async_computation.2 | async-start | bytes 1048576 | tf_op jit(solution)/shard_map/all_to_all | solution.py:411
  79.3 0.0 copy-done.6
  79.3 0.0 copy-done.7
  79.3 0.0 copy-done.1
  79.3 0.0 copy-done.2
  79.3 0.1 carry.1
  79.4 19.8 %all-to-all-done.2.x_ref = bf16[64,2,16,128]{3,2,1,0:T(8,128)(2,1)S(1)} async-done(((bf16[64,2,16,128]{3,2,1,0:T(8,128)(2,1)}), bf16[64,2,16,128]{3,2,1,0:T(8,128)(2,1)S(1)}, u32[]{:S(2)}, u32[]{:S(2)}) %all-to-all-start.2) | async-done | bytes 524320 | tf_op jit(solution)/shard_map/all_to_all | solution.py:411
  99.2 2.8 %finish.1 = (f32[32,4,1024]{2,1,0:T(4,128)}, f32[32,4,1024]{2,1,0:T(4,128)}) custom-call(bf16[64,2,16,128]{3,2,1,0:T(8,128)(2,1)S(1)} %all-to-all-done.2.x_ref, bf16[512,512]{1,0:T(8,128)(2,1)S(1)} %get-tuple-element.10.a_high_ref, bf16[512,512]{1,0:T(8,128)(2,1)S(1)} %get-tuple-element.11.a_low_ref, bf16[256,256]{1,0:T(8,128)(2,1)S(1)} %get-tuple-element.12.b_high_ref, ...), custom_call_target="tpu_custom_call" | custom-call | tf_op jit(solution)/shard_map/finish/pallas_call | solution.py:308
  (14 shorter events, 0.3 us)
Async XLA Ops:
  0.6 1.0 copy-start
  1.6 0.9 copy-start.3
  2.6 13.0 %collective-permute-start = (bf16[16,48,128]{2,1,0:T(8,128)(2,1)S(1)}, bf16[16,48,128]{2,1,0:T(8,128)(2,1)S(1)}, u32[]{:S(2)}, u32[]{:S(2)}) collective-permute-start(bf16[16,48,128]{2,1,0:T(8,128)(2,1)S(1)} %get-tuple-element.9), channel_id=1, source_target_pairs={{0,8},{8,0},{1,9},{9,1},{2,10},{10,2},{3,11},{11,3},{4,12},{12,4},... | collective-permute-start | bytes 589832 | tf_op jit(solution)/shard_map/ppermute | solution.py:376
  42.9 9.2 %collective-permute-start.2 = (bf16[1536,128]{1,0:T(8,128)(2,1)S(1)}, bf16[1536,128]{1,0:T(8,128)(2,1)S(1)}, u32[]{:S(2)}, u32[]{:S(2)}) collective-permute-start(bf16[1536,128]{1,0:T(8,128)(2,1)S(1)} %pad_maximum_fusion.refs_0_), channel_id=1, source_target_pairs={{0,16},{16,0},{1,17},{17,1},{2,18},{18,2},{3,19},{19,3},{4,20},{20... | collective-permute-start | bytes 1179656 | tf_op jit(solution)/shard_map/ppermute | solution.py:376
  44.0 19.5 %collective-permute-start.1 = (bf16[1536,128]{1,0:T(8,128)(2,1)S(1)}, bf16[1536,128]{1,0:T(8,128)(2,1)S(1)}, u32[]{:S(2)}, u32[]{:S(2)}) collective-permute-start(bf16[1536,128]{1,0:T(8,128)(2,1)S(1)} %pad_maximum_fusion.refs_0_), channel_id=1, source_target_pairs={{0,8},{8,0},{1,9},{9,1},{2,10},{10,2},{3,11},{11,3},{4,12},{12,4},... | collective-permute-start | bytes 1179656 | tf_op jit(solution)/shard_map/ppermute | solution.py:376
  52.1 17.7 %collective-permute-start.3 = (bf16[1536,128]{1,0:T(8,128)(2,1)S(1)}, bf16[1536,128]{1,0:T(8,128)(2,1)S(1)}, u32[]{:S(2)}, u32[]{:S(2)}) collective-permute-start(bf16[1536,128]{1,0:T(8,128)(2,1)S(1)} %collective-permute-done.2.refs_2_), channel_id=1, source_target_pairs={{0,8},{8,0},{1,9},{9,1},{2,10},{10,2},{3,11},{11,3},{4,12},{12,4},... | collective-permute-start | bytes 1179656 | tf_op jit(solution)/shard_map/ppermute | solution.py:376
  52.2 6.4 %collective-permute-start.6 = (bf16[512,128]{1,0:T(8,128)(2,1)S(1)}, bf16[512,128]{1,0:T(8,128)(2,1)S(1)}, u32[]{:S(2)}, u32[]{:S(2)}) collective-permute-start(bf16[512,128]{1,0:T(8,128)(2,1)S(1)} %pad_maximum_fusion.3.first_ref.refs_4_), channel_id=1, source_target_pairs={{0,3},{1,0},{2,1},{3,2},{4,7},{5,4},{6,5},{7,6},{8,11},{9,8},{10,9... | collective-permute-start | bytes 393224 | tf_op jit(solution)/shard_map/ppermute | solution.py:372
  53.2 7.9 %collective-permute-start.5 = (bf16[512,128]{1,0:T(8,128)(2,1)S(1)}, bf16[512,128]{1,0:T(8,128)(2,1)S(1)}, u32[]{:S(2)}, u32[]{:S(2)}) collective-permute-start(bf16[512,128]{1,0:T(8,128)(2,1)S(1)} %pad_maximum_fusion.3.first_ref.refs_4_), channel_id=1, source_target_pairs={{0,2},{1,3},{2,0},{3,1},{4,6},{5,7},{6,4},{7,5},{8,10},{9,11},{10,... | collective-permute-start | bytes 393224 | tf_op jit(solution)/shard_map/ppermute | solution.py:372
  55.1 8.1 %collective-permute-start.4 = (bf16[512,128]{1,0:T(8,128)(2,1)S(1)}, bf16[512,128]{1,0:T(8,128)(2,1)S(1)}, u32[]{:S(2)}, u32[]{:S(2)}) collective-permute-start(bf16[512,128]{1,0:T(8,128)(2,1)S(1)} %pad_maximum_fusion.3.first_ref.refs_4_), channel_id=1, source_target_pairs={{0,1},{1,2},{2,3},{3,0},{4,5},{5,6},{6,7},{7,4},{8,9},{9,10},{10,1... | collective-permute-start | bytes 393224 | tf_op jit(solution)/shard_map/ppermute | solution.py:372
  61.1 5.0 %collective-permute-start.8 = (bf16[512,128]{1,0:T(8,128)(2,1)S(1)}, bf16[512,128]{1,0:T(8,128)(2,1)S(1)}, u32[]{:S(2)}, u32[]{:S(2)}) collective-permute-start(bf16[512,128]{1,0:T(8,128)(2,1)S(1)} %join.3), channel_id=1, source_target_pairs={{0,132},{4,0},{128,4},{132,128},{1,133},{5,1},{129,5},{133,129},{2... | collective-permute-start | bytes 393224 | tf_op jit(solution)/shard_map/ppermute | solution.py:372
  63.1 6.7 %copy-start.4 = (bf16[512,256]{1,0:T(8,128)(2,1)S(1)}, bf16[512,256]{1,0:T(8,128)(2,1)}, u32[]{:S(2)}) copy-start(bf16[512,256]{1,0:T(8,128)(2,1)} %constant.51.clone.refs_11_) | copy-start | bytes 786436
  63.1 6.7 %copy-start.5 = (bf16[512,256]{1,0:T(8,128)(2,1)S(1)}, bf16[512,256]{1,0:T(8,128)(2,1)}, u32[]{:S(2)}) copy-start(bf16[512,256]{1,0:T(8,128)(2,1)} %constant.50.clone.refs_10_) | copy-start | bytes 786436
  63.2 6.7 %collective-permute-start.7 = (bf16[512,128]{1,0:T(8,128)(2,1)S(1)}, bf16[512,128]{1,0:T(8,128)(2,1)S(1)}, u32[]{:S(2)}, u32[]{:S(2)}) collective-permute-start(bf16[512,128]{1,0:T(8,128)(2,1)S(1)} %join.2), channel_id=1, source_target_pairs={{0,4},{4,128},{128,132},{132,0},{1,5},{5,129},{129,133},{133,1},{2... | collective-permute-start | bytes 393224 | tf_op jit(solution)/shard_map/ppermute | solution.py:372
  69.8 9.4 %copy-start.6 = (bf16[256,256]{1,0:T(8,128)(2,1)S(1)}, bf16[256,256]{1,0:T(8,128)(2,1)}, u32[]{:S(2)}) copy-start(bf16[256,256]{1,0:T(8,128)(2,1)} %constant.55.clone.refs_3_) | copy-start | bytes 393220
  69.9 9.4 %copy-start.7 = (bf16[256,256]{1,0:T(8,128)(2,1)S(1)}, bf16[256,256]{1,0:T(8,128)(2,1)}, u32[]{:S(2)}) copy-start(bf16[256,256]{1,0:T(8,128)(2,1)} %constant.54.clone.refs_2_) | copy-start | bytes 393220
  72.5 6.8 %copy-start.1 = (bf16[512,512]{1,0:T(8,128)(2,1)S(1)}, bf16[512,512]{1,0:T(8,128)(2,1)}, u32[]{:S(2)}) copy-start(bf16[512,512]{1,0:T(8,128)(2,1)} %constant.53.clone.refs_1_) | copy-start | bytes 1572868
  72.5 6.8 %copy-start.2 = (bf16[512,512]{1,0:T(8,128)(2,1)S(1)}, bf16[512,512]{1,0:T(8,128)(2,1)}, u32[]{:S(2)}) copy-start(bf16[512,512]{1,0:T(8,128)(2,1)} %constant.52.clone.refs_0_) | copy-start | bytes 1572868
  72.5 26.7 %all-to-all-start.2 = ((bf16[64,2,16,128]{3,2,1,0:T(8,128)(2,1)}), bf16[64,2,16,128]{3,2,1,0:T(8,128)(2,1)S(1)}, u32[]{:S(2)}, u32[]{:S(2)}) async-start(bf16[64,2,16,128]{3,2,1,0:T(8,128)(2,1)} %polar.1), calls=%async_computation.2 | async-start | bytes 1048576 | tf_op jit(solution)/shard_map/all_to_all | solution.py:411

commit v4 on v2

--- a/solution.py
+++ b/solution.py
@@ -79,8 +79,9 @@
 
 
 def prepare_rows(
-    row, occ_decay_ref, vir_decay_ref, occ_hbm, vir_hbm, out_hbm, occ_ref, vir_ref, out_ref, sems
+    row, occ_decay_ref, vir_decay_ref, occ_hbm, vir_hbm, *refs
 ):
+    out_hbm, (occ_ref, vir_ref, out_ref, sems) = refs[:4], refs[4:]
     copies = [
         pltpu.make_async_copy(occ_hbm.at[:, :1024], occ_ref, sems.at[0]),
         pltpu.make_async_copy(vir_hbm.at[:, :1024], vir_ref, sems.at[1]),
@@ -113,20 +114,21 @@
     vir = scaled_tiles(vir_ref, column(vir_decay_ref, 16))
     for y1 in range(2):
         for t in range(2):
-            for kind in range(4):
-                piece = jnp.concatenate(
-                    [
-                        occ[t][kind][8 * y1 : 8 * (y1 + 1)],
-                        occ[t][kind][8 * (2 + y1) : 8 * (3 + y1)],
-                        vir[t][kind][8 * y1 : 8 * (y1 + 1)],
-                    ],
-                    axis=0,
-                ).astype(BF16)
-                for xl in range(2):
-                    out_ref[4 * xl + 2 * y1 + t, kind] = piece
-    result = pltpu.make_async_copy(out_ref, out_hbm, sems.at[2])
-    result.start()
-    result.wait()
+            for core in range(2):
+                pieces = []
+                for z0 in range(2):
+                    kind = 2 * z0 + core
+                    pieces.append(occ[t][kind][8 * y1 : 8 * (y1 + 1)])
+                    pieces.append(occ[t][kind][8 * (2 + y1) : 8 * (3 + y1)])
+                    pieces.append(vir[t][kind][8 * y1 : 8 * (y1 + 1)])
+                out_ref[2 * y1 + t, core] = jnp.concatenate(pieces, axis=0).astype(BF16)
+    results = [
+        pltpu.make_async_copy(out_ref.at[y], out_hbm[y], sems.at[2 + y]) for y in range(4)
+    ]
+    for result in results:
+        result.start()
+    for result in results:
+        result.wait()
 
 
 def prepare(row, col, occ_decay, vir_decay, occ, vir):
@@ -134,36 +136,85 @@
     hbm = pl.BlockSpec(memory_space=pl.ANY)
     return pl.pallas_call(
         prepare_kernel,
-        out_shape=jax.ShapeDtypeStruct((8, 4, 24, 128), BF16),
+        out_shape=[jax.ShapeDtypeStruct((2, 48, 128), BF16)] * 4,
         in_specs=[smem] * 4 + [hbm] * 2,
-        out_specs=hbm,
+        out_specs=[hbm] * 4,
         scratch_shapes=[
             pltpu.VMEM((32, 1024), BF16),
             pltpu.VMEM((16, 1024), BF16),
-            pltpu.VMEM((8, 4, 24, 128), BF16),
-            pltpu.SemaphoreType.DMA((3,)),
+            pltpu.VMEM((4, 2, 48, 128), BF16),
+            pltpu.SemaphoreType.DMA((6,)),
         ],
         name="prepare",
     )(row, col, occ_decay, vir_decay, occ, vir)
 
 
-def pack_kernel(occ_ref, vir_ref, rows_ref, out_ref):
-    for p in range(32):
-        out_ref[p, 0:32, :] = occ_ref[:, 128 * p : 128 * (p + 1)]
-        out_ref[p, 32:48, :] = vir_ref[:, 128 * p : 128 * (p + 1)]
-        out_ref[p, 48:72, :] = rows_ref[0, p % 4]
-
-
-def pack(occ, vir, rows):
+def divide_kernel(core_ref, occ_ref, vir_ref, kept_ref, sent_ref):
+    core = core_ref[0]
+    for out_ref, which in ((kept_ref, core), (sent_ref, 1 - core)):
+        for p in range(16):
+            lanes = pl.ds(pl.multiple_of(128 * (2 * p + which), 128), 128)
+            out_ref[p, :32, :] = occ_ref[:, lanes]
+            out_ref[p, 32:, :] = vir_ref[:, lanes]
+
+
+def divide(core, occ, vir):
     vmem = pl.BlockSpec(memory_space=pltpu.VMEM)
-    return pl.pallas_call(
-        pack_kernel,
-        out_shape=jax.ShapeDtypeStruct((32, 72, 128), BF16),
-        in_specs=[vmem] * 3,
-        out_specs=vmem,
-        compiler_params=pltpu.CompilerParams(vmem_limit_bytes=LIMIT),
-        name="pack",
-    )(occ, vir, rows)
+    shape = jax.ShapeDtypeStruct((16, 48, 128), BF16)
+    return pl.pallas_call(
+        divide_kernel,
+        out_shape=(shape, shape),
+        in_specs=[pl.BlockSpec(memory_space=pltpu.SMEM), vmem, vmem],
+        out_specs=(vmem, vmem),
+        compiler_params=pltpu.CompilerParams(vmem_limit_bytes=LIMIT),
+        name="divide",
+    )(core, occ, vir)
+
+
+def call(kernel, out_shapes, scalars, *arrays):
+    vmem = pl.BlockSpec(memory_space=pltpu.VMEM)
+    smem = pl.BlockSpec(memory_space=pltpu.SMEM)
+    return pl.pallas_call(
+        kernel,
+        out_shape=[jax.ShapeDtypeStruct(shape, BF16) for shape in out_shapes],
+        in_specs=[smem] * len(scalars) + [vmem] * len(arrays),
+        out_specs=[vmem] * len(out_shapes),
+        compiler_params=pltpu.CompilerParams(vmem_limit_bytes=LIMIT),
+    )(*scalars, *arrays)
+
+
+def pack_kernel(core_ref, kept_ref, other_ref, out_ref):
+    core = core_ref[0]
+    out_ref[:, pl.ds(pl.multiple_of(48 * core, 16), 48), :] = kept_ref[...]
+    out_ref[:, pl.ds(pl.multiple_of(48 * (1 - core), 16), 48), :] = other_ref[...]
+
+
+def choose_y_kernel(y_ref, *refs):
+    for y in range(4):
+
+        @pl.when(y_ref[0] == y)
+        def _():
+            refs[4][...] = refs[y][...]
+
+
+def choose_x_kernel(xl_ref, core_ref, *refs):
+    for xl in range(2):
+
+        @pl.when(xl_ref[0] == xl)
+        def _():
+            refs[2][...] = refs[xl][core_ref[0]]
+            refs[3][...] = refs[xl][1 - core_ref[0]]
+
+
+def pack_share_kernel(core_ref, kept_ref, other_ref, out_ref):
+    for core in range(2):
+        for ref, own in ((kept_ref, core), (other_ref, 1 - core)):
+
+            @pl.when(core_ref[0] == own)
+            def _():
+                for p in range(16):
+                    rows = 24 * (p % 2)
+                    out_ref[p, 24 * core : 24 * (core + 1), :] = ref[rows : rows + 24, :]
 
 
 def polar_kernel(core_ref, z0_ref, y_ref, *refs):
@@ -332,29 +383,47 @@
     return lax.ppermute(x, axis, [(0, 1), (1, 0)])
 
 
+def by_group(part, first, count):
+    parts = [part[:, start : start + 8 * count] for start in first]
+    parts = jnp.stack([part.reshape(16, count, 8, 128) for part in parts])
+    return jnp.transpose(parts, (2, 0, 1, 3, 4)).reshape(256 * count, 128)
+
+
 def body(occ, vir, occ_decay, vir_decay):
-    row = lax.axis_index(ROW).astype(jnp.int32).reshape(1)
-    col = lax.axis_index(COL).astype(jnp.int32).reshape(1)
-    place = [lax.axis_index(a).astype(jnp.int32).reshape(1) for a in ("c", "z0", Y)]
-    scattered = lax.all_to_all(prepare(row, col, occ_decay, vir_decay, occ, vir), COL, 0, 0, tiled=True)
-    arrived = lax.all_to_all(pack(occ, vir, scattered), ROW, 0, 0, tiled=True)
-
-    def by_group(part, count):
-        part = part.reshape(32, count, 8, 128)
-        return jnp.transpose(part, (1, 0, 2, 3)).reshape(256 * count, 128)
-
-    near = jnp.concatenate([by_group(arrived[:, 48:64], 2), by_group(arrived[:, 64:], 1)], axis=0)
-    near = [near]
+    def index(axes):
+        return lax.axis_index(axes).astype(jnp.int32).reshape(1)
+
+    core, xl, y = index("c"), index("xl"), index(Y)
+
+    kept, sent = divide(core, occ, vir)
+    other = swap(sent, "c")
+    packed = call(pack_kernel, [(16, 96, 128)], [core], kept, other)[0]
+    arrived = lax.all_to_all(packed, ("xh", *Z), 0, 0, tiled=True)
+
+    pieces = list(prepare(index(ROW), index(COL), occ_decay, vir_decay, occ, vir))
+    for by in (1, 2, 3):
+        pieces[by] = lax.ppermute(pieces[by], COL, [(0, by)])
+    piece = call(choose_y_kernel, [(2, 48, 128)], [y], *pieces)[0]
+    handed = lax.ppermute(piece, COL, [(k, 4 + k) for k in range(4)])
+    shapes = [(48, 128)] * 2
+    kept, sent = call(choose_x_kernel, shapes, [xl, core], piece, handed)
+    other = swap(sent, "c")
+    share = call(pack_share_kernel, [(16, 48, 128)], [core], kept, other)[0]
+    share = lax.all_to_all(share, ("xh", *Z), 0, 0, tiled=True)
+
+    parts = [by_group(share, (8 * k, 24 + 8 * k), 1) for k in range(3)]
+    near = [jnp.concatenate(parts, axis=0)]
     for by in (1, 2, 3):
         near.append(shift(near[0], Y, 4, by))
-    own = jnp.concatenate([by_group(arrived[:, :32], 4), by_group(arrived[:, 32:48], 2)], axis=0)
+
+    own = jnp.concatenate([by_group(arrived, (0, 48), 4), by_group(arrived, (32, 80), 2)], axis=0)
     across = swap(own, "z0")
     beside = swap(own, "c")
     beside = fence(beside)
     opposite = swap(across, "c")
     points = (own, beside, across, opposite)
+    place = (core, index("z0"), y)
     messages = polar_messages(*place, *points, *near, *c_table())
-
     received = lax.all_to_all(messages, LAST, 0, 0, tiled=True)
     tables = carry(*a_table(), *b_table())
     return finish(received, *tables)

time: 102 us -> 109 us (1.069)
  blocking collectives: 42.1 us -> 0 us
  starting transfers between devices: 9.26 us -> 44 us
  waiting for transfers between devices: 41.1 us -> 50.8 us
  local copies, waits for them, and re-layouts: 0.16 us -> 2.75 us
  Pallas kernels: 8.01 us -> 9.51 us
    all_to_all x2 -> x0, blocking collectives: 42.1 us -> none  [the longest x1 31.3 us: body(): arrived = lax.all_to_all(pack(occ, vir, scattered), ROW, 0, 0, tiled=True)]
    all_to_all x0 -> x2, starting transfers between devices: none -> 20.7 us  [the longest x1 11 us: body(): arrived = lax.all_to_all(packed, ('xh', *Z), 0, 0, tiled=True)]
    all_to_all x0 -> x2, waiting for transfers between devices: none -> 10.3 us  [the longest x1 10.3 us: body(): share = lax.all_to_all(share, ('xh', *Z), 0, 0, tiled=True)]
    ppermute x0 -> x4, starting transfers between devices: none -> 6.7 us  [the longest x3 5.42 us: body(): pieces[by] = lax.ppermute(pieces[by], COL, [(0, by)])]
    all_to_all x1, starting transfers between devices: 6.02 us -> 11.7 us  [body(): received = lax.all_to_all(messages, LAST, 0, 0, tiled=True)]
    ppermute x3 -> x5, waiting for transfers between devices: 9.18 us -> 5.26 us  [swap(): return lax.ppermute(x, axis, [(0, 1), (1, 0)])]
    ppermute x0 -> x4, waiting for transfers between devices: none -> 3.21 us  [the longest x3 1.7 us: body(): pieces[by] = lax.ppermute(pieces[by], COL, [(0, by)])]
    unnamed x16 -> x18, local copies, waits for them, and re-layouts: 0.05 us -> 2.62 us
  transfers between devices with their start and end apart: 7 -> 15, of which waited for: 5 -> 11; matrix products, arithmetic and copies ran while one was open for 0% -> 0% of each run, Pallas kernels for 0% -> 3%
where the time goes in v4:
time: 109 us; the launch traced here: 108 us
  waiting for transfers between devices  50.8 us (47%)
  starting transfers between devices  44 us (40%)
  Pallas kernels  9.51 us (9%)
  local copies, waits for them, and re-layouts  2.75 us (3%)
    all_to_all x1, waiting for transfers between devices, body(): received = lax.all_to_all(messages, LAST, 0, 0, tiled=True)  20.5 us
    all_to_all x1, starting transfers between devices, body(): received = lax.all_to_all(messages, LAST, 0, 0, tiled=True)  11.7 us
    ppermute x3, waiting for transfers between devices, shift(): return lax.ppermute(x, axes, [(i, (i + by) % count) for i in range(count)])  11.5 us
    all_to_all x1, starting transfers between devices, body(): arrived = lax.all_to_all(packed, ('xh', *Z), 0, 0, tiled=True)  11 us
    all_to_all x1, waiting for transfers between devices, body(): share = lax.all_to_all(share, ('xh', *Z), 0, 0, tiled=True)  10.3 us
    all_to_all x1, starting transfers between devices, body(): share = lax.all_to_all(share, ('xh', *Z), 0, 0, tiled=True)  9.63 us
    ppermute x3, starting transfers between devices, body(): pieces[by] = lax.ppermute(pieces[by], COL, [(0, by)])  5.42 us
    ppermute x5, waiting for transfers between devices, swap(): return lax.ppermute(x, axis, [(0, 1), (1, 0)])  5.26 us
  transfers between devices with their start and end apart: 15, of which 11 were waited for; matrix products, arithmetic and copies ran while one was open for 0% of the time, Pallas kernels for 3%

profile of v4, /device:TPU:32, one launch (start us, length us, event | category | flops | bytes accessed | tf_op | source)
XLA Modules:
  0.0 108.0 jit_solution(5520468190625442581)
XLA Ops:
  0.6 0.0 copy-start
  0.6 0.9 copy-done
  1.6 0.0 copy-start.1
  1.6 0.9 copy-done.1
  2.5 0.1 divide.1
  2.6 0.1 collective-permute-start
  2.7 1.4 %collective-permute-done.other_ref = bf16[16,48,128]{2,1,0:T(8,128)(2,1)S(1)} collective-permute-done((bf16[16,48,128]{2,1,0:T(8,128)(2,1)S(1)}, bf16[16,48,128]{2,1,0:T(8,128)(2,1)S(1)}, u32[]{:S(2)}, u32[]{:S(2)}) %collective-permute-start) | collective-permute-done | bytes 196640 | tf_op jit(solution)/shard_map/ppermute | solution.py:383
  4.1 0.8 shard_map.113
  4.9 11.0 %all-to-all-start = ((bf16[16,96,128]{2,1,0:T(8,128)(2,1)}), bf16[16,96,128]{2,1,0:T(8,128)(2,1)S(1)}, u32[]{:S(2)}, u32[]{:S(2)}) async-start(bf16[16,96,128]{2,1,0:T(8,128)(2,1)} %shard_map.113), calls=%async_computation | async-start | bytes 786432 | tf_op jit(solution)/shard_map/all_to_all | solution.py:401
  15.9 2.4 %prepare.1 = (bf16[2,48,128]{2,1,0:T(8,128)(2,1)}, bf16[2,48,128]{2,1,0:T(8,128)(2,1)}, bf16[2,48,128]{2,1,0:T(8,128)(2,1)}, bf16[2,48,128]{2,1,0:T(8,128)(2,1)}) custom-call(s32[1]{0:T(128)} %bitcast.12.row_ref, s32[1]{0:T(128)} %bitcast.13.col_ref, f32[1024]{0:T(1024)} %refs_0_.2, f32[512]{0:T(512)} %refs_1_.2, bf16[32,4096]{1,0:T(8,128)(2,1)} %refs_2_.2, ...), custom_call_target="tpu_custom_call" | custom-call | tf_op jit(solution)/shard_map/prepare/pallas_call | solution.py:137
  18.4 1.9 %collective-permute-start.4 = (bf16[2,48,128]{2,1,0:T(8,128)(2,1)}, bf16[2,48,128]{2,1,0:T(8,128)(2,1)S(1)}, u32[]{:S(2)}, u32[]{:S(2)}) collective-permute-start(bf16[2,48,128]{2,1,0:T(8,128)(2,1)} %get-tuple-element.17), channel_id=1, source_target_pairs={{0,1},{8,9},{16,17},{24,25},{32,33},{40,41},{48,49},{56,57},{64,65... | collective-permute-start | bytes 73736 | tf_op jit(solution)/shard_map/ppermute | solution.py:405
  20.3 2.3 %collective-permute-start.5 = (bf16[2,48,128]{2,1,0:T(8,128)(2,1)}, bf16[2,48,128]{2,1,0:T(8,128)(2,1)S(1)}, u32[]{:S(2)}, u32[]{:S(2)}) collective-permute-start(bf16[2,48,128]{2,1,0:T(8,128)(2,1)} %get-tuple-element.18), channel_id=1, source_target_pairs={{0,2},{8,10},{16,18},{24,26},{32,34},{40,42},{48,50},{56,58},{64,6... | collective-permute-start | bytes 73736 | tf_op jit(solution)/shard_map/ppermute | solution.py:405
  22.5 1.3 %collective-permute-start.6 = (bf16[2,48,128]{2,1,0:T(8,128)(2,1)}, bf16[2,48,128]{2,1,0:T(8,128)(2,1)S(1)}, u32[]{:S(2)}, u32[]{:S(2)}) collective-permute-start(bf16[2,48,128]{2,1,0:T(8,128)(2,1)} %get-tuple-element.19), channel_id=1, source_target_pairs={{0,3},{8,11},{16,19},{24,27},{32,35},{40,43},{48,51},{56,59},{64,6... | collective-permute-start | bytes 73736 | tf_op jit(solution)/shard_map/ppermute | solution.py:405
  23.8 0.0 collective-permute-done.4.refs_1_
  23.9 0.4 collective-permute-done.5.refs_2_
  24.3 1.3 %collective-permute-done.6.refs_3_ = bf16[2,48,128]{2,1,0:T(8,128)(2,1)S(1)} collective-permute-done((bf16[2,48,128]{2,1,0:T(8,128)(2,1)}, bf16[2,48,128]{2,1,0:T(8,128)(2,1)S(1)}, u32[]{:S(2)}, u32[]{:S(2)}) %collective-permute-start.6) | collective-permute-done | bytes 24608 | tf_op jit(solution)/shard_map/ppermute | solution.py:405
  25.6 0.0 copy-start.8
  25.6 0.7 copy-done.8
  26.3 1.3 %collective-permute-start.7 = (bf16[2,48,128]{2,1,0:T(8,128)(2,1)S(1)}, bf16[2,48,128]{2,1,0:T(8,128)(2,1)S(1)}, u32[]{:S(2)}, u32[]{:S(2)}) collective-permute-start(bf16[2,48,128]{2,1,0:T(8,128)(2,1)S(1)} %shard_map.114.refs_0_), channel_id=1, source_target_pairs={{0,4},{1,5},{2,6},{3,7},{8,12},{9,13},{10,14},{11,15},{16,20},{17,... | collective-permute-start | bytes 73736 | tf_op jit(solution)/shard_map/ppermute | solution.py:407
  27.6 1.5 %collective-permute-done.7.refs_1_ = bf16[2,48,128]{2,1,0:T(8,128)(2,1)S(1)} collective-permute-done((bf16[2,48,128]{2,1,0:T(8,128)(2,1)S(1)}, bf16[2,48,128]{2,1,0:T(8,128)(2,1)S(1)}, u32[]{:S(2)}, u32[]{:S(2)}) %collective-permute-start.7) | collective-permute-done | bytes 24608 | tf_op jit(solution)/shard_map/ppermute | solution.py:407
  29.1 0.0 collective-permute-start.8
  29.1 1.2 %collective-permute-done.8.other_ref = bf16[48,128]{1,0:T(8,128)(2,1)S(1)} collective-permute-done((bf16[48,128]{1,0:T(8,128)(2,1)S(1)}, bf16[48,128]{1,0:T(8,128)(2,1)S(1)}, u32[]{:S(2)}, u32[]{:S(2)}) %collective-permute-start.8) | collective-permute-done | bytes 12320 | tf_op jit(solution)/shard_map/ppermute | solution.py:383
  30.3 0.7 shard_map.116
  31.0 0.0 all-to-all-done
  31.0 9.6 %all-to-all-start.1 = ((bf16[16,48,128]{2,1,0:T(8,128)(2,1)}), bf16[16,48,128]{2,1,0:T(8,128)(2,1)S(1)}, u32[]{:S(2)}, u32[]{:S(2)}) async-start(bf16[16,48,128]{2,1,0:T(8,128)(2,1)} %shard_map.116), calls=%async_computation.1 | async-start | bytes 393216 | tf_op jit(solution)/shard_map/all_to_all | solution.py:412
  40.8 0.2 collective-permute-start.2
  41.0 10.3 %all-to-all-done.1 = bf16[16,48,128]{2,1,0:T(8,128)(2,1)S(1)} async-done(((bf16[16,48,128]{2,1,0:T(8,128)(2,1)}), bf16[16,48,128]{2,1,0:T(8,128)(2,1)S(1)}, u32[]{:S(2)}, u32[]{:S(2)}) %all-to-all-start.1) | async-done | bytes 196640 | tf_op jit(solution)/shard_map/all_to_all | solution.py:412
  51.4 0.1 collective-permute-start.1
  51.5 2.7 %collective-permute-done.2.refs_2_ = bf16[1536,128]{1,0:T(8,128)(2,1)S(1)} collective-permute-done((bf16[1536,128]{1,0:T(8,128)(2,1)S(1)}, bf16[1536,128]{1,0:T(8,128)(2,1)S(1)}, u32[]{:S(2)}, u32[]{:S(2)}) %collective-permute-start.2) | collective-permute-done | bytes 393248 | tf_op jit(solution)/shard_map/ppermute | solution.py:383
  54.2 0.0 collective-permute-start.3
  54.2 0.0 copy-start.4
  54.3 0.0 copy-start.5
  54.3 3.6 %collective-permute-start.11 = (bf16[768,128]{1,0:T(8,128)(2,1)S(1)}, bf16[768,128]{1,0:T(8,128)(2,1)S(1)}, u32[]{:S(2)}, u32[]{:S(2)}) collective-permute-start(bf16[768,128]{1,0:T(8,128)(2,1)S(1)} %pad_maximum_fusion.2.refs_4_), channel_id=1, source_target_pairs={{0,3},{1,0},{2,1},{3,2},{4,7},{5,4},{6,5},{7,6},{8,11},{9,8},{10,9... | collective-permute-start | bytes 589832 | tf_op jit(solution)/shard_map/ppermute | solution.py:379
  57.9 0.0 collective-permute-start.10
  57.9 1.0 collective-permute-start.9
  58.8 0.0 collective-permute-done.1.in_ref
  58.8 8.1 %collective-permute-done.11.refs_7_ = bf16[768,128]{1,0:T(8,128)(2,1)S(1)} collective-permute-done((bf16[768,128]{1,0:T(8,128)(2,1)S(1)}, bf16[768,128]{1,0:T(8,128)(2,1)S(1)}, u32[]{:S(2)}, u32[]{:S(2)}) %collective-permute-start.11) | collective-permute-done | bytes 196640 | tf_op jit(solution)/shard_map/ppermute | solution.py:379
  66.9 0.3 collective-permute-done.10.refs_6_
  67.2 3.1 %collective-permute-done.9.refs_5_ = bf16[768,128]{1,0:T(8,128)(2,1)S(1)} collective-permute-done((bf16[768,128]{1,0:T(8,128)(2,1)S(1)}, bf16[768,128]{1,0:T(8,128)(2,1)S(1)}, u32[]{:S(2)}, u32[]{:S(2)}) %collective-permute-start.9) | collective-permute-done | bytes 196640 | tf_op jit(solution)/shard_map/ppermute | solution.py:379
  70.3 0.0 collective-permute-done.3.refs_3_
  70.3 0.0 copy-done.4
  70.3 0.0 copy-done.5
  70.3 0.0 copy-start.6
  70.3 0.0 copy-start.7
  70.4 2.6 %polar.1 = bf16[64,2,16,128]{3,2,1,0:T(8,128)(2,1)} custom-call(s32[1]{0:T(128)} %bitcast.core_ref, s32[1]{0:T(128)} %bitcast.1.z0_ref, s32[1]{0:T(128)} %bitcast.2.y_ref, bf16[1536,128]{1,0:T(8,128)(2,1)S(1)} %pad_maximum_fusion.refs_0_, bf16[1536,128]{1,0:T(8,128)(2,1)S(1)} %fence.1.refs_1_, bf16[1536,128]{1,0:T(8,128)(2,1)S(1)} %collective-permute-done.2.refs_2_, ...), custom_call_target="tpu_custom_call" | custom-call | tf_op jit(solution)/shard_map/polar/pallas_call | solution.py:261
  73.0 0.0 copy-start.2
  73.0 0.0 copy-start.3
  73.0 11.7 %all-to-all-start.2 = ((bf16[64,2,16,128]{3,2,1,0:T(8,128)(2,1)}), bf16[64,2,16,128]{3,2,1,0:T(8,128)(2,1)S(1)}, u32[]{:S(2)}, u32[]{:S(2)}) async-start(bf16[64,2,16,128]{3,2,1,0:T(8,128)(2,1)} %polar.1), calls=%async_computation.2 | async-start | bytes 1048576 | tf_op jit(solution)/shard_map/all_to_all | solution.py:427
  84.6 0.0 copy-done.6
  84.6 0.0 copy-done.7
  84.6 0.0 copy-done.2
  84.7 0.0 copy-done.3
  84.7 0.1 carry.1
  84.8 20.5 %all-to-all-done.2.x_ref = bf16[64,2,16,128]{3,2,1,0:T(8,128)(2,1)S(1)} async-done(((bf16[64,2,16,128]{3,2,1,0:T(8,128)(2,1)}), bf16[64,2,16,128]{3,2,1,0:T(8,128)(2,1)S(1)}, u32[]{:S(2)}, u32[]{:S(2)}) %all-to-all-start.2) | async-done | bytes 524320 | tf_op jit(solution)/shard_map/all_to_all | solution.py:427
  105.2 2.8 %finish.1 = (f32[32,4,1024]{2,1,0:T(4,128)}, f32[32,4,1024]{2,1,0:T(4,128)}) custom-call(bf16[64,2,16,128]{3,2,1,0:T(8,128)(2,1)S(1)} %all-to-all-done.2.x_ref, bf16[512,512]{1,0:T(8,128)(2,1)S(1)} %get-tuple-element.22.a_high_ref, bf16[512,512]{1,0:T(8,128)(2,1)S(1)} %get-tuple-element.23.a_low_ref, bf16[256,256]{1,0:T(8,128)(2,1)S(1)} %get-tuple-element.24.b_high_ref, ...), custom_call_target="tpu_custom_call" | custom-call | tf_op jit(solution)/shard_map/finish/pallas_call | solution.py:332
  (14 shorter events, 0.2 us)
Async XLA Ops:
  0.6 1.0 copy-start
  1.6 0.9 copy-start.1
  2.6 1.5 %collective-permute-start = (bf16[16,48,128]{2,1,0:T(8,128)(2,1)S(1)}, bf16[16,48,128]{2,1,0:T(8,128)(2,1)S(1)}, u32[]{:S(2)}, u32[]{:S(2)}) collective-permute-start(bf16[16,48,128]{2,1,0:T(8,128)(2,1)S(1)} %get-tuple-element.15), channel_id=1, source_target_pairs={{0,8},{8,0},{1,9},{9,1},{2,10},{10,2},{3,11},{11,3},{4,12},{12,4},... | collective-permute-start | bytes 589832 | tf_op jit(solution)/shard_map/ppermute | solution.py:383
  4.9 26.1 %all-to-all-start = ((bf16[16,96,128]{2,1,0:T(8,128)(2,1)}), bf16[16,96,128]{2,1,0:T(8,128)(2,1)S(1)}, u32[]{:S(2)}, u32[]{:S(2)}) async-start(bf16[16,96,128]{2,1,0:T(8,128)(2,1)} %shard_map.113), calls=%async_computation | async-start | bytes 786432 | tf_op jit(solution)/shard_map/all_to_all | solution.py:401
  18.4 5.4 %collective-permute-start.4 = (bf16[2,48,128]{2,1,0:T(8,128)(2,1)}, bf16[2,48,128]{2,1,0:T(8,128)(2,1)S(1)}, u32[]{:S(2)}, u32[]{:S(2)}) collective-permute-start(bf16[2,48,128]{2,1,0:T(8,128)(2,1)} %get-tuple-element.17), channel_id=1, source_target_pairs={{0,1},{8,9},{16,17},{24,25},{32,33},{40,41},{48,49},{56,57},{64,65... | collective-permute-start | bytes 73736 | tf_op jit(solution)/shard_map/ppermute | solution.py:405
  20.3 4.0 %collective-permute-start.5 = (bf16[2,48,128]{2,1,0:T(8,128)(2,1)}, bf16[2,48,128]{2,1,0:T(8,128)(2,1)S(1)}, u32[]{:S(2)}, u32[]{:S(2)}) collective-permute-start(bf16[2,48,128]{2,1,0:T(8,128)(2,1)} %get-tuple-element.18), channel_id=1, source_target_pairs={{0,2},{8,10},{16,18},{24,26},{32,34},{40,42},{48,50},{56,58},{64,6... | collective-permute-start | bytes 73736 | tf_op jit(solution)/shard_map/ppermute | solution.py:405
  22.5 3.0 %collective-permute-start.6 = (bf16[2,48,128]{2,1,0:T(8,128)(2,1)}, bf16[2,48,128]{2,1,0:T(8,128)(2,1)S(1)}, u32[]{:S(2)}, u32[]{:S(2)}) collective-permute-start(bf16[2,48,128]{2,1,0:T(8,128)(2,1)} %get-tuple-element.19), channel_id=1, source_target_pairs={{0,3},{8,11},{16,19},{24,27},{32,35},{40,43},{48,51},{56,59},{64,6... | collective-permute-start | bytes 73736 | tf_op jit(solution)/shard_map/ppermute | solution.py:405
  25.6 0.7 copy-start.8
  26.3 2.8 %collective-permute-start.7 = (bf16[2,48,128]{2,1,0:T(8,128)(2,1)S(1)}, bf16[2,48,128]{2,1,0:T(8,128)(2,1)S(1)}, u32[]{:S(2)}, u32[]{:S(2)}) collective-permute-start(bf16[2,48,128]{2,1,0:T(8,128)(2,1)S(1)} %shard_map.114.refs_0_), channel_id=1, source_target_pairs={{0,4},{1,5},{2,6},{3,7},{8,12},{9,13},{10,14},{11,15},{16,20},{17,... | collective-permute-start | bytes 73736 | tf_op jit(solution)/shard_map/ppermute | solution.py:407
  29.1 1.2 %collective-permute-start.8 = (bf16[48,128]{1,0:T(8,128)(2,1)S(1)}, bf16[48,128]{1,0:T(8,128)(2,1)S(1)}, u32[]{:S(2)}, u32[]{:S(2)}) collective-permute-start(bf16[48,128]{1,0:T(8,128)(2,1)S(1)} %get-tuple-element.21), channel_id=1, source_target_pairs={{0,8},{8,0},{1,9},{9,1},{2,10},{10,2},{3,11},{11,3},{4,12},{12,4},... | collective-permute-start | bytes 36872 | tf_op jit(solution)/shard_map/ppermute | solution.py:383
  31.0 20.4 %all-to-all-start.1 = ((bf16[16,48,128]{2,1,0:T(8,128)(2,1)}), bf16[16,48,128]{2,1,0:T(8,128)(2,1)S(1)}, u32[]{:S(2)}, u32[]{:S(2)}) async-start(bf16[16,48,128]{2,1,0:T(8,128)(2,1)} %shard_map.116), calls=%async_computation.1 | async-start | bytes 393216 | tf_op jit(solution)/shard_map/all_to_all | solution.py:412
  40.8 13.4 %collective-permute-start.2 = (bf16[1536,128]{1,0:T(8,128)(2,1)S(1)}, bf16[1536,128]{1,0:T(8,128)(2,1)S(1)}, u32[]{:S(2)}, u32[]{:S(2)}) collective-permute-start(bf16[1536,128]{1,0:T(8,128)(2,1)S(1)} %pad_maximum_fusion.refs_0_), channel_id=1, source_target_pairs={{0,16},{16,0},{1,17},{17,1},{2,18},{18,2},{3,19},{19,3},{4,20},{20... | collective-permute-start | bytes 1179656 | tf_op jit(solution)/shard_map/ppermute | solution.py:383
  51.4 7.4 %collective-permute-start.1 = (bf16[1536,128]{1,0:T(8,128)(2,1)S(1)}, bf16[1536,128]{1,0:T(8,128)(2,1)S(1)}, u32[]{:S(2)}, u32[]{:S(2)}) collective-permute-start(bf16[1536,128]{1,0:T(8,128)(2,1)S(1)} %pad_maximum_fusion.refs_0_), channel_id=1, source_target_pairs={{0,8},{8,0},{1,9},{9,1},{2,10},{10,2},{3,11},{11,3},{4,12},{12,4},... | collective-permute-start | bytes 1179656 | tf_op jit(solution)/shard_map/ppermute | solution.py:383
  54.2 16.1 %collective-permute-start.3 = (bf16[1536,128]{1,0:T(8,128)(2,1)S(1)}, bf16[1536,128]{1,0:T(8,128)(2,1)S(1)}, u32[]{:S(2)}, u32[]{:S(2)}) collective-permute-start(bf16[1536,128]{1,0:T(8,128)(2,1)S(1)} %collective-permute-done.2.refs_2_), channel_id=1, source_target_pairs={{0,8},{8,0},{1,9},{9,1},{2,10},{10,2},{3,11},{11,3},{4,12},{12,4},... | collective-permute-start | bytes 1179656 | tf_op jit(solution)/shard_map/ppermute | solution.py:383
  54.2 16.1 %copy-start.4 = (bf16[512,256]{1,0:T(8,128)(2,1)S(1)}, bf16[512,256]{1,0:T(8,128)(2,1)}, u32[]{:S(2)}) copy-start(bf16[512,256]{1,0:T(8,128)(2,1)} %constant.51.clone.refs_9_) | copy-start | bytes 786436
  54.3 16.1 %copy-start.5 = (bf16[512,256]{1,0:T(8,128)(2,1)S(1)}, bf16[512,256]{1,0:T(8,128)(2,1)}, u32[]{:S(2)}) copy-start(bf16[512,256]{1,0:T(8,128)(2,1)} %constant.50.clone.refs_8_) | copy-start | bytes 786436
  54.3 12.6 %collective-permute-start.11 = (bf16[768,128]{1,0:T(8,128)(2,1)S(1)}, bf16[768,128]{1,0:T(8,128)(2,1)S(1)}, u32[]{:S(2)}, u32[]{:S(2)}) collective-permute-start(bf16[768,128]{1,0:T(8,128)(2,1)S(1)} %pad_maximum_fusion.2.refs_4_), channel_id=1, source_target_pairs={{0,3},{1,0},{2,1},{3,2},{4,7},{5,4},{6,5},{7,6},{8,11},{9,8},{10,9... | collective-permute-start | bytes 589832 | tf_op jit(solution)/shard_map/ppermute | solution.py:379
  57.9 9.3 %collective-permute-start.10 = (bf16[768,128]{1,0:T(8,128)(2,1)S(1)}, bf16[768,128]{1,0:T(8,128)(2,1)S(1)}, u32[]{:S(2)}, u32[]{:S(2)}) collective-permute-start(bf16[768,128]{1,0:T(8,128)(2,1)S(1)} %pad_maximum_fusion.2.refs_4_), channel_id=1, source_target_pairs={{0,2},{1,3},{2,0},{3,1},{4,6},{5,7},{6,4},{7,5},{8,10},{9,11},{10,... | collective-permute-start | bytes 589832 | tf_op jit(solution)/shard_map/ppermute | solution.py:379
  57.9 12.4 %collective-permute-start.9 = (bf16[768,128]{1,0:T(8,128)(2,1)S(1)}, bf16[768,128]{1,0:T(8,128)(2,1)S(1)}, u32[]{:S(2)}, u32[]{:S(2)}) collective-permute-start(bf16[768,128]{1,0:T(8,128)(2,1)S(1)} %pad_maximum_fusion.2.refs_4_), channel_id=1, source_target_pairs={{0,1},{1,2},{2,3},{3,0},{4,5},{5,6},{6,7},{7,4},{8,9},{9,10},{10,1... | collective-permute-start | bytes 589832 | tf_op jit(solution)/shard_map/ppermute | solution.py:379
  70.3 14.3 %copy-start.6 = (bf16[256,256]{1,0:T(8,128)(2,1)S(1)}, bf16[256,256]{1,0:T(8,128)(2,1)}, u32[]{:S(2)}) copy-start(bf16[256,256]{1,0:T(8,128)(2,1)} %constant.55.clone.refs_3_) | copy-start | bytes 393220
  70.3 14.3 %copy-start.7 = (bf16[256,256]{1,0:T(8,128)(2,1)S(1)}, bf16[256,256]{1,0:T(8,128)(2,1)}, u32[]{:S(2)}) copy-start(bf16[256,256]{1,0:T(8,128)(2,1)} %constant.54.clone.refs_2_) | copy-start | bytes 393220
  73.0 11.7 %copy-start.2 = (bf16[512,512]{1,0:T(8,128)(2,1)S(1)}, bf16[512,512]{1,0:T(8,128)(2,1)}, u32[]{:S(2)}) copy-start(bf16[512,512]{1,0:T(8,128)(2,1)} %constant.53.clone.refs_1_) | copy-start | bytes 1572868
  73.0 11.7 %copy-start.3 = (bf16[512,512]{1,0:T(8,128)(2,1)S(1)}, bf16[512,512]{1,0:T(8,128)(2,1)}, u32[]{:S(2)}) copy-start(bf16[512,512]{1,0:T(8,128)(2,1)} %constant.52.clone.refs_0_) | copy-start | bytes 1572868
  73.0 32.2 %all-to-all-start.2 = ((bf16[64,2,16,128]{3,2,1,0:T(8,128)(2,1)}), bf16[64,2,16,128]{3,2,1,0:T(8,128)(2,1)S(1)}, u32[]{:S(2)}, u32[]{:S(2)}) async-start(bf16[64,2,16,128]{3,2,1,0:T(8,128)(2,1)} %polar.1), calls=%async_computation.2 | async-start | bytes 1048576 | tf_op jit(solution)/shard_map/all_to_all | solution.py:427

commit v5 on v2

--- a/solution.py
+++ b/solution.py
@@ -123,7 +123,7 @@
                     axis=0,
                 ).astype(BF16)
                 for xl in range(2):
-                    out_ref[4 * xl + 2 * y1 + t, kind] = piece
+                    out_ref[8 * (kind % 2) + 4 * xl + 2 * y1 + t, kind // 2] = piece
     result = pltpu.make_async_copy(out_ref, out_hbm, sems.at[2])
     result.start()
     result.wait()
@@ -134,41 +134,66 @@
     hbm = pl.BlockSpec(memory_space=pl.ANY)
     return pl.pallas_call(
         prepare_kernel,
-        out_shape=jax.ShapeDtypeStruct((8, 4, 24, 128), BF16),
+        out_shape=jax.ShapeDtypeStruct((16, 2, 24, 128), BF16),
         in_specs=[smem] * 4 + [hbm] * 2,
         out_specs=hbm,
         scratch_shapes=[
             pltpu.VMEM((32, 1024), BF16),
             pltpu.VMEM((16, 1024), BF16),
-            pltpu.VMEM((8, 4, 24, 128), BF16),
+            pltpu.VMEM((16, 2, 24, 128), BF16),
             pltpu.SemaphoreType.DMA((3,)),
         ],
         name="prepare",
     )(row, col, occ_decay, vir_decay, occ, vir)
 
 
-def pack_kernel(occ_ref, vir_ref, rows_ref, out_ref):
-    for p in range(32):
-        out_ref[p, 0:32, :] = occ_ref[:, 128 * p : 128 * (p + 1)]
-        out_ref[p, 32:48, :] = vir_ref[:, 128 * p : 128 * (p + 1)]
-        out_ref[p, 48:72, :] = rows_ref[0, p % 4]
-
-
-def pack(occ, vir, rows):
+def divide_kernel(core_ref, occ_ref, vir_ref, kept_ref, sent_ref):
+    core = core_ref[0]
+    for out_ref, which in ((kept_ref, core), (sent_ref, 1 - core)):
+        for p in range(16):
+            lanes = pl.ds(pl.multiple_of(128 * (2 * p + which), 128), 128)
+            out_ref[p, :32, :] = occ_ref[:, lanes]
+            out_ref[p, 32:, :] = vir_ref[:, lanes]
+
+
+def divide(core, occ, vir):
     vmem = pl.BlockSpec(memory_space=pltpu.VMEM)
+    shape = jax.ShapeDtypeStruct((16, 48, 128), BF16)
+    return pl.pallas_call(
+        divide_kernel,
+        out_shape=(shape, shape),
+        in_specs=[pl.BlockSpec(memory_space=pltpu.SMEM), vmem, vmem],
+        out_specs=(vmem, vmem),
+        compiler_params=pltpu.CompilerParams(vmem_limit_bytes=LIMIT),
+        name="divide",
+    )(core, occ, vir)
+
+
+def pack_kernel(core_ref, kept_ref, other_ref, rows_ref, out_ref):
+    core = core_ref[0]
+    out_ref[:, pl.ds(pl.multiple_of(48 * core, 16), 48), :] = kept_ref[...]
+    out_ref[:, pl.ds(pl.multiple_of(48 * (1 - core), 16), 48), :] = other_ref[...]
+    for p in range(16):
+        out_ref[p, 96:120, :] = rows_ref[0, p % 2]
+        out_ref[p, 120:144, :] = rows_ref[8, p % 2]
+
+
+def pack(core, kept, other, rows):
+    vmem = pl.BlockSpec(memory_space=pltpu.VMEM)
     return pl.pallas_call(
         pack_kernel,
-        out_shape=jax.ShapeDtypeStruct((32, 72, 128), BF16),
-        in_specs=[vmem] * 3,
+        out_shape=jax.ShapeDtypeStruct((16, 144, 128), BF16),
+        in_specs=[pl.BlockSpec(memory_space=pltpu.SMEM)] + [vmem] * 3,
         out_specs=vmem,
         compiler_params=pltpu.CompilerParams(vmem_limit_bytes=LIMIT),
         name="pack",
-    )(occ, vir, rows)
+    )(core, kept, other, rows)
 
 
 def polar_kernel(core_ref, z0_ref, y_ref, *refs):
     points, near, (high_ref, low_ref) = refs[:4], refs[4:8], refs[8:10]
-    out_ref, polar_ref, occ_ref, vir_ref = refs[-4:]
+    out_hbm, polar_ref, occ_ref, vir_ref, out_ref, sems = refs[10:]
+    copies = []
     core, z0, y = core_ref[0], z0_ref[0], y_ref[0]
     for step in range(4):
         chunk = lax.rem(y + 4 - step, 4)
@@ -202,7 +227,12 @@
             pieces = [spectrum[128 * i : 128 * (i + 1), 32 * m : 32 * (m + 1)] for i in range(4)]
             message = jnp.concatenate(pieces, axis=1).astype(BF16)
             for j in range(8):
-                out_ref[place_in_last(m, j), half] = message[16 * j : 16 * (j + 1)]
+                out_ref[half, place_in_last(m, j)] = message[16 * j : 16 * (j + 1)]
+        copy = pltpu.make_async_copy(out_ref.at[half], out_hbm.at[:, half], sems.at[half])
+        copy.start()
+        copies.append(copy)
+    for copy in copies:
+        copy.wait()
 
 
 def polar_messages(*arrays):
@@ -211,11 +241,13 @@
         polar_kernel,
         out_shape=jax.ShapeDtypeStruct((64, 2, 16, 128), BF16),
         in_specs=[pl.BlockSpec(memory_space=pltpu.SMEM)] * 3 + [vmem] * 10,
-        out_specs=vmem,
+        out_specs=pl.BlockSpec(memory_space=pl.ANY),
         scratch_shapes=[
             pltpu.VMEM((512, 256), F32),
             pltpu.VMEM((1024, 256), BF16),
             pltpu.VMEM((512, 256), BF16),
+            pltpu.VMEM((2, 64, 16, 128), BF16),
+            pltpu.SemaphoreType.DMA((2,)),
         ],
         compiler_params=pltpu.CompilerParams(vmem_limit_bytes=LIMIT),
         name="polar",
@@ -336,18 +368,23 @@
     row = lax.axis_index(ROW).astype(jnp.int32).reshape(1)
     col = lax.axis_index(COL).astype(jnp.int32).reshape(1)
     place = [lax.axis_index(a).astype(jnp.int32).reshape(1) for a in ("c", "z0", Y)]
-    scattered = lax.all_to_all(prepare(row, col, occ_decay, vir_decay, occ, vir), COL, 0, 0, tiled=True)
-    arrived = lax.all_to_all(pack(occ, vir, scattered), ROW, 0, 0, tiled=True)
-
-    def by_group(part, count):
-        part = part.reshape(32, count, 8, 128)
-        return jnp.transpose(part, (1, 0, 2, 3)).reshape(256 * count, 128)
-
-    near = jnp.concatenate([by_group(arrived[:, 48:64], 2), by_group(arrived[:, 64:], 1)], axis=0)
+    scattered = prepare(row, col, occ_decay, vir_decay, occ, vir)
+    scattered = lax.all_to_all(scattered, ("c", *COL), 0, 0, tiled=True)
+    kept, sent = divide(place[0], occ, vir)
+    other = swap(sent, "c")
+    arrived = lax.all_to_all(pack(place[0], kept, other, scattered), ("xh", *Z), 0, 0, tiled=True)
+
+    def by_group(first, count):
+        parts = [arrived[:, start : start + 8 * count] for start in first]
+        parts = jnp.stack([part.reshape(16, count, 8, 128) for part in parts])
+        return jnp.transpose(parts, (2, 0, 1, 3, 4)).reshape(256 * count, 128)
+
+    parts = [by_group((96 + 8 * k, 120 + 8 * k), 1) for k in range(3)]
+    near = jnp.concatenate(parts, axis=0)
     near = [near]
     for by in (1, 2, 3):
         near.append(shift(near[0], Y, 4, by))
-    own = jnp.concatenate([by_group(arrived[:, :32], 4), by_group(arrived[:, 32:48], 2)], axis=0)
+    own = jnp.concatenate([by_group((0, 48), 4), by_group((32, 80), 2)], axis=0)
     across = swap(own, "z0")
     beside = swap(own, "c")
     beside = fence(beside)

time: 102 us -> 103 us (level)
  local copies, waits for them, and re-layouts: 0.16 us -> 2.02 us
  waiting for transfers between devices: 41.1 us -> 39.7 us
  starting transfers between devices: 9.26 us -> 10.3 us
    unnamed x16, local copies, waits for them, and re-layouts: 0.05 us -> 1.89 us
    ppermute x3 -> x4, waiting for transfers between devices: 9.18 us -> 8.78 us  [swap(): return lax.ppermute(x, axis, [(0, 1), (1, 0)])]
    pallas_call x2 -> x3, Pallas kernels: 2.56 us -> 2.63 us  [the longest x1 2.47 us: prepare(): pl.pallas_call(prepare_kernel, out_shape=jax.ShapeDtypeStruct((16, 2, 24,...]
  transfers between devices with their start and end apart: 7 -> 8, of which waited for: 5 -> 5; matrix products, arithmetic and copies ran while one was open for 0% -> 0% of each run, Pallas kernels for 0% -> 2%
where the time goes in v5:
time: 103 us
  blocking collectives  41.7 us (40%)
  waiting for transfers between devices  39.7 us (39%)
  starting transfers between devices  10.3 us (10%)
  Pallas kernels  8.09 us (8%)
  local copies, waits for them, and re-layouts  2.02 us (2%)
    all_to_all x1, blocking collectives, body(): lax.all_to_all(pack(place[0], kept, other, scattered), ('xh', *Z), 0, 0,...  30.7 us
    all_to_all x1, waiting for transfers between devices, body(): received = lax.all_to_all(messages, LAST, 0, 0, tiled=True)  20.4 us
    all_to_all x1, blocking collectives, body(): scattered = lax.all_to_all(scattered, ('c', *COL), 0, 0, tiled=True)  11 us
    ppermute x3, waiting for transfers between devices, shift(): return lax.ppermute(x, axes, [(i, (i + by) % count) for i in range(count)])  10.5 us
    ppermute x4, waiting for transfers between devices, swap(): return lax.ppermute(x, axis, [(0, 1), (1, 0)])  8.78 us
    all_to_all x1, starting transfers between devices, body(): received = lax.all_to_all(messages, LAST, 0, 0, tiled=True)  6.35 us
    pallas_call x1, Pallas kernels, finish(): pl.pallas_call(finish_kernel, out_shape=(shape, shape), in_specs=[vmem] *...  2.76 us
    ppermute x3, starting transfers between devices, shift(): return lax.ppermute(x, axes, [(i, (i + by) % count) for i in range(count)])  2.7 us
  transfers between devices with their start and end apart: 8, of which 5 were waited for; matrix products, arithmetic and copies ran while one was open for 0% of the time, Pallas kernels for 2%

profile of v5, /device:TPU:32, one launch (start us, length us, event | category | flops | bytes accessed | tf_op | source)
XLA Modules:
  0.0 102.7 jit_solution(7378212303782915194)
XLA Ops:
  0.6 0.0 copy-start
  0.6 0.9 copy-done
  1.6 0.0 copy-start.3
  1.6 0.9 copy-done.3
  2.5 0.1 divide.1
  2.6 0.1 collective-permute-start
  2.7 2.5 %prepare.1 = bf16[16,2,24,128]{3,2,1,0:T(8,128)(2,1)} custom-call(s32[1]{0:T(128)} %bitcast.3.row_ref, s32[1]{0:T(128)} %bitcast.4.col_ref, f32[1024]{0:T(1024)} %refs_0_.2, f32[512]{0:T(512)} %refs_1_.2, bf16[32,4096]{1,0:T(8,128)(2,1)} %refs_2_.2, bf16[16,4096]{1,0:T(8,128)(2,1)} %refs_3_.2), custom_call_target="tpu_custom_call" | custom-call | tf_op jit(solution)/shard_map/prepare/pallas_call | solution.py:135
  5.2 11.0 %all_to_all.15.rows_ref = bf16[16,2,24,128]{3,2,1,0:T(8,128)(2,1)S(1)} all-to-all(bf16[16,2,24,128]{3,2,1,0:T(8,128)(2,1)} %prepare.1), channel_id=1, replica_groups=mesh['xh'=2,'z2'=2,'z1'=2,'z0'=2,'c'=2,'xl'=2,'y1'=2,'y0'=2] {'c','xl','..., dimensions={0} | all-to-all | bytes 393216 | tf_op jit(solution)/shard_map/all_to_all | solution.py:372
  16.2 0.0 collective-permute-done.other_ref
  16.2 0.1 pack.1
  16.3 30.7 %all_to_all.16 = bf16[16,144,128]{2,1,0:T(8,128)(2,1)S(1)} all-to-all(bf16[16,144,128]{2,1,0:T(8,128)(2,1)S(1)} %pack.1), channel_id=1, replica_groups=mesh['xh'=2,'z2'=2,'z1'=2,'z0'=2,'c'=2,'xl'=2,'y1'=2,'y0'=2] {'xh','z2',..., dimensions={0} | all-to-all | bytes 1179648 | tf_op jit(solution)/shard_map/all_to_all | solution.py:375
  47.2 1.1 %collective-permute-start.2 = (bf16[1536,128]{1,0:T(8,128)(2,1)S(1)}, bf16[1536,128]{1,0:T(8,128)(2,1)S(1)}, u32[]{:S(2)}, u32[]{:S(2)}) collective-permute-start(bf16[1536,128]{1,0:T(8,128)(2,1)S(1)} %pad_maximum_fusion.refs_0_), channel_id=1, source_target_pairs={{0,16},{16,0},{1,17},{17,1},{2,18},{18,2},{3,19},{19,3},{4,20},{20... | collective-permute-start | bytes 1179656 | tf_op jit(solution)/shard_map/ppermute | solution.py:364
  48.3 0.0 collective-permute-start.1
  48.3 8.8 %collective-permute-done.2.refs_2_ = bf16[1536,128]{1,0:T(8,128)(2,1)S(1)} collective-permute-done((bf16[1536,128]{1,0:T(8,128)(2,1)S(1)}, bf16[1536,128]{1,0:T(8,128)(2,1)S(1)}, u32[]{:S(2)}, u32[]{:S(2)}) %collective-permute-start.2) | collective-permute-done | bytes 393248 | tf_op jit(solution)/shard_map/ppermute | solution.py:364
  57.1 0.0 collective-permute-start.3
  57.1 0.0 copy-start.4
  57.2 0.0 copy-start.5
  57.2 0.1 collective-permute-start.6
  57.3 2.6 %collective-permute-start.5 = (bf16[768,128]{1,0:T(8,128)(2,1)S(1)}, bf16[768,128]{1,0:T(8,128)(2,1)S(1)}, u32[]{:S(2)}, u32[]{:S(2)}) collective-permute-start(bf16[768,128]{1,0:T(8,128)(2,1)S(1)} %pad_maximum_fusion.2.refs_4_), channel_id=1, source_target_pairs={{0,2},{1,3},{2,0},{3,1},{4,6},{5,7},{6,4},{7,5},{8,10},{9,11},{10,... | collective-permute-start | bytes 589832 | tf_op jit(solution)/shard_map/ppermute | solution.py:360
  59.9 0.0 collective-permute-start.4
  59.9 0.0 collective-permute-done.1.in_ref
  59.9 5.1 %collective-permute-done.6.refs_7_ = bf16[768,128]{1,0:T(8,128)(2,1)S(1)} collective-permute-done((bf16[768,128]{1,0:T(8,128)(2,1)S(1)}, bf16[768,128]{1,0:T(8,128)(2,1)S(1)}, u32[]{:S(2)}, u32[]{:S(2)}) %collective-permute-start.6) | collective-permute-done | bytes 196640 | tf_op jit(solution)/shard_map/ppermute | solution.py:360
  65.0 1.6 %collective-permute-done.5.refs_6_ = bf16[768,128]{1,0:T(8,128)(2,1)S(1)} collective-permute-done((bf16[768,128]{1,0:T(8,128)(2,1)S(1)}, bf16[768,128]{1,0:T(8,128)(2,1)S(1)}, u32[]{:S(2)}, u32[]{:S(2)}) %collective-permute-start.5) | collective-permute-done | bytes 196640 | tf_op jit(solution)/shard_map/ppermute | solution.py:360
  66.7 3.7 %collective-permute-done.4.refs_5_ = bf16[768,128]{1,0:T(8,128)(2,1)S(1)} collective-permute-done((bf16[768,128]{1,0:T(8,128)(2,1)S(1)}, bf16[768,128]{1,0:T(8,128)(2,1)S(1)}, u32[]{:S(2)}, u32[]{:S(2)}) %collective-permute-start.4) | collective-permute-done | bytes 196640 | tf_op jit(solution)/shard_map/ppermute | solution.py:360
  70.4 0.0 collective-permute-done.3.refs_3_
  70.4 0.0 copy-done.4
  70.4 0.0 copy-done.5
  70.4 0.0 copy-start.6
  70.4 0.0 copy-start.7
  70.4 2.6 %polar.1 = bf16[64,2,16,128]{3,2,1,0:T(8,128)(2,1)} custom-call(s32[1]{0:T(128)} %bitcast.core_ref, s32[1]{0:T(128)} %bitcast.1.z0_ref, s32[1]{0:T(128)} %bitcast.2.y_ref, bf16[1536,128]{1,0:T(8,128)(2,1)S(1)} %pad_maximum_fusion.refs_0_, bf16[1536,128]{1,0:T(8,128)(2,1)S(1)} %fence.1.refs_1_, bf16[1536,128]{1,0:T(8,128)(2,1)S(1)} %collective-permute-done.2.refs_2_, ...), custom_call_target="tpu_custom_call" | custom-call | tf_op jit(solution)/shard_map/polar/pallas_call | solution.py:240
  73.0 0.0 copy-start.1
  73.0 0.0 copy-start.2
  73.1 6.3 %all-to-all-start.2 = ((bf16[64,2,16,128]{3,2,1,0:T(8,128)(2,1)}), bf16[64,2,16,128]{3,2,1,0:T(8,128)(2,1)S(1)}, u32[]{:S(2)}, u32[]{:S(2)}) async-start(bf16[64,2,16,128]{3,2,1,0:T(8,128)(2,1)} %polar.1), calls=%async_computation.2 | async-start | bytes 1048576 | tf_op jit(solution)/shard_map/all_to_all | solution.py:395
  79.4 0.0 copy-done.6
  79.4 0.0 copy-done.7
  79.4 0.0 copy-done.1
  79.4 0.0 copy-done.2
  79.4 0.1 carry.1
  79.5 20.4 %all-to-all-done.2.x_ref = bf16[64,2,16,128]{3,2,1,0:T(8,128)(2,1)S(1)} async-done(((bf16[64,2,16,128]{3,2,1,0:T(8,128)(2,1)}), bf16[64,2,16,128]{3,2,1,0:T(8,128)(2,1)S(1)}, u32[]{:S(2)}, u32[]{:S(2)}) %all-to-all-start.2) | async-done | bytes 524320 | tf_op jit(solution)/shard_map/all_to_all | solution.py:395
  99.9 2.8 %finish.1 = (f32[32,4,1024]{2,1,0:T(4,128)}, f32[32,4,1024]{2,1,0:T(4,128)}) custom-call(bf16[64,2,16,128]{3,2,1,0:T(8,128)(2,1)S(1)} %all-to-all-done.2.x_ref, bf16[512,512]{1,0:T(8,128)(2,1)S(1)} %get-tuple-element.10.a_high_ref, bf16[512,512]{1,0:T(8,128)(2,1)S(1)} %get-tuple-element.11.a_low_ref, bf16[256,256]{1,0:T(8,128)(2,1)S(1)} %get-tuple-element.12.b_high_ref, ...), custom_call_target="tpu_custom_call" | custom-call | tf_op jit(solution)/shard_map/finish/pallas_call | solution.py:313
  (12 shorter events, 0.2 us)
Async XLA Ops:
  0.6 1.0 copy-start
  1.6 0.9 copy-start.3
  2.6 13.6 %collective-permute-start = (bf16[16,48,128]{2,1,0:T(8,128)(2,1)S(1)}, bf16[16,48,128]{2,1,0:T(8,128)(2,1)S(1)}, u32[]{:S(2)}, u32[]{:S(2)}) collective-permute-start(bf16[16,48,128]{2,1,0:T(8,128)(2,1)S(1)} %get-tuple-element.9), channel_id=1, source_target_pairs={{0,8},{8,0},{1,9},{9,1},{2,10},{10,2},{3,11},{11,3},{4,12},{12,4},... | collective-permute-start | bytes 589832 | tf_op jit(solution)/shard_map/ppermute | solution.py:364
  47.2 9.9 %collective-permute-start.2 = (bf16[1536,128]{1,0:T(8,128)(2,1)S(1)}, bf16[1536,128]{1,0:T(8,128)(2,1)S(1)}, u32[]{:S(2)}, u32[]{:S(2)}) collective-permute-start(bf16[1536,128]{1,0:T(8,128)(2,1)S(1)} %pad_maximum_fusion.refs_0_), channel_id=1, source_target_pairs={{0,16},{16,0},{1,17},{17,1},{2,18},{18,2},{3,19},{19,3},{4,20},{20... | collective-permute-start | bytes 1179656 | tf_op jit(solution)/shard_map/ppermute | solution.py:364
  48.3 11.6 %collective-permute-start.1 = (bf16[1536,128]{1,0:T(8,128)(2,1)S(1)}, bf16[1536,128]{1,0:T(8,128)(2,1)S(1)}, u32[]{:S(2)}, u32[]{:S(2)}) collective-permute-start(bf16[1536,128]{1,0:T(8,128)(2,1)S(1)} %pad_maximum_fusion.refs_0_), channel_id=1, source_target_pairs={{0,8},{8,0},{1,9},{9,1},{2,10},{10,2},{3,11},{11,3},{4,12},{12,4},... | collective-permute-start | bytes 1179656 | tf_op jit(solution)/shard_map/ppermute | solution.py:364
  57.1 13.3 %collective-permute-start.3 = (bf16[1536,128]{1,0:T(8,128)(2,1)S(1)}, bf16[1536,128]{1,0:T(8,128)(2,1)S(1)}, u32[]{:S(2)}, u32[]{:S(2)}) collective-permute-start(bf16[1536,128]{1,0:T(8,128)(2,1)S(1)} %collective-permute-done.2.refs_2_), channel_id=1, source_target_pairs={{0,8},{8,0},{1,9},{9,1},{2,10},{10,2},{3,11},{11,3},{4,12},{12,4},... | collective-permute-start | bytes 1179656 | tf_op jit(solution)/shard_map/ppermute | solution.py:364
  57.1 13.2 %copy-start.4 = (bf16[512,256]{1,0:T(8,128)(2,1)S(1)}, bf16[512,256]{1,0:T(8,128)(2,1)}, u32[]{:S(2)}) copy-start(bf16[512,256]{1,0:T(8,128)(2,1)} %constant.51.clone.refs_9_) | copy-start | bytes 786436
  57.2 13.2 %copy-start.5 = (bf16[512,256]{1,0:T(8,128)(2,1)S(1)}, bf16[512,256]{1,0:T(8,128)(2,1)}, u32[]{:S(2)}) copy-start(bf16[512,256]{1,0:T(8,128)(2,1)} %constant.50.clone.refs_8_) | copy-start | bytes 786436
  57.2 7.8 %collective-permute-start.6 = (bf16[768,128]{1,0:T(8,128)(2,1)S(1)}, bf16[768,128]{1,0:T(8,128)(2,1)S(1)}, u32[]{:S(2)}, u32[]{:S(2)}) collective-permute-start(bf16[768,128]{1,0:T(8,128)(2,1)S(1)} %pad_maximum_fusion.2.refs_4_), channel_id=1, source_target_pairs={{0,3},{1,0},{2,1},{3,2},{4,7},{5,4},{6,5},{7,6},{8,11},{9,8},{10,9... | collective-permute-start | bytes 589832 | tf_op jit(solution)/shard_map/ppermute | solution.py:360
  57.3 9.4 %collective-permute-start.5 = (bf16[768,128]{1,0:T(8,128)(2,1)S(1)}, bf16[768,128]{1,0:T(8,128)(2,1)S(1)}, u32[]{:S(2)}, u32[]{:S(2)}) collective-permute-start(bf16[768,128]{1,0:T(8,128)(2,1)S(1)} %pad_maximum_fusion.2.refs_4_), channel_id=1, source_target_pairs={{0,2},{1,3},{2,0},{3,1},{4,6},{5,7},{6,4},{7,5},{8,10},{9,11},{10,... | collective-permute-start | bytes 589832 | tf_op jit(solution)/shard_map/ppermute | solution.py:360
  59.9 10.5 %collective-permute-start.4 = (bf16[768,128]{1,0:T(8,128)(2,1)S(1)}, bf16[768,128]{1,0:T(8,128)(2,1)S(1)}, u32[]{:S(2)}, u32[]{:S(2)}) collective-permute-start(bf16[768,128]{1,0:T(8,128)(2,1)S(1)} %pad_maximum_fusion.2.refs_4_), channel_id=1, source_target_pairs={{0,1},{1,2},{2,3},{3,0},{4,5},{5,6},{6,7},{7,4},{8,9},{9,10},{10,1... | collective-permute-start | bytes 589832 | tf_op jit(solution)/shard_map/ppermute | solution.py:360
  70.4 9.0 %copy-start.6 = (bf16[256,256]{1,0:T(8,128)(2,1)S(1)}, bf16[256,256]{1,0:T(8,128)(2,1)}, u32[]{:S(2)}) copy-start(bf16[256,256]{1,0:T(8,128)(2,1)} %constant.55.clone.refs_3_) | copy-start | bytes 393220
  70.4 9.0 %copy-start.7 = (bf16[256,256]{1,0:T(8,128)(2,1)S(1)}, bf16[256,256]{1,0:T(8,128)(2,1)}, u32[]{:S(2)}) copy-start(bf16[256,256]{1,0:T(8,128)(2,1)} %constant.54.clone.refs_2_) | copy-start | bytes 393220
  73.0 6.4 %copy-start.1 = (bf16[512,512]{1,0:T(8,128)(2,1)S(1)}, bf16[512,512]{1,0:T(8,128)(2,1)}, u32[]{:S(2)}) copy-start(bf16[512,512]{1,0:T(8,128)(2,1)} %constant.53.clone.refs_1_) | copy-start | bytes 1572868
  73.0 6.4 %copy-start.2 = (bf16[512,512]{1,0:T(8,128)(2,1)S(1)}, bf16[512,512]{1,0:T(8,128)(2,1)}, u32[]{:S(2)}) copy-start(bf16[512,512]{1,0:T(8,128)(2,1)} %constant.52.clone.refs_0_) | copy-start | bytes 1572868
  73.1 26.9 %all-to-all-start.2 = ((bf16[64,2,16,128]{3,2,1,0:T(8,128)(2,1)}), bf16[64,2,16,128]{3,2,1,0:T(8,128)(2,1)S(1)}, u32[]{:S(2)}, u32[]{:S(2)}) async-start(bf16[64,2,16,128]{3,2,1,0:T(8,128)(2,1)} %polar.1), calls=%async_computation.2 | async-start | bytes 1048576 | tf_op jit(solution)/shard_map/all_to_all | solution.py:395

commit v6 on v2

--- a/solution.py
+++ b/solution.py
@@ -181,8 +181,8 @@
         occ_ref[rows(y1), lanes] = near[step][:256]
         occ_ref[rows(2 + y1), lanes] = near[step][256:512]
         vir_ref[rows(y1), lanes] = near[step][512:]
-    occ = jnp.concatenate([ref[:1024].T for ref in points], axis=0)
-    vir = jnp.concatenate([ref[1024:].T for ref in points], axis=0)
+    occ = jnp.concatenate([ref[:, :1024] for ref in points], axis=0)
+    vir = jnp.concatenate([ref[:, 1024:] for ref in points], axis=0)
     product = dot(occ, occ_ref[...]) * dot(vir, vir_ref[...]) * POLAR_FACTOR
     for k in range(4):
         place = 2 * (z0 if k < 2 else 1 - z0) + (core if k % 2 == 0 else 1 - core)
@@ -197,10 +197,10 @@
             dot(high_ref[...], polar_high)
             + dot(high_ref[...], polar_low)
             + dot(low_ref[...], polar_high)
-        )
+        ).astype(BF16)
         for m in range(8):
             pieces = [spectrum[128 * i : 128 * (i + 1), 32 * m : 32 * (m + 1)] for i in range(4)]
-            message = jnp.concatenate(pieces, axis=1).astype(BF16)
+            message = jnp.concatenate(pieces, axis=1)
             for j in range(8):
                 out_ref[place_in_last(m, j), half] = message[16 * j : 16 * (j + 1)]
 
@@ -311,6 +311,22 @@
     )(*arrays)
 
 
+def turn_kernel(in_ref, out_ref):
+    out_ref[...] = in_ref[...].T
+
+
+def turn(x):
+    vmem = pl.BlockSpec(memory_space=pltpu.VMEM)
+    return pl.pallas_call(
+        turn_kernel,
+        out_shape=jax.ShapeDtypeStruct(x.shape[::-1], x.dtype),
+        in_specs=[vmem],
+        out_specs=vmem,
+        compiler_params=pltpu.CompilerParams(vmem_limit_bytes=LIMIT),
+        name="turn",
+    )(x)
+
+
 def fence(x):
     anywhere = pl.BlockSpec(memory_space=pl.ANY)
     return pl.pallas_call(
@@ -348,6 +364,7 @@
     for by in (1, 2, 3):
         near.append(shift(near[0], Y, 4, by))
     own = jnp.concatenate([by_group(arrived[:, :32], 4), by_group(arrived[:, 32:48], 2)], axis=0)
+    own = turn(own)
     across = swap(own, "z0")
     beside = swap(own, "c")
     beside = fence(beside)

time: 102 us -> 102 us (level)
  no operation moved by 1% of the time
where the time goes in v6:
time: 102 us; the launch traced here: 101 us
  blocking collectives  42.1 us (41%)
  waiting for transfers between devices  41.1 us (40%)
  starting transfers between devices  9.25 us (9%)
  Pallas kernels  7.99 us (8%)
    all_to_all x1, blocking collectives, body(): arrived = lax.all_to_all(pack(occ, vir, scattered), ROW, 0, 0, tiled=True)  31.3 us
    all_to_all x1, waiting for transfers between devices, body(): received = lax.all_to_all(messages, LAST, 0, 0, tiled=True)  20.6 us
    ppermute x3, waiting for transfers between devices, shift(): return lax.ppermute(x, axes, [(i, (i + by) % count) for i in range(count)])  11.3 us
    all_to_all x1, blocking collectives, body(): lax.all_to_all(prepare(row, col, occ_decay, vir_decay, occ, vir), COL, 0,...  10.8 us
    ppermute x3, waiting for transfers between devices, swap(): return lax.ppermute(x, axis, [(0, 1), (1, 0)])  9.18 us
    all_to_all x1, starting transfers between devices, body(): received = lax.all_to_all(messages, LAST, 0, 0, tiled=True)  6.01 us
    pallas_call x1, Pallas kernels, finish(): pl.pallas_call(finish_kernel, out_shape=(shape, shape), in_specs=[vmem] *...  2.76 us
    ppermute x3, starting transfers between devices, shift(): return lax.ppermute(x, axes, [(i, (i + by) % count) for i in range(count)])  2.48 us
  transfers between devices with their start and end apart: 7, of which 5 were waited for; matrix products, arithmetic and copies ran while one was open for 0% of the time, Pallas kernels for 0%

profile of v6, /device:TPU:32, one launch (start us, length us, event | category | flops | bytes accessed | tf_op | source)
XLA Modules:
  0.0 101.5 jit_solution(4650111657727579981)
XLA Ops:
  0.6 2.5 %prepare.1 = bf16[8,4,24,128]{3,2,1,0:T(8,128)(2,1)} custom-call(s32[1]{0:T(128)} %bitcast.3.row_ref, s32[1]{0:T(128)} %bitcast.4.col_ref, f32[1024]{0:T(1024)} %refs_0_.2, f32[512]{0:T(512)} %refs_1_.2, bf16[32,4096]{1,0:T(8,128)(2,1)} %occ_ref.1, bf16[16,4096]{1,0:T(8,128)(2,1)} %vir_ref.1), custom_call_target="tpu_custom_call" | custom-call | tf_op jit(solution)/shard_map/prepare/pallas_call | solution.py:135
  3.1 0.0 copy-start
  3.1 0.0 copy-start.3
  3.2 10.8 %all_to_all.15.rows_ref = bf16[8,4,24,128]{3,2,1,0:T(8,128)(2,1)S(1)} all-to-all(bf16[8,4,24,128]{3,2,1,0:T(8,128)(2,1)} %prepare.1), channel_id=1, replica_groups=mesh['xh'=2,'z2'=2,'z1'=2,'z0'=2,'c'=2,'xl'=2,'y1'=2,'y0'=2] {'xl','y1',..., dimensions={0} | all-to-all | bytes 393216 | tf_op jit(solution)/shard_map/all_to_all | solution.py:355
  13.9 0.0 copy-done
  13.9 0.0 copy-done.3
  13.9 0.1 pack.1
  14.0 31.3 %all_to_all.16 = bf16[32,72,128]{2,1,0:T(8,128)(2,1)S(1)} all-to-all(bf16[32,72,128]{2,1,0:T(8,128)(2,1)S(1)} %pack.1), channel_id=1, replica_groups=mesh['xh'=2,'z2'=2,'z1'=2,'z0'=2,'c'=2,'xl'=2,'y1'=2,'y0'=2] {'xh','z2',..., dimensions={0} | all-to-all | bytes 1179648 | tf_op jit(solution)/shard_map/all_to_all | solution.py:356
  45.5 0.2 turn.1.refs_0_
  45.7 0.8 collective-permute-start.1
  46.4 0.0 collective-permute-start
  46.5 9.2 %collective-permute-done.1.refs_2_ = bf16[128,1536]{1,0:T(8,128)(2,1)S(1)} collective-permute-done((bf16[128,1536]{1,0:T(8,128)(2,1)S(1)}, bf16[128,1536]{1,0:T(8,128)(2,1)S(1)}, u32[]{:S(2)}, u32[]{:S(2)}) %collective-permute-start.1) | collective-permute-done | bytes 393248 | tf_op jit(solution)/shard_map/ppermute | solution.py:348
  55.6 0.0 collective-permute-start.2
  55.7 0.0 copy-start.4
  55.7 0.0 copy-start.5
  55.7 1.0 collective-permute-start.5
  56.7 1.5 %collective-permute-start.4 = (bf16[768,128]{1,0:T(8,128)(2,1)S(1)}, bf16[768,128]{1,0:T(8,128)(2,1)S(1)}, u32[]{:S(2)}, u32[]{:S(2)}) collective-permute-start(bf16[768,128]{1,0:T(8,128)(2,1)S(1)} %pad_maximum_fusion.1.refs_4_), channel_id=1, source_target_pairs={{0,2},{1,3},{2,0},{3,1},{4,6},{5,7},{6,4},{7,5},{8,10},{9,11},{10,... | collective-permute-start | bytes 589832 | tf_op jit(solution)/shard_map/ppermute | solution.py:344
  58.2 0.0 collective-permute-start.3
  58.2 0.0 collective-permute-done.in_ref
  58.2 5.4 %collective-permute-done.5.refs_7_ = bf16[768,128]{1,0:T(8,128)(2,1)S(1)} collective-permute-done((bf16[768,128]{1,0:T(8,128)(2,1)S(1)}, bf16[768,128]{1,0:T(8,128)(2,1)S(1)}, u32[]{:S(2)}, u32[]{:S(2)}) %collective-permute-start.5) | collective-permute-done | bytes 196640 | tf_op jit(solution)/shard_map/ppermute | solution.py:344
  63.5 2.5 %collective-permute-done.4.refs_6_ = bf16[768,128]{1,0:T(8,128)(2,1)S(1)} collective-permute-done((bf16[768,128]{1,0:T(8,128)(2,1)S(1)}, bf16[768,128]{1,0:T(8,128)(2,1)S(1)}, u32[]{:S(2)}, u32[]{:S(2)}) %collective-permute-start.4) | collective-permute-done | bytes 196640 | tf_op jit(solution)/shard_map/ppermute | solution.py:344
  66.0 3.4 %collective-permute-done.3.refs_5_ = bf16[768,128]{1,0:T(8,128)(2,1)S(1)} collective-permute-done((bf16[768,128]{1,0:T(8,128)(2,1)S(1)}, bf16[768,128]{1,0:T(8,128)(2,1)S(1)}, u32[]{:S(2)}, u32[]{:S(2)}) %collective-permute-start.3) | collective-permute-done | bytes 196640 | tf_op jit(solution)/shard_map/ppermute | solution.py:344
  69.5 0.0 collective-permute-done.2.refs_3_
  69.5 0.0 copy-done.4
  69.5 0.0 copy-done.5
  69.5 0.0 copy-start.6
  69.5 0.0 copy-start.7
  69.5 2.4 %polar.1 = bf16[64,2,16,128]{3,2,1,0:T(8,128)(2,1)} custom-call(s32[1]{0:T(128)} %bitcast.core_ref, s32[1]{0:T(128)} %bitcast.1.z0_ref, s32[1]{0:T(128)} %bitcast.2.y_ref, bf16[128,1536]{1,0:T(8,128)(2,1)S(1)} %turn.1.refs_0_, bf16[128,1536]{1,0:T(8,128)(2,1)S(1)} %fence.1.refs_1_, bf16[128,1536]{1,0:T(8,128)(2,1)S(1)} %collective-permute-done.1.refs_2_, ...), custom_call_target="tpu_custom_call" | custom-call | tf_op jit(solution)/shard_map/polar/pallas_call | solution.py:210
  71.9 0.0 copy-start.1
  71.9 0.0 copy-start.2
  71.9 6.0 %all-to-all-start.2 = ((bf16[64,2,16,128]{3,2,1,0:T(8,128)(2,1)}), bf16[64,2,16,128]{3,2,1,0:T(8,128)(2,1)S(1)}, u32[]{:S(2)}, u32[]{:S(2)}) async-start(bf16[64,2,16,128]{3,2,1,0:T(8,128)(2,1)} %polar.1), calls=%async_computation.2 | async-start | bytes 1048576 | tf_op jit(solution)/shard_map/all_to_all | solution.py:375
  77.9 0.0 copy-done.6
  78.0 0.0 copy-done.7
  78.0 0.0 copy-done.1
  78.0 0.0 copy-done.2
  78.0 0.1 carry.1
  78.1 20.6 %all-to-all-done.2.x_ref = bf16[64,2,16,128]{3,2,1,0:T(8,128)(2,1)S(1)} async-done(((bf16[64,2,16,128]{3,2,1,0:T(8,128)(2,1)}), bf16[64,2,16,128]{3,2,1,0:T(8,128)(2,1)S(1)}, u32[]{:S(2)}, u32[]{:S(2)}) %all-to-all-start.2) | async-done | bytes 524320 | tf_op jit(solution)/shard_map/all_to_all | solution.py:375
  98.7 2.8 %finish.1 = (f32[32,4,1024]{2,1,0:T(4,128)}, f32[32,4,1024]{2,1,0:T(4,128)}) custom-call(bf16[64,2,16,128]{3,2,1,0:T(8,128)(2,1)S(1)} %all-to-all-done.2.x_ref, bf16[512,512]{1,0:T(8,128)(2,1)S(1)} %get-tuple-element.6.a_high_ref, bf16[512,512]{1,0:T(8,128)(2,1)S(1)} %get-tuple-element.7.a_low_ref, bf16[256,256]{1,0:T(8,128)(2,1)S(1)} %get-tuple-element.8.b_high_ref, ...), custom_call_target="tpu_custom_call" | custom-call | tf_op jit(solution)/shard_map/finish/pallas_call | solution.py:281
  (9 shorter events, 0.2 us)
Async XLA Ops:
  3.1 10.8 %copy-start = (bf16[32,4096]{1,0:T(8,128)(2,1)S(1)}, bf16[32,4096]{1,0:T(8,128)(2,1)}, u32[]{:S(2)}) copy-start(bf16[32,4096]{1,0:T(8,128)(2,1)} %occ_ref.1) | copy-start | bytes 786436
  3.1 10.8 %copy-start.3 = (bf16[16,4096]{1,0:T(8,128)(2,1)S(1)}, bf16[16,4096]{1,0:T(8,128)(2,1)}, u32[]{:S(2)}) copy-start(bf16[16,4096]{1,0:T(8,128)(2,1)} %vir_ref.1) | copy-start | bytes 393220
  45.7 9.9 %collective-permute-start.1 = (bf16[128,1536]{1,0:T(8,128)(2,1)S(1)}, bf16[128,1536]{1,0:T(8,128)(2,1)S(1)}, u32[]{:S(2)}, u32[]{:S(2)}) collective-permute-start(bf16[128,1536]{1,0:T(8,128)(2,1)S(1)} %turn.1.refs_0_), channel_id=1, source_target_pairs={{0,16},{16,0},{1,17},{17,1},{2,18},{18,2},{3,19},{19,3},{4,20},{20... | collective-permute-start | bytes 1179656 | tf_op jit(solution)/shard_map/ppermute | solution.py:348
  46.4 11.7 %collective-permute-start = (bf16[128,1536]{1,0:T(8,128)(2,1)S(1)}, bf16[128,1536]{1,0:T(8,128)(2,1)S(1)}, u32[]{:S(2)}, u32[]{:S(2)}) collective-permute-start(bf16[128,1536]{1,0:T(8,128)(2,1)S(1)} %turn.1.refs_0_), channel_id=1, source_target_pairs={{0,8},{8,0},{1,9},{9,1},{2,10},{10,2},{3,11},{11,3},{4,12},{12,4},... | collective-permute-start | bytes 1179656 | tf_op jit(solution)/shard_map/ppermute | solution.py:348
  55.6 13.8 %collective-permute-start.2 = (bf16[128,1536]{1,0:T(8,128)(2,1)S(1)}, bf16[128,1536]{1,0:T(8,128)(2,1)S(1)}, u32[]{:S(2)}, u32[]{:S(2)}) collective-permute-start(bf16[128,1536]{1,0:T(8,128)(2,1)S(1)} %collective-permute-done.1.refs_2_), channel_id=1, source_target_pairs={{0,8},{8,0},{1,9},{9,1},{2,10},{10,2},{3,11},{11,3},{4,12},{12,4},... | collective-permute-start | bytes 1179656 | tf_op jit(solution)/shard_map/ppermute | solution.py:348
  55.7 13.8 %copy-start.4 = (bf16[512,256]{1,0:T(8,128)(2,1)S(1)}, bf16[512,256]{1,0:T(8,128)(2,1)}, u32[]{:S(2)}) copy-start(bf16[512,256]{1,0:T(8,128)(2,1)} %constant.51.clone.refs_9_) | copy-start | bytes 786436
  55.7 13.8 %copy-start.5 = (bf16[512,256]{1,0:T(8,128)(2,1)S(1)}, bf16[512,256]{1,0:T(8,128)(2,1)}, u32[]{:S(2)}) copy-start(bf16[512,256]{1,0:T(8,128)(2,1)} %constant.50.clone.refs_8_) | copy-start | bytes 786436
  55.7 7.8 %collective-permute-start.5 = (bf16[768,128]{1,0:T(8,128)(2,1)S(1)}, bf16[768,128]{1,0:T(8,128)(2,1)S(1)}, u32[]{:S(2)}, u32[]{:S(2)}) collective-permute-start(bf16[768,128]{1,0:T(8,128)(2,1)S(1)} %pad_maximum_fusion.1.refs_4_), channel_id=1, source_target_pairs={{0,3},{1,0},{2,1},{3,2},{4,7},{5,4},{6,5},{7,6},{8,11},{9,8},{10,9... | collective-permute-start | bytes 589832 | tf_op jit(solution)/shard_map/ppermute | solution.py:344
  56.7 9.3 %collective-permute-start.4 = (bf16[768,128]{1,0:T(8,128)(2,1)S(1)}, bf16[768,128]{1,0:T(8,128)(2,1)S(1)}, u32[]{:S(2)}, u32[]{:S(2)}) collective-permute-start(bf16[768,128]{1,0:T(8,128)(2,1)S(1)} %pad_maximum_fusion.1.refs_4_), channel_id=1, source_target_pairs={{0,2},{1,3},{2,0},{3,1},{4,6},{5,7},{6,4},{7,5},{8,10},{9,11},{10,... | collective-permute-start | bytes 589832 | tf_op jit(solution)/shard_map/ppermute | solution.py:344
  58.2 11.3 %collective-permute-start.3 = (bf16[768,128]{1,0:T(8,128)(2,1)S(1)}, bf16[768,128]{1,0:T(8,128)(2,1)S(1)}, u32[]{:S(2)}, u32[]{:S(2)}) collective-permute-start(bf16[768,128]{1,0:T(8,128)(2,1)S(1)} %pad_maximum_fusion.1.refs_4_), channel_id=1, source_target_pairs={{0,1},{1,2},{2,3},{3,0},{4,5},{5,6},{6,7},{7,4},{8,9},{9,10},{10,1... | collective-permute-start | bytes 589832 | tf_op jit(solution)/shard_map/ppermute | solution.py:344
  69.5 8.5 %copy-start.6 = (bf16[256,256]{1,0:T(8,128)(2,1)S(1)}, bf16[256,256]{1,0:T(8,128)(2,1)}, u32[]{:S(2)}) copy-start(bf16[256,256]{1,0:T(8,128)(2,1)} %constant.55.clone.refs_3_) | copy-start | bytes 393220
  69.5 8.5 %copy-start.7 = (bf16[256,256]{1,0:T(8,128)(2,1)S(1)}, bf16[256,256]{1,0:T(8,128)(2,1)}, u32[]{:S(2)}) copy-start(bf16[256,256]{1,0:T(8,128)(2,1)} %constant.54.clone.refs_2_) | copy-start | bytes 393220
  71.9 6.0 %copy-start.1 = (bf16[512,512]{1,0:T(8,128)(2,1)S(1)}, bf16[512,512]{1,0:T(8,128)(2,1)}, u32[]{:S(2)}) copy-start(bf16[512,512]{1,0:T(8,128)(2,1)} %constant.53.clone.refs_1_) | copy-start | bytes 1572868
  71.9 6.1 %copy-start.2 = (bf16[512,512]{1,0:T(8,128)(2,1)S(1)}, bf16[512,512]{1,0:T(8,128)(2,1)}, u32[]{:S(2)}) copy-start(bf16[512,512]{1,0:T(8,128)(2,1)} %constant.52.clone.refs_0_) | copy-start | bytes 1572868
  71.9 26.8 %all-to-all-start.2 = ((bf16[64,2,16,128]{3,2,1,0:T(8,128)(2,1)}), bf16[64,2,16,128]{3,2,1,0:T(8,128)(2,1)S(1)}, u32[]{:S(2)}, u32[]{:S(2)}) async-start(bf16[64,2,16,128]{3,2,1,0:T(8,128)(2,1)} %polar.1), calls=%async_computation.2 | async-start | bytes 1048576 | tf_op jit(solution)/shard_map/all_to_all | solution.py:375

commit v7 on v6

--- a/solution.py
+++ b/solution.py
@@ -72,23 +72,24 @@
     return lax.dot_general(a, b, (((1,), (0,)), ((), ())), preferred_element_type=F32)
 
 
-def prepare_kernel(row_ref, col_ref, *refs):
-    @pl.when(col_ref[0] == 0)
+def prepare_kernel(*refs):
+    @pl.when(lax.axis_index(COL) == 0)
     def _():
-        prepare_rows(row_ref[0], *refs)
-
-
-def prepare_rows(
-    row, occ_decay_ref, vir_decay_ref, occ_hbm, vir_hbm, out_hbm, occ_ref, vir_ref, out_ref, sems
-):
+        prepare_rows(lax.axis_index(ROW), *refs)
+
+
+def prepare_rows(row, *refs):
+    sources, out_hbm, targets, (out_ref, sems) = refs[:4], refs[4], refs[5:9], refs[9:]
+    sources = (sources[0], sources[1], sources[2].at[:, :1024], sources[3].at[:, :1024])
     copies = [
-        pltpu.make_async_copy(occ_hbm.at[:, :1024], occ_ref, sems.at[0]),
-        pltpu.make_async_copy(vir_hbm.at[:, :1024], vir_ref, sems.at[1]),
+        pltpu.make_async_copy(source, target, sems.at[k])
+        for k, (source, target) in enumerate(zip(sources, targets))
     ]
     for copy in copies:
         copy.start()
     for copy in copies:
         copy.wait()
+    occ_decay_ref, vir_decay_ref, occ_ref, vir_ref = targets
 
     def column(decay_ref, count):
         index = lax.broadcasted_iota(jnp.int32, (count, 128), 0)
@@ -124,27 +125,28 @@
                 ).astype(BF16)
                 for xl in range(2):
                     out_ref[4 * xl + 2 * y1 + t, kind] = piece
-    result = pltpu.make_async_copy(out_ref, out_hbm, sems.at[2])
+    result = pltpu.make_async_copy(out_ref, out_hbm, sems.at[4])
     result.start()
     result.wait()
 
 
-def prepare(row, col, occ_decay, vir_decay, occ, vir):
-    smem = pl.BlockSpec(memory_space=pltpu.SMEM)
+def prepare(occ_decay, vir_decay, occ, vir):
     hbm = pl.BlockSpec(memory_space=pl.ANY)
     return pl.pallas_call(
         prepare_kernel,
         out_shape=jax.ShapeDtypeStruct((8, 4, 24, 128), BF16),
-        in_specs=[smem] * 4 + [hbm] * 2,
+        in_specs=[hbm] * 4,
         out_specs=hbm,
         scratch_shapes=[
+            pltpu.SMEM((1024,), F32),
+            pltpu.SMEM((512,), F32),
             pltpu.VMEM((32, 1024), BF16),
             pltpu.VMEM((16, 1024), BF16),
             pltpu.VMEM((8, 4, 24, 128), BF16),
-            pltpu.SemaphoreType.DMA((3,)),
+            pltpu.SemaphoreType.DMA((5,)),
         ],
         name="prepare",
-    )(row, col, occ_decay, vir_decay, occ, vir)
+    )(occ_decay, vir_decay, occ, vir)
 
 
 def pack_kernel(occ_ref, vir_ref, rows_ref, out_ref):
@@ -166,10 +168,10 @@
     )(occ, vir, rows)
 
 
-def polar_kernel(core_ref, z0_ref, y_ref, *refs):
+def polar_kernel(*refs):
     points, near, (high_ref, low_ref) = refs[:4], refs[4:8], refs[8:10]
     out_ref, polar_ref, occ_ref, vir_ref = refs[-4:]
-    core, z0, y = core_ref[0], z0_ref[0], y_ref[0]
+    core, z0, y = (lax.axis_index(axes) for axes in ("c", "z0", Y))
     for step in range(4):
         chunk = lax.rem(y + 4 - step, 4)
         y1, y0 = lax.div(chunk, 2), lax.rem(chunk, 2)
@@ -210,7 +212,7 @@
     return pl.pallas_call(
         polar_kernel,
         out_shape=jax.ShapeDtypeStruct((64, 2, 16, 128), BF16),
-        in_specs=[pl.BlockSpec(memory_space=pltpu.SMEM)] * 3 + [vmem] * 10,
+        in_specs=[vmem] * 10,
         out_specs=vmem,
         scratch_shapes=[
             pltpu.VMEM((512, 256), F32),
@@ -349,10 +351,7 @@
 
 
 def body(occ, vir, occ_decay, vir_decay):
-    row = lax.axis_index(ROW).astype(jnp.int32).reshape(1)
-    col = lax.axis_index(COL).astype(jnp.int32).reshape(1)
-    place = [lax.axis_index(a).astype(jnp.int32).reshape(1) for a in ("c", "z0", Y)]
-    scattered = lax.all_to_all(prepare(row, col, occ_decay, vir_decay, occ, vir), COL, 0, 0, tiled=True)
+    scattered = lax.all_to_all(prepare(occ_decay, vir_decay, occ, vir), COL, 0, 0, tiled=True)
     arrived = lax.all_to_all(pack(occ, vir, scattered), ROW, 0, 0, tiled=True)
 
     def by_group(part, count):
@@ -370,7 +369,7 @@
     beside = fence(beside)
     opposite = swap(across, "c")
     points = (own, beside, across, opposite)
-    messages = polar_messages(*place, *points, *near, *c_table())
+    messages = polar_messages(*points, *near, *c_table())
 
     received = lax.all_to_all(messages, LAST, 0, 0, tiled=True)
     tables = carry(*a_table(), *b_table())

time: 102 us -> 101 us (level)
  no operation moved by 1% of the time
where the time goes in v7:
time: 101 us
  blocking collectives  42.1 us (42%)
  waiting for transfers between devices  41.1 us (41%)
  starting transfers between devices  9.26 us (9%)
  Pallas kernels  7.3 us (7%)
    all_to_all x1, blocking collectives, body(): arrived = lax.all_to_all(pack(occ, vir, scattered), ROW, 0, 0, tiled=True)  31.3 us
    all_to_all x1, waiting for transfers between devices, body(): received = lax.all_to_all(messages, LAST, 0, 0, tiled=True)  20.6 us
    ppermute x3, waiting for transfers between devices, shift(): return lax.ppermute(x, axes, [(i, (i + by) % count) for i in range(count)])  11.3 us
    all_to_all x1, blocking collectives, body(): lax.all_to_all(prepare(occ_decay, vir_decay, occ, vir), COL, 0, 0, tiled=...  10.8 us
    ppermute x3, waiting for transfers between devices, swap(): return lax.ppermute(x, axis, [(0, 1), (1, 0)])  9.18 us
    all_to_all x1, starting transfers between devices, body(): received = lax.all_to_all(messages, LAST, 0, 0, tiled=True)  6.02 us
    pallas_call x1, Pallas kernels, finish(): pl.pallas_call(finish_kernel, out_shape=(shape, shape), in_specs=[vmem] *...  2.76 us
    ppermute x3, starting transfers between devices, shift(): return lax.ppermute(x, axes, [(i, (i + by) % count) for i in range(count)])  2.48 us
  transfers between devices with their start and end apart: 7, of which 5 were waited for; matrix products, arithmetic and copies ran while one was open for 0% of the time, Pallas kernels for 0%

profile of v7, /device:TPU:32, one launch (start us, length us, event | category | flops | bytes accessed | tf_op | source)
XLA Modules:
  0.0 100.8 jit_solution(9173014366274358288)
XLA Ops:
  0.6 1.8 %prepare.1 = bf16[8,4,24,128]{3,2,1,0:T(8,128)(2,1)} custom-call(f32[1024]{0:T(1024)} %refs_0_.2, f32[512]{0:T(512)} %refs_1_.2, bf16[32,4096]{1,0:T(8,128)(2,1)} %occ_ref.1, bf16[16,4096]{1,0:T(8,128)(2,1)} %vir_ref.1), custom_call_target="tpu_custom_call" | custom-call | tf_op jit(solution)/shard_map/prepare/pallas_call | solution.py:135
  2.4 0.0 copy-start
  2.4 0.0 copy-start.3
  2.4 10.8 %all_to_all.15.rows_ref = bf16[8,4,24,128]{3,2,1,0:T(8,128)(2,1)S(1)} all-to-all(bf16[8,4,24,128]{3,2,1,0:T(8,128)(2,1)} %prepare.1), channel_id=1, replica_groups=mesh['xh'=2,'z2'=2,'z1'=2,'z0'=2,'c'=2,'xl'=2,'y1'=2,'y0'=2] {'xl','y1',..., dimensions={0} | all-to-all | bytes 393216 | tf_op jit(solution)/shard_map/all_to_all | solution.py:354
  13.2 0.0 copy-done
  13.2 0.0 copy-done.3
  13.2 0.1 pack.1
  13.3 31.3 %all_to_all.16 = bf16[32,72,128]{2,1,0:T(8,128)(2,1)S(1)} all-to-all(bf16[32,72,128]{2,1,0:T(8,128)(2,1)S(1)} %pack.1), channel_id=1, replica_groups=mesh['xh'=2,'z2'=2,'z1'=2,'z0'=2,'c'=2,'xl'=2,'y1'=2,'y0'=2] {'xh','z2',..., dimensions={0} | all-to-all | bytes 1179648 | tf_op jit(solution)/shard_map/all_to_all | solution.py:355
  44.8 0.2 turn.1.refs_0_
  44.9 0.8 collective-permute-start.1
  45.7 0.0 collective-permute-start
  45.7 9.2 %collective-permute-done.1.refs_2_ = bf16[128,1536]{1,0:T(8,128)(2,1)S(1)} collective-permute-done((bf16[128,1536]{1,0:T(8,128)(2,1)S(1)}, bf16[128,1536]{1,0:T(8,128)(2,1)S(1)}, u32[]{:S(2)}, u32[]{:S(2)}) %collective-permute-start.1) | collective-permute-done | bytes 393248 | tf_op jit(solution)/shard_map/ppermute | solution.py:350
  54.9 0.0 collective-permute-start.2
  54.9 0.0 copy-start.4
  54.9 0.0 copy-start.5
  55.0 1.0 %collective-permute-start.5 = (bf16[768,128]{1,0:T(8,128)(2,1)S(1)}, bf16[768,128]{1,0:T(8,128)(2,1)S(1)}, u32[]{:S(2)}, u32[]{:S(2)}) collective-permute-start(bf16[768,128]{1,0:T(8,128)(2,1)S(1)} %pad_maximum_fusion.1.refs_4_), channel_id=1, source_target_pairs={{0,3},{1,0},{2,1},{3,2},{4,7},{5,4},{6,5},{7,6},{8,11},{9,8},{10,9... | collective-permute-start | bytes 589832 | tf_op jit(solution)/shard_map/ppermute | solution.py:346
  56.0 1.5 %collective-permute-start.4 = (bf16[768,128]{1,0:T(8,128)(2,1)S(1)}, bf16[768,128]{1,0:T(8,128)(2,1)S(1)}, u32[]{:S(2)}, u32[]{:S(2)}) collective-permute-start(bf16[768,128]{1,0:T(8,128)(2,1)S(1)} %pad_maximum_fusion.1.refs_4_), channel_id=1, source_target_pairs={{0,2},{1,3},{2,0},{3,1},{4,6},{5,7},{6,4},{7,5},{8,10},{9,11},{10,... | collective-permute-start | bytes 589832 | tf_op jit(solution)/shard_map/ppermute | solution.py:346
  57.4 0.0 collective-permute-start.3
  57.4 0.0 collective-permute-done.in_ref
  57.4 5.4 %collective-permute-done.5.refs_7_ = bf16[768,128]{1,0:T(8,128)(2,1)S(1)} collective-permute-done((bf16[768,128]{1,0:T(8,128)(2,1)S(1)}, bf16[768,128]{1,0:T(8,128)(2,1)S(1)}, u32[]{:S(2)}, u32[]{:S(2)}) %collective-permute-start.5) | collective-permute-done | bytes 196640 | tf_op jit(solution)/shard_map/ppermute | solution.py:346
  62.8 2.5 %collective-permute-done.4.refs_6_ = bf16[768,128]{1,0:T(8,128)(2,1)S(1)} collective-permute-done((bf16[768,128]{1,0:T(8,128)(2,1)S(1)}, bf16[768,128]{1,0:T(8,128)(2,1)S(1)}, u32[]{:S(2)}, u32[]{:S(2)}) %collective-permute-start.4) | collective-permute-done | bytes 196640 | tf_op jit(solution)/shard_map/ppermute | solution.py:346
  65.3 3.4 %collective-permute-done.3.refs_5_ = bf16[768,128]{1,0:T(8,128)(2,1)S(1)} collective-permute-done((bf16[768,128]{1,0:T(8,128)(2,1)S(1)}, bf16[768,128]{1,0:T(8,128)(2,1)S(1)}, u32[]{:S(2)}, u32[]{:S(2)}) %collective-permute-start.3) | collective-permute-done | bytes 196640 | tf_op jit(solution)/shard_map/ppermute | solution.py:346
  68.7 0.0 collective-permute-done.2.refs_3_
  68.7 0.0 copy-done.4
  68.7 0.0 copy-done.5
  68.7 0.0 copy-start.6
  68.7 0.0 copy-start.7
  68.7 2.5 %polar.1 = bf16[64,2,16,128]{3,2,1,0:T(8,128)(2,1)} custom-call(bf16[128,1536]{1,0:T(8,128)(2,1)S(1)} %turn.1.refs_0_, bf16[128,1536]{1,0:T(8,128)(2,1)S(1)} %fence.1.refs_1_, bf16[128,1536]{1,0:T(8,128)(2,1)S(1)} %collective-permute-done.1.refs_2_, bf16[128,1536]{1,0:T(8,128)(2,1)S(1)} %collective-permute-done.2.refs_3_, ...), custom_call_target="tpu_custom_call" | custom-call | tf_op jit(solution)/shard_map/polar/pallas_call | solution.py:212
  71.2 0.0 copy-start.1
  71.2 0.0 copy-start.2
  71.2 6.0 %all-to-all-start.2 = ((bf16[64,2,16,128]{3,2,1,0:T(8,128)(2,1)}), bf16[64,2,16,128]{3,2,1,0:T(8,128)(2,1)S(1)}, u32[]{:S(2)}, u32[]{:S(2)}) async-start(bf16[64,2,16,128]{3,2,1,0:T(8,128)(2,1)} %polar.1), calls=%async_computation.2 | async-start | bytes 1048576 | tf_op jit(solution)/shard_map/all_to_all | solution.py:374
  77.2 0.0 copy-done.6
  77.2 0.0 copy-done.7
  77.2 0.0 copy-done.1
  77.3 0.0 copy-done.2
  77.3 0.1 carry.1
  77.4 20.6 %all-to-all-done.2.x_ref = bf16[64,2,16,128]{3,2,1,0:T(8,128)(2,1)S(1)} async-done(((bf16[64,2,16,128]{3,2,1,0:T(8,128)(2,1)}), bf16[64,2,16,128]{3,2,1,0:T(8,128)(2,1)S(1)}, u32[]{:S(2)}, u32[]{:S(2)}) %all-to-all-start.2) | async-done | bytes 524320 | tf_op jit(solution)/shard_map/all_to_all | solution.py:374
  98.0 2.8 %finish.1 = (f32[32,4,1024]{2,1,0:T(4,128)}, f32[32,4,1024]{2,1,0:T(4,128)}) custom-call(bf16[64,2,16,128]{3,2,1,0:T(8,128)(2,1)S(1)} %all-to-all-done.2.x_ref, bf16[512,512]{1,0:T(8,128)(2,1)S(1)} %get-tuple-element.6.a_high_ref, bf16[512,512]{1,0:T(8,128)(2,1)S(1)} %get-tuple-element.7.a_low_ref, bf16[256,256]{1,0:T(8,128)(2,1)S(1)} %get-tuple-element.8.b_high_ref, ...), custom_call_target="tpu_custom_call" | custom-call | tf_op jit(solution)/shard_map/finish/pallas_call | solution.py:283
  (9 shorter events, 0.2 us)
Async XLA Ops:
  2.4 10.8 %copy-start = (bf16[32,4096]{1,0:T(8,128)(2,1)S(1)}, bf16[32,4096]{1,0:T(8,128)(2,1)}, u32[]{:S(2)}) copy-start(bf16[32,4096]{1,0:T(8,128)(2,1)} %occ_ref.1) | copy-start | bytes 786436
  2.4 10.8 %copy-start.3 = (bf16[16,4096]{1,0:T(8,128)(2,1)S(1)}, bf16[16,4096]{1,0:T(8,128)(2,1)}, u32[]{:S(2)}) copy-start(bf16[16,4096]{1,0:T(8,128)(2,1)} %vir_ref.1) | copy-start | bytes 393220
  44.9 9.9 %collective-permute-start.1 = (bf16[128,1536]{1,0:T(8,128)(2,1)S(1)}, bf16[128,1536]{1,0:T(8,128)(2,1)S(1)}, u32[]{:S(2)}, u32[]{:S(2)}) collective-permute-start(bf16[128,1536]{1,0:T(8,128)(2,1)S(1)} %turn.1.refs_0_), channel_id=1, source_target_pairs={{0,16},{16,0},{1,17},{17,1},{2,18},{18,2},{3,19},{19,3},{4,20},{20... | collective-permute-start | bytes 1179656 | tf_op jit(solution)/shard_map/ppermute | solution.py:350
  45.7 11.7 %collective-permute-start = (bf16[128,1536]{1,0:T(8,128)(2,1)S(1)}, bf16[128,1536]{1,0:T(8,128)(2,1)S(1)}, u32[]{:S(2)}, u32[]{:S(2)}) collective-permute-start(bf16[128,1536]{1,0:T(8,128)(2,1)S(1)} %turn.1.refs_0_), channel_id=1, source_target_pairs={{0,8},{8,0},{1,9},{9,1},{2,10},{10,2},{3,11},{11,3},{4,12},{12,4},... | collective-permute-start | bytes 1179656 | tf_op jit(solution)/shard_map/ppermute | solution.py:350
  54.9 13.8 %collective-permute-start.2 = (bf16[128,1536]{1,0:T(8,128)(2,1)S(1)}, bf16[128,1536]{1,0:T(8,128)(2,1)S(1)}, u32[]{:S(2)}, u32[]{:S(2)}) collective-permute-start(bf16[128,1536]{1,0:T(8,128)(2,1)S(1)} %collective-permute-done.1.refs_2_), channel_id=1, source_target_pairs={{0,8},{8,0},{1,9},{9,1},{2,10},{10,2},{3,11},{11,3},{4,12},{12,4},... | collective-permute-start | bytes 1179656 | tf_op jit(solution)/shard_map/ppermute | solution.py:350
  54.9 13.8 %copy-start.4 = (bf16[512,256]{1,0:T(8,128)(2,1)S(1)}, bf16[512,256]{1,0:T(8,128)(2,1)}, u32[]{:S(2)}) copy-start(bf16[512,256]{1,0:T(8,128)(2,1)} %constant.13.clone.refs_9_) | copy-start | bytes 786436
  54.9 13.8 %copy-start.5 = (bf16[512,256]{1,0:T(8,128)(2,1)S(1)}, bf16[512,256]{1,0:T(8,128)(2,1)}, u32[]{:S(2)}) copy-start(bf16[512,256]{1,0:T(8,128)(2,1)} %constant.12.clone.refs_8_) | copy-start | bytes 786436
  55.0 7.8 %collective-permute-start.5 = (bf16[768,128]{1,0:T(8,128)(2,1)S(1)}, bf16[768,128]{1,0:T(8,128)(2,1)S(1)}, u32[]{:S(2)}, u32[]{:S(2)}) collective-permute-start(bf16[768,128]{1,0:T(8,128)(2,1)S(1)} %pad_maximum_fusion.1.refs_4_), channel_id=1, source_target_pairs={{0,3},{1,0},{2,1},{3,2},{4,7},{5,4},{6,5},{7,6},{8,11},{9,8},{10,9... | collective-permute-start | bytes 589832 | tf_op jit(solution)/shard_map/ppermute | solution.py:346
  56.0 9.3 %collective-permute-start.4 = (bf16[768,128]{1,0:T(8,128)(2,1)S(1)}, bf16[768,128]{1,0:T(8,128)(2,1)S(1)}, u32[]{:S(2)}, u32[]{:S(2)}) collective-permute-start(bf16[768,128]{1,0:T(8,128)(2,1)S(1)} %pad_maximum_fusion.1.refs_4_), channel_id=1, source_target_pairs={{0,2},{1,3},{2,0},{3,1},{4,6},{5,7},{6,4},{7,5},{8,10},{9,11},{10,... | collective-permute-start | bytes 589832 | tf_op jit(solution)/shard_map/ppermute | solution.py:346
  57.4 11.3 %collective-permute-start.3 = (bf16[768,128]{1,0:T(8,128)(2,1)S(1)}, bf16[768,128]{1,0:T(8,128)(2,1)S(1)}, u32[]{:S(2)}, u32[]{:S(2)}) collective-permute-start(bf16[768,128]{1,0:T(8,128)(2,1)S(1)} %pad_maximum_fusion.1.refs_4_), channel_id=1, source_target_pairs={{0,1},{1,2},{2,3},{3,0},{4,5},{5,6},{6,7},{7,4},{8,9},{9,10},{10,1... | collective-permute-start | bytes 589832 | tf_op jit(solution)/shard_map/ppermute | solution.py:346
  68.7 8.5 %copy-start.6 = (bf16[256,256]{1,0:T(8,128)(2,1)S(1)}, bf16[256,256]{1,0:T(8,128)(2,1)}, u32[]{:S(2)}) copy-start(bf16[256,256]{1,0:T(8,128)(2,1)} %constant.17.clone.refs_3_) | copy-start | bytes 393220
  68.7 8.5 %copy-start.7 = (bf16[256,256]{1,0:T(8,128)(2,1)S(1)}, bf16[256,256]{1,0:T(8,128)(2,1)}, u32[]{:S(2)}) copy-start(bf16[256,256]{1,0:T(8,128)(2,1)} %constant.16.clone.refs_2_) | copy-start | bytes 393220
  71.2 6.1 %copy-start.1 = (bf16[512,512]{1,0:T(8,128)(2,1)S(1)}, bf16[512,512]{1,0:T(8,128)(2,1)}, u32[]{:S(2)}) copy-start(bf16[512,512]{1,0:T(8,128)(2,1)} %constant.15.clone.refs_1_) | copy-start | bytes 1572868
  71.2 6.1 %copy-start.2 = (bf16[512,512]{1,0:T(8,128)(2,1)S(1)}, bf16[512,512]{1,0:T(8,128)(2,1)}, u32[]{:S(2)}) copy-start(bf16[512,512]{1,0:T(8,128)(2,1)} %constant.14.clone.refs_0_) | copy-start | bytes 1572868
  71.2 26.8 %all-to-all-start.2 = ((bf16[64,2,16,128]{3,2,1,0:T(8,128)(2,1)}), bf16[64,2,16,128]{3,2,1,0:T(8,128)(2,1)S(1)}, u32[]{:S(2)}, u32[]{:S(2)}) async-start(bf16[64,2,16,128]{3,2,1,0:T(8,128)(2,1)} %polar.1), calls=%async_computation.2 | async-start | bytes 1048576 | tf_op jit(solution)/shard_map/all_to_all | solution.py:374

commit v8 on v7

--- a/solution.py
+++ b/solution.py
@@ -224,7 +224,7 @@
     )(*arrays)
 
 
-def finish_kernel(x_ref, a_high_ref, a_low_ref, b_high_ref, b_low_ref, *refs):
+def finish_kernel(x_ref, a_ref, b_high_ref, b_low_ref, *refs):
     outs, parts, sems = refs[:2], refs[2:4], refs[4]
     x = jnp.concatenate(
         [
@@ -236,7 +236,7 @@
         ],
         axis=1,
     )
-    planes = dot(a_high_ref[...], x) + dot(a_low_ref[...], x)
+    planes = dot(a_ref[...], x)
     copies = []
     for part in range(4):
         z = jnp.concatenate(
@@ -283,7 +283,7 @@
     return pl.pallas_call(
         finish_kernel,
         out_shape=(shape, shape),
-        in_specs=[vmem] * 5,
+        in_specs=[vmem] * 4,
         out_specs=(hbm, hbm),
         scratch_shapes=[
             pltpu.VMEM((32, 4, 1024), F32),
@@ -293,24 +293,6 @@
         compiler_params=pltpu.CompilerParams(vmem_limit_bytes=LIMIT),
         name="finish",
     )(x, *tables)
-
-
-def carry_kernel(*refs):
-    count = len(refs) // 2
-    for in_ref, out_ref in zip(refs[:count], refs[count:]):
-        out_ref[...] = in_ref[...]
-
-
-def carry(*arrays):
-    vmem = pl.BlockSpec(memory_space=pltpu.VMEM)
-    return pl.pallas_call(
-        carry_kernel,
-        out_shape=[jax.ShapeDtypeStruct(a.shape, a.dtype) for a in arrays],
-        in_specs=[vmem] * len(arrays),
-        out_specs=[vmem] * len(arrays),
-        compiler_params=pltpu.CompilerParams(vmem_limit_bytes=LIMIT),
-        name="carry",
-    )(*arrays)
 
 
 def turn_kernel(in_ref, out_ref):
@@ -372,8 +354,7 @@
     messages = polar_messages(*points, *near, *c_table())
 
     received = lax.all_to_all(messages, LAST, 0, 0, tiled=True)
-    tables = carry(*a_table(), *b_table())
-    return finish(received, *tables)
+    return finish(received, a_table()[0], *b_table())
 
 
 def solution(mesh):

time: 101 us -> 99.8 us (0.988)
  blocking collectives: 42.1 us -> 68.7 us
  waiting for transfers between devices: 41.1 us -> 20.4 us
  starting transfers between devices: 9.26 us -> 3.24 us
  Pallas kernels: 7.3 us -> 6.15 us
    all_to_all x0 -> x1, blocking collectives: none -> 26.6 us  [body(): received = lax.all_to_all(messages, LAST, 0, 0, tiled=True)]
    all_to_all x1 -> x0, waiting for transfers between devices: 20.6 us -> none  [body(): received = lax.all_to_all(messages, LAST, 0, 0, tiled=True)]
    all_to_all x1 -> x0, starting transfers between devices: 6.02 us -> none  [body(): received = lax.all_to_all(messages, LAST, 0, 0, tiled=True)]
  transfers between devices with their start and end apart: 7 -> 6, of which waited for: 5 -> 4; matrix products, arithmetic and copies ran while one was open for 0% -> 0% of each run, Pallas kernels for 0% -> 0%
where the time goes in v8:
time: 99.8 us; the launch traced here: 99.5 us
  blocking collectives  68.7 us (69%)
  waiting for transfers between devices  20.4 us (20%)
  Pallas kernels  6.15 us (6%)
  starting transfers between devices  3.24 us (3%)
    all_to_all x1, blocking collectives, body(): arrived = lax.all_to_all(pack(occ, vir, scattered), ROW, 0, 0, tiled=True)  31.3 us
    all_to_all x1, blocking collectives, body(): received = lax.all_to_all(messages, LAST, 0, 0, tiled=True)  26.6 us
    ppermute x3, waiting for transfers between devices, shift(): return lax.ppermute(x, axes, [(i, (i + by) % count) for i in range(count)])  11.3 us
    all_to_all x1, blocking collectives, body(): lax.all_to_all(prepare(occ_decay, vir_decay, occ, vir), COL, 0, 0, tiled=...  10.8 us
    ppermute x3, waiting for transfers between devices, swap(): return lax.ppermute(x, axis, [(0, 1), (1, 0)])  9.18 us
    pallas_call x1, Pallas kernels, finish(): pl.pallas_call(finish_kernel, out_shape=(shape, shape), in_specs=[vmem] *...  2.5 us
    ppermute x3, starting transfers between devices, shift(): return lax.ppermute(x, axes, [(i, (i + by) % count) for i in range(count)])  2.48 us
  transfers between devices with their start and end apart: 6, of which 4 were waited for; matrix products, arithmetic and copies ran while one was open for 0% of the time, Pallas kernels for 0%

profile of v8, /device:TPU:32, one launch (start us, length us, event | category | flops | bytes accessed | tf_op | source)
XLA Modules:
  0.0 99.5 jit_solution(13294460811653556274)
XLA Ops:
  0.6 1.8 %prepare.1 = bf16[8,4,24,128]{3,2,1,0:T(8,128)(2,1)} custom-call(f32[1024]{0:T(1024)} %refs_0_.1, f32[512]{0:T(512)} %refs_1_.1, bf16[32,4096]{1,0:T(8,128)(2,1)} %occ_ref.1, bf16[16,4096]{1,0:T(8,128)(2,1)} %vir_ref.1), custom_call_target="tpu_custom_call" | custom-call | tf_op jit(solution)/shard_map/prepare/pallas_call | solution.py:135
  2.4 0.0 copy-start
  2.4 0.0 copy-start.2
  2.4 10.8 %all_to_all.15.rows_ref = bf16[8,4,24,128]{3,2,1,0:T(8,128)(2,1)S(1)} all-to-all(bf16[8,4,24,128]{3,2,1,0:T(8,128)(2,1)} %prepare.1), channel_id=1, replica_groups=mesh['xh'=2,'z2'=2,'z1'=2,'z0'=2,'c'=2,'xl'=2,'y1'=2,'y0'=2] {'xl','y1',..., dimensions={0} | all-to-all | bytes 393216 | tf_op jit(solution)/shard_map/all_to_all | solution.py:336
  13.2 0.0 copy-done
  13.2 0.0 copy-done.2
  13.2 0.1 pack.1
  13.3 31.3 %all_to_all.16 = bf16[32,72,128]{2,1,0:T(8,128)(2,1)S(1)} all-to-all(bf16[32,72,128]{2,1,0:T(8,128)(2,1)S(1)} %pack.1), channel_id=1, replica_groups=mesh['xh'=2,'z2'=2,'z1'=2,'z0'=2,'c'=2,'xl'=2,'y1'=2,'y0'=2] {'xh','z2',..., dimensions={0} | all-to-all | bytes 1179648 | tf_op jit(solution)/shard_map/all_to_all | solution.py:337
  44.8 0.2 turn.1.refs_0_
  44.9 0.8 collective-permute-start.1
  45.7 0.0 collective-permute-start
  45.7 9.2 %collective-permute-done.1.refs_2_ = bf16[128,1536]{1,0:T(8,128)(2,1)S(1)} collective-permute-done((bf16[128,1536]{1,0:T(8,128)(2,1)S(1)}, bf16[128,1536]{1,0:T(8,128)(2,1)S(1)}, u32[]{:S(2)}, u32[]{:S(2)}) %collective-permute-start.1) | collective-permute-done | bytes 393248 | tf_op jit(solution)/shard_map/ppermute | solution.py:332
  54.9 0.0 collective-permute-start.2
  54.9 0.0 copy-start.3
  54.9 0.0 copy-start.4
  55.0 1.0 %collective-permute-start.5 = (bf16[768,128]{1,0:T(8,128)(2,1)S(1)}, bf16[768,128]{1,0:T(8,128)(2,1)S(1)}, u32[]{:S(2)}, u32[]{:S(2)}) collective-permute-start(bf16[768,128]{1,0:T(8,128)(2,1)S(1)} %pad_maximum_fusion.1.refs_4_), channel_id=1, source_target_pairs={{0,3},{1,0},{2,1},{3,2},{4,7},{5,4},{6,5},{7,6},{8,11},{9,8},{10,9... | collective-permute-start | bytes 589832 | tf_op jit(solution)/shard_map/ppermute | solution.py:328
  56.0 1.5 %collective-permute-start.4 = (bf16[768,128]{1,0:T(8,128)(2,1)S(1)}, bf16[768,128]{1,0:T(8,128)(2,1)S(1)}, u32[]{:S(2)}, u32[]{:S(2)}) collective-permute-start(bf16[768,128]{1,0:T(8,128)(2,1)S(1)} %pad_maximum_fusion.1.refs_4_), channel_id=1, source_target_pairs={{0,2},{1,3},{2,0},{3,1},{4,6},{5,7},{6,4},{7,5},{8,10},{9,11},{10,... | collective-permute-start | bytes 589832 | tf_op jit(solution)/shard_map/ppermute | solution.py:328
  57.4 0.0 collective-permute-start.3
  57.4 0.0 collective-permute-done.in_ref
  57.4 5.4 %collective-permute-done.5.refs_7_ = bf16[768,128]{1,0:T(8,128)(2,1)S(1)} collective-permute-done((bf16[768,128]{1,0:T(8,128)(2,1)S(1)}, bf16[768,128]{1,0:T(8,128)(2,1)S(1)}, u32[]{:S(2)}, u32[]{:S(2)}) %collective-permute-start.5) | collective-permute-done | bytes 196640 | tf_op jit(solution)/shard_map/ppermute | solution.py:328
  62.8 2.5 %collective-permute-done.4.refs_6_ = bf16[768,128]{1,0:T(8,128)(2,1)S(1)} collective-permute-done((bf16[768,128]{1,0:T(8,128)(2,1)S(1)}, bf16[768,128]{1,0:T(8,128)(2,1)S(1)}, u32[]{:S(2)}, u32[]{:S(2)}) %collective-permute-start.4) | collective-permute-done | bytes 196640 | tf_op jit(solution)/shard_map/ppermute | solution.py:328
  65.3 3.4 %collective-permute-done.3.refs_5_ = bf16[768,128]{1,0:T(8,128)(2,1)S(1)} collective-permute-done((bf16[768,128]{1,0:T(8,128)(2,1)S(1)}, bf16[768,128]{1,0:T(8,128)(2,1)S(1)}, u32[]{:S(2)}, u32[]{:S(2)}) %collective-permute-start.3) | collective-permute-done | bytes 196640 | tf_op jit(solution)/shard_map/ppermute | solution.py:328
  68.7 0.0 collective-permute-done.2.refs_3_
  68.7 0.0 copy-done.3
  68.7 0.0 copy-done.4
  68.7 1.7 %polar.1 = bf16[64,2,16,128]{3,2,1,0:T(8,128)(2,1)S(1)} custom-call(bf16[128,1536]{1,0:T(8,128)(2,1)S(1)} %turn.1.refs_0_, bf16[128,1536]{1,0:T(8,128)(2,1)S(1)} %fence.1.refs_1_, bf16[128,1536]{1,0:T(8,128)(2,1)S(1)} %collective-permute-done.1.refs_2_, bf16[128,1536]{1,0:T(8,128)(2,1)S(1)} %collective-permute-done.2.refs_3_, ...), custom_call_target="tpu_custom_call" | custom-call | tf_op jit(solution)/shard_map/polar/pallas_call | solution.py:212
  70.4 0.0 copy-start.1
  70.4 0.0 copy-start.5
  70.4 0.0 copy-start.6
  70.4 26.6 %all_to_all.17.x_ref = bf16[64,2,16,128]{3,2,1,0:T(8,128)(2,1)S(1)} all-to-all(bf16[64,2,16,128]{3,2,1,0:T(8,128)(2,1)S(1)} %polar.1), channel_id=1, replica_groups=mesh['xh'=2,'z2'=2,'z1'=2,'z0'=2,'c'=2,'xl'=2,'y1'=2,'y0'=2] {'z1','xl',..., dimensions={0} | all-to-all | bytes 1048576 | tf_op jit(solution)/shard_map/all_to_all | solution.py:356
  97.0 0.0 copy-done.1
  97.0 0.0 copy-done.5
  97.0 0.0 copy-done.6
  97.0 2.5 %finish.1 = (f32[32,4,1024]{2,1,0:T(4,128)}, f32[32,4,1024]{2,1,0:T(4,128)}) custom-call(bf16[64,2,16,128]{3,2,1,0:T(8,128)(2,1)S(1)} %all_to_all.17.x_ref, bf16[512,512]{1,0:T(8,128)(2,1)S(1)} %copy-done.1, bf16[256,256]{1,0:T(8,128)(2,1)S(1)} %copy-done.6, bf16[256,256]{1,0:T(8,128)(2,1)S(1)} %copy-done.5), custom_call_target="tpu_custom_call" | custom-call | tf_op jit(solution)/shard_map/finish/pallas_call | solution.py:283
  (9 shorter events, 0.2 us)
Async XLA Ops:
  2.4 10.8 %copy-start = (bf16[32,4096]{1,0:T(8,128)(2,1)S(1)}, bf16[32,4096]{1,0:T(8,128)(2,1)}, u32[]{:S(2)}) copy-start(bf16[32,4096]{1,0:T(8,128)(2,1)} %occ_ref.1) | copy-start | bytes 786436
  2.4 10.8 %copy-start.2 = (bf16[16,4096]{1,0:T(8,128)(2,1)S(1)}, bf16[16,4096]{1,0:T(8,128)(2,1)}, u32[]{:S(2)}) copy-start(bf16[16,4096]{1,0:T(8,128)(2,1)} %vir_ref.1) | copy-start | bytes 393220
  44.9 9.9 %collective-permute-start.1 = (bf16[128,1536]{1,0:T(8,128)(2,1)S(1)}, bf16[128,1536]{1,0:T(8,128)(2,1)S(1)}, u32[]{:S(2)}, u32[]{:S(2)}) collective-permute-start(bf16[128,1536]{1,0:T(8,128)(2,1)S(1)} %turn.1.refs_0_), channel_id=1, source_target_pairs={{0,16},{16,0},{1,17},{17,1},{2,18},{18,2},{3,19},{19,3},{4,20},{20... | collective-permute-start | bytes 1179656 | tf_op jit(solution)/shard_map/ppermute | solution.py:332
  45.7 11.7 %collective-permute-start = (bf16[128,1536]{1,0:T(8,128)(2,1)S(1)}, bf16[128,1536]{1,0:T(8,128)(2,1)S(1)}, u32[]{:S(2)}, u32[]{:S(2)}) collective-permute-start(bf16[128,1536]{1,0:T(8,128)(2,1)S(1)} %turn.1.refs_0_), channel_id=1, source_target_pairs={{0,8},{8,0},{1,9},{9,1},{2,10},{10,2},{3,11},{11,3},{4,12},{12,4},... | collective-permute-start | bytes 1179656 | tf_op jit(solution)/shard_map/ppermute | solution.py:332
  54.9 13.8 %collective-permute-start.2 = (bf16[128,1536]{1,0:T(8,128)(2,1)S(1)}, bf16[128,1536]{1,0:T(8,128)(2,1)S(1)}, u32[]{:S(2)}, u32[]{:S(2)}) collective-permute-start(bf16[128,1536]{1,0:T(8,128)(2,1)S(1)} %collective-permute-done.1.refs_2_), channel_id=1, source_target_pairs={{0,8},{8,0},{1,9},{9,1},{2,10},{10,2},{3,11},{11,3},{4,12},{12,4},... | collective-permute-start | bytes 1179656 | tf_op jit(solution)/shard_map/ppermute | solution.py:332
  54.9 13.8 %copy-start.3 = (bf16[512,256]{1,0:T(8,128)(2,1)S(1)}, bf16[512,256]{1,0:T(8,128)(2,1)}, u32[]{:S(2)}) copy-start(bf16[512,256]{1,0:T(8,128)(2,1)} %constant.11.clone.refs_9_) | copy-start | bytes 786436
  54.9 13.8 %copy-start.4 = (bf16[512,256]{1,0:T(8,128)(2,1)S(1)}, bf16[512,256]{1,0:T(8,128)(2,1)}, u32[]{:S(2)}) copy-start(bf16[512,256]{1,0:T(8,128)(2,1)} %constant.10.clone.refs_8_) | copy-start | bytes 786436
  55.0 7.8 %collective-permute-start.5 = (bf16[768,128]{1,0:T(8,128)(2,1)S(1)}, bf16[768,128]{1,0:T(8,128)(2,1)S(1)}, u32[]{:S(2)}, u32[]{:S(2)}) collective-permute-start(bf16[768,128]{1,0:T(8,128)(2,1)S(1)} %pad_maximum_fusion.1.refs_4_), channel_id=1, source_target_pairs={{0,3},{1,0},{2,1},{3,2},{4,7},{5,4},{6,5},{7,6},{8,11},{9,8},{10,9... | collective-permute-start | bytes 589832 | tf_op jit(solution)/shard_map/ppermute | solution.py:328
  56.0 9.3 %collective-permute-start.4 = (bf16[768,128]{1,0:T(8,128)(2,1)S(1)}, bf16[768,128]{1,0:T(8,128)(2,1)S(1)}, u32[]{:S(2)}, u32[]{:S(2)}) collective-permute-start(bf16[768,128]{1,0:T(8,128)(2,1)S(1)} %pad_maximum_fusion.1.refs_4_), channel_id=1, source_target_pairs={{0,2},{1,3},{2,0},{3,1},{4,6},{5,7},{6,4},{7,5},{8,10},{9,11},{10,... | collective-permute-start | bytes 589832 | tf_op jit(solution)/shard_map/ppermute | solution.py:328
  57.4 11.3 %collective-permute-start.3 = (bf16[768,128]{1,0:T(8,128)(2,1)S(1)}, bf16[768,128]{1,0:T(8,128)(2,1)S(1)}, u32[]{:S(2)}, u32[]{:S(2)}) collective-permute-start(bf16[768,128]{1,0:T(8,128)(2,1)S(1)} %pad_maximum_fusion.1.refs_4_), channel_id=1, source_target_pairs={{0,1},{1,2},{2,3},{3,0},{4,5},{5,6},{6,7},{7,4},{8,9},{9,10},{10,1... | collective-permute-start | bytes 589832 | tf_op jit(solution)/shard_map/ppermute | solution.py:328
  70.4 26.6 %copy-start.1 = (bf16[512,512]{1,0:T(8,128)(2,1)S(1)}, bf16[512,512]{1,0:T(8,128)(2,1)}, u32[]{:S(2)}) copy-start(bf16[512,512]{1,0:T(8,128)(2,1)} %constant.12.clone.a_ref) | copy-start | bytes 1572868
  70.4 26.6 %copy-start.5 = (bf16[256,256]{1,0:T(8,128)(2,1)S(1)}, bf16[256,256]{1,0:T(8,128)(2,1)}, u32[]{:S(2)}) copy-start(bf16[256,256]{1,0:T(8,128)(2,1)} %constant.14.clone.b_low_ref) | copy-start | bytes 393220
  70.4 26.6 %copy-start.6 = (bf16[256,256]{1,0:T(8,128)(2,1)S(1)}, bf16[256,256]{1,0:T(8,128)(2,1)}, u32[]{:S(2)}) copy-start(bf16[256,256]{1,0:T(8,128)(2,1)} %constant.13.clone.b_high_ref) | copy-start | bytes 393220

commit v9 on v8

--- a/solution.py
+++ b/solution.py
@@ -12,8 +12,7 @@
 NOCC = 1024
 NVIR = 512
 NGRID = 32768
-POLAR_FACTOR = -1.0 / math.sqrt(NOCC * NVIR)
-NORMAL = 1.0 / math.sqrt(NGRID)
+POLAR_FACTOR = -1.0 / math.sqrt(NOCC * NVIR) / math.sqrt(NGRID)
 Z = ("z2", "z1", "z0")
 Y = ("y1", "y0")
 ROW = ("xh", *Z, "c")
@@ -34,12 +33,6 @@
     return place
 
 
-def split_table(table):
-    high = table.astype(np.float32).astype(jnp.bfloat16)
-    low = (table - high.astype(np.float64)).astype(np.float32).astype(jnp.bfloat16)
-    return high, low
-
-
 def rotation(phase):
     cosine, sine = np.cos(phase), np.sin(phase)
     return np.array([[cosine, sine], [-sine, cosine]])
@@ -49,7 +42,7 @@
     kc = np.arange(32).reshape(8, 4)
     turn = rotation(2 * np.pi * (kc[..., None] * np.arange(32) % 32) / 32)[:, 0]
     full = np.einsum("pjic,bd->ijpbdc", turn, np.eye(8))
-    return split_table(full.reshape(512, 256))
+    return full.reshape(512, 256).astype(BF16)
 
 
 def a_table():
@@ -57,15 +50,15 @@
     turn = rotation(2 * np.pi * (ka[:, None] * ka[None, :] % 32) / 32)
     turn = turn.reshape(2, 2, 8, 4, 8, 4)
     full = np.einsum("pqghck,bd->ghpbkcqd", turn, np.eye(8))
-    return split_table(full.reshape(512, 512))
+    return full.reshape(512, 512).astype(BF16)
 
 
 def b_table():
     kb = np.arange(32)
-    turn = rotation(2 * np.pi * (kb[:, None] * kb[None, :] % 32) / 32) * NORMAL
+    turn = rotation(2 * np.pi * (kb[:, None] * kb[None, :] % 32) / 32)
     turn = turn.reshape(2, 2, 32, 4, 8)
     full = np.einsum("pqkBb,hj->Bhqbpjk", turn, np.eye(4))
-    return split_table(full.reshape(256, 256))
+    return full.reshape(256, 256).astype(BF16)
 
 
 def dot(a, b):
@@ -169,7 +162,7 @@
 
 
 def polar_kernel(*refs):
-    points, near, (high_ref, low_ref) = refs[:4], refs[4:8], refs[8:10]
+    points, near, table_ref = refs[:4], refs[4:8], refs[8]
     out_ref, polar_ref, occ_ref, vir_ref = refs[-4:]
     core, z0, y = (lax.axis_index(axes) for axes in ("c", "z0", Y))
     for step in range(4):
@@ -195,11 +188,8 @@
         polar = polar_ref[256 * half : 256 * (half + 1), :]
         polar_high = polar.astype(BF16)
         polar_low = (polar - polar_high.astype(F32)).astype(BF16)
-        spectrum = (
-            dot(high_ref[...], polar_high)
-            + dot(high_ref[...], polar_low)
-            + dot(low_ref[...], polar_high)
-        ).astype(BF16)
+        spectrum = dot(table_ref[...], polar_high) + dot(table_ref[...], polar_low)
+        spectrum = spectrum.astype(BF16)
         for m in range(8):
             pieces = [spectrum[128 * i : 128 * (i + 1), 32 * m : 32 * (m + 1)] for i in range(4)]
             message = jnp.concatenate(pieces, axis=1)
@@ -212,7 +202,7 @@
     return pl.pallas_call(
         polar_kernel,
         out_shape=jax.ShapeDtypeStruct((64, 2, 16, 128), BF16),
-        in_specs=[vmem] * 10,
+        in_specs=[vmem] * 9,
         out_specs=vmem,
         scratch_shapes=[
             pltpu.VMEM((512, 256), F32),
@@ -224,7 +214,7 @@
     )(*arrays)
 
 
-def finish_kernel(x_ref, a_ref, b_high_ref, b_low_ref, *refs):
+def finish_kernel(x_ref, a_ref, b_ref, *refs):
     outs, parts, sems = refs[:2], refs[2:4], refs[4]
     x = jnp.concatenate(
         [
@@ -254,11 +244,7 @@
         )
         z_high = z.astype(BF16)
         z_low = (z - z_high.astype(F32)).astype(BF16)
-        out = (
-            dot(z_high, b_high_ref[...])
-            + dot(z_high, b_low_ref[...])
-            + dot(z_low, b_high_ref[...])
-        )
+        out = dot(z_high, b_ref[...]) + dot(z_low, b_ref[...])
         for which in range(2):
             for g in range(2):
                 for i in range(4):
@@ -283,7 +269,7 @@
     return pl.pallas_call(
         finish_kernel,
         out_shape=(shape, shape),
-        in_specs=[vmem] * 4,
+        in_specs=[vmem] * 3,
         out_specs=(hbm, hbm),
         scratch_shapes=[
             pltpu.VMEM((32, 4, 1024), F32),
@@ -351,10 +337,10 @@
     beside = fence(beside)
     opposite = swap(across, "c")
     points = (own, beside, across, opposite)
-    messages = polar_messages(*points, *near, *c_table())
+    messages = polar_messages(*points, *near, c_table())
 
     received = lax.all_to_all(messages, LAST, 0, 0, tiled=True)
-    return finish(received, a_table()[0], *b_table())
+    return finish(received, a_table(), b_table())
 
 
 def solution(mesh):

time: 99.8 us -> 99.6 us (level)
  no operation moved by 1% of the time
where the time goes in v9:
time: 99.6 us; the launch traced here: 99.3 us
  blocking collectives  68.7 us (69%)
  waiting for transfers between devices  20.4 us (20%)
  Pallas kernels  5.92 us (6%)
  starting transfers between devices  3.24 us (3%)
    all_to_all x1, blocking collectives, body(): arrived = lax.all_to_all(pack(occ, vir, scattered), ROW, 0, 0, tiled=True)  31.3 us
    all_to_all x1, blocking collectives, body(): received = lax.all_to_all(messages, LAST, 0, 0, tiled=True)  26.6 us
    ppermute x3, waiting for transfers between devices, shift(): return lax.ppermute(x, axes, [(i, (i + by) % count) for i in range(count)])  11.3 us
    all_to_all x1, blocking collectives, body(): lax.all_to_all(prepare(occ_decay, vir_decay, occ, vir), COL, 0, 0, tiled=...  10.8 us
    ppermute x3, waiting for transfers between devices, swap(): return lax.ppermute(x, axis, [(0, 1), (1, 0)])  9.18 us
    ppermute x3, starting transfers between devices, shift(): return lax.ppermute(x, axes, [(i, (i + by) % count) for i in range(count)])  2.48 us
    pallas_call x1, Pallas kernels, finish(): pl.pallas_call(finish_kernel, out_shape=(shape, shape), in_specs=[vmem] *...  2.41 us
  transfers between devices with their start and end apart: 6, of which 4 were waited for; matrix products, arithmetic and copies ran while one was open for 0% of the time, Pallas kernels for 0%

profile of v9, /device:TPU:32, one launch (start us, length us, event | category | flops | bytes accessed | tf_op | source)
XLA Modules:
  0.0 99.3 jit_solution(123916097337697999)
XLA Ops:
  0.6 1.8 %prepare.1 = bf16[8,4,24,128]{3,2,1,0:T(8,128)(2,1)} custom-call(f32[1024]{0:T(1024)} %refs_0_.1, f32[512]{0:T(512)} %refs_1_.1, bf16[32,4096]{1,0:T(8,128)(2,1)} %occ_ref.1, bf16[16,4096]{1,0:T(8,128)(2,1)} %vir_ref.1), custom_call_target="tpu_custom_call" | custom-call | tf_op jit(solution)/shard_map/prepare/pallas_call | solution.py:128
  2.4 0.0 copy-start
  2.4 0.0 copy-start.2
  2.4 10.8 %all_to_all.15.rows_ref = bf16[8,4,24,128]{3,2,1,0:T(8,128)(2,1)S(1)} all-to-all(bf16[8,4,24,128]{3,2,1,0:T(8,128)(2,1)} %prepare.1), channel_id=1, replica_groups=mesh['xh'=2,'z2'=2,'z1'=2,'z0'=2,'c'=2,'xl'=2,'y1'=2,'y0'=2] {'xl','y1',..., dimensions={0} | all-to-all | bytes 393216 | tf_op jit(solution)/shard_map/all_to_all | solution.py:322
  13.2 0.0 copy-done
  13.2 0.0 copy-done.2
  13.2 0.1 pack.1
  13.3 31.3 %all_to_all.16 = bf16[32,72,128]{2,1,0:T(8,128)(2,1)S(1)} all-to-all(bf16[32,72,128]{2,1,0:T(8,128)(2,1)S(1)} %pack.1), channel_id=1, replica_groups=mesh['xh'=2,'z2'=2,'z1'=2,'z0'=2,'c'=2,'xl'=2,'y1'=2,'y0'=2] {'xh','z2',..., dimensions={0} | all-to-all | bytes 1179648 | tf_op jit(solution)/shard_map/all_to_all | solution.py:323
  44.8 0.2 turn.1.refs_0_
  44.9 0.8 collective-permute-start.1
  45.7 0.0 collective-permute-start
  45.7 9.2 %collective-permute-done.1.refs_2_ = bf16[128,1536]{1,0:T(8,128)(2,1)S(1)} collective-permute-done((bf16[128,1536]{1,0:T(8,128)(2,1)S(1)}, bf16[128,1536]{1,0:T(8,128)(2,1)S(1)}, u32[]{:S(2)}, u32[]{:S(2)}) %collective-permute-start.1) | collective-permute-done | bytes 393248 | tf_op jit(solution)/shard_map/ppermute | solution.py:318
  54.9 0.0 collective-permute-start.2
  54.9 0.0 copy-start.3
  54.9 1.0 %collective-permute-start.5 = (bf16[768,128]{1,0:T(8,128)(2,1)S(1)}, bf16[768,128]{1,0:T(8,128)(2,1)S(1)}, u32[]{:S(2)}, u32[]{:S(2)}) collective-permute-start(bf16[768,128]{1,0:T(8,128)(2,1)S(1)} %pad_maximum_fusion.1.refs_4_), channel_id=1, source_target_pairs={{0,3},{1,0},{2,1},{3,2},{4,7},{5,4},{6,5},{7,6},{8,11},{9,8},{10,9... | collective-permute-start | bytes 589832 | tf_op jit(solution)/shard_map/ppermute | solution.py:314
  56.0 1.5 %collective-permute-start.4 = (bf16[768,128]{1,0:T(8,128)(2,1)S(1)}, bf16[768,128]{1,0:T(8,128)(2,1)S(1)}, u32[]{:S(2)}, u32[]{:S(2)}) collective-permute-start(bf16[768,128]{1,0:T(8,128)(2,1)S(1)} %pad_maximum_fusion.1.refs_4_), channel_id=1, source_target_pairs={{0,2},{1,3},{2,0},{3,1},{4,6},{5,7},{6,4},{7,5},{8,10},{9,11},{10,... | collective-permute-start | bytes 589832 | tf_op jit(solution)/shard_map/ppermute | solution.py:314
  57.4 0.0 collective-permute-start.3
  57.4 0.0 collective-permute-done.in_ref
  57.4 5.4 %collective-permute-done.5.refs_7_ = bf16[768,128]{1,0:T(8,128)(2,1)S(1)} collective-permute-done((bf16[768,128]{1,0:T(8,128)(2,1)S(1)}, bf16[768,128]{1,0:T(8,128)(2,1)S(1)}, u32[]{:S(2)}, u32[]{:S(2)}) %collective-permute-start.5) | collective-permute-done | bytes 196640 | tf_op jit(solution)/shard_map/ppermute | solution.py:314
  62.8 2.5 %collective-permute-done.4.refs_6_ = bf16[768,128]{1,0:T(8,128)(2,1)S(1)} collective-permute-done((bf16[768,128]{1,0:T(8,128)(2,1)S(1)}, bf16[768,128]{1,0:T(8,128)(2,1)S(1)}, u32[]{:S(2)}, u32[]{:S(2)}) %collective-permute-start.4) | collective-permute-done | bytes 196640 | tf_op jit(solution)/shard_map/ppermute | solution.py:314
  65.3 3.4 %collective-permute-done.3.refs_5_ = bf16[768,128]{1,0:T(8,128)(2,1)S(1)} collective-permute-done((bf16[768,128]{1,0:T(8,128)(2,1)S(1)}, bf16[768,128]{1,0:T(8,128)(2,1)S(1)}, u32[]{:S(2)}, u32[]{:S(2)}) %collective-permute-start.3) | collective-permute-done | bytes 196640 | tf_op jit(solution)/shard_map/ppermute | solution.py:314
  68.7 0.0 collective-permute-done.2.refs_3_
  68.7 0.0 copy-done.3
  68.7 1.5 %polar.1 = bf16[64,2,16,128]{3,2,1,0:T(8,128)(2,1)S(1)} custom-call(bf16[128,1536]{1,0:T(8,128)(2,1)S(1)} %turn.1.refs_0_, bf16[128,1536]{1,0:T(8,128)(2,1)S(1)} %fence.1.refs_1_, bf16[128,1536]{1,0:T(8,128)(2,1)S(1)} %collective-permute-done.1.refs_2_, bf16[128,1536]{1,0:T(8,128)(2,1)S(1)} %collective-permute-done.2.refs_3_, ...), custom_call_target="tpu_custom_call" | custom-call | tf_op jit(solution)/shard_map/polar/pallas_call | solution.py:202
  70.2 0.0 copy-start.1
  70.2 0.0 copy-start.4
  70.2 26.6 %all_to_all.17.x_ref = bf16[64,2,16,128]{3,2,1,0:T(8,128)(2,1)S(1)} all-to-all(bf16[64,2,16,128]{3,2,1,0:T(8,128)(2,1)S(1)} %polar.1), channel_id=1, replica_groups=mesh['xh'=2,'z2'=2,'z1'=2,'z0'=2,'c'=2,'xl'=2,'y1'=2,'y0'=2] {'z1','xl',..., dimensions={0} | all-to-all | bytes 1048576 | tf_op jit(solution)/shard_map/all_to_all | solution.py:342
  96.8 0.0 copy-done.1
  96.8 0.0 copy-done.4
  96.9 2.4 %finish.1 = (f32[32,4,1024]{2,1,0:T(4,128)}, f32[32,4,1024]{2,1,0:T(4,128)}) custom-call(bf16[64,2,16,128]{3,2,1,0:T(8,128)(2,1)S(1)} %all_to_all.17.x_ref, bf16[512,512]{1,0:T(8,128)(2,1)S(1)} %copy-done.1, bf16[256,256]{1,0:T(8,128)(2,1)S(1)} %copy-done.4), custom_call_target="tpu_custom_call" | custom-call | tf_op jit(solution)/shard_map/finish/pallas_call | solution.py:269
  (9 shorter events, 0.2 us)
Async XLA Ops:
  2.4 10.8 %copy-start = (bf16[32,4096]{1,0:T(8,128)(2,1)S(1)}, bf16[32,4096]{1,0:T(8,128)(2,1)}, u32[]{:S(2)}) copy-start(bf16[32,4096]{1,0:T(8,128)(2,1)} %occ_ref.1) | copy-start | bytes 786436
  2.4 10.8 %copy-start.2 = (bf16[16,4096]{1,0:T(8,128)(2,1)S(1)}, bf16[16,4096]{1,0:T(8,128)(2,1)}, u32[]{:S(2)}) copy-start(bf16[16,4096]{1,0:T(8,128)(2,1)} %vir_ref.1) | copy-start | bytes 393220
  44.9 9.9 %collective-permute-start.1 = (bf16[128,1536]{1,0:T(8,128)(2,1)S(1)}, bf16[128,1536]{1,0:T(8,128)(2,1)S(1)}, u32[]{:S(2)}, u32[]{:S(2)}) collective-permute-start(bf16[128,1536]{1,0:T(8,128)(2,1)S(1)} %turn.1.refs_0_), channel_id=1, source_target_pairs={{0,16},{16,0},{1,17},{17,1},{2,18},{18,2},{3,19},{19,3},{4,20},{20... | collective-permute-start | bytes 1179656 | tf_op jit(solution)/shard_map/ppermute | solution.py:318
  45.7 11.7 %collective-permute-start = (bf16[128,1536]{1,0:T(8,128)(2,1)S(1)}, bf16[128,1536]{1,0:T(8,128)(2,1)S(1)}, u32[]{:S(2)}, u32[]{:S(2)}) collective-permute-start(bf16[128,1536]{1,0:T(8,128)(2,1)S(1)} %turn.1.refs_0_), channel_id=1, source_target_pairs={{0,8},{8,0},{1,9},{9,1},{2,10},{10,2},{3,11},{11,3},{4,12},{12,4},... | collective-permute-start | bytes 1179656 | tf_op jit(solution)/shard_map/ppermute | solution.py:318
  54.9 13.8 %collective-permute-start.2 = (bf16[128,1536]{1,0:T(8,128)(2,1)S(1)}, bf16[128,1536]{1,0:T(8,128)(2,1)S(1)}, u32[]{:S(2)}, u32[]{:S(2)}) collective-permute-start(bf16[128,1536]{1,0:T(8,128)(2,1)S(1)} %collective-permute-done.1.refs_2_), channel_id=1, source_target_pairs={{0,8},{8,0},{1,9},{9,1},{2,10},{10,2},{3,11},{11,3},{4,12},{12,4},... | collective-permute-start | bytes 1179656 | tf_op jit(solution)/shard_map/ppermute | solution.py:318
  54.9 13.8 %copy-start.3 = (bf16[512,256]{1,0:T(8,128)(2,1)S(1)}, bf16[512,256]{1,0:T(8,128)(2,1)}, u32[]{:S(2)}) copy-start(bf16[512,256]{1,0:T(8,128)(2,1)} %constant.6.clone.refs_8_) | copy-start | bytes 786436
  54.9 7.8 %collective-permute-start.5 = (bf16[768,128]{1,0:T(8,128)(2,1)S(1)}, bf16[768,128]{1,0:T(8,128)(2,1)S(1)}, u32[]{:S(2)}, u32[]{:S(2)}) collective-permute-start(bf16[768,128]{1,0:T(8,128)(2,1)S(1)} %pad_maximum_fusion.1.refs_4_), channel_id=1, source_target_pairs={{0,3},{1,0},{2,1},{3,2},{4,7},{5,4},{6,5},{7,6},{8,11},{9,8},{10,9... | collective-permute-start | bytes 589832 | tf_op jit(solution)/shard_map/ppermute | solution.py:314
  56.0 9.3 %collective-permute-start.4 = (bf16[768,128]{1,0:T(8,128)(2,1)S(1)}, bf16[768,128]{1,0:T(8,128)(2,1)S(1)}, u32[]{:S(2)}, u32[]{:S(2)}) collective-permute-start(bf16[768,128]{1,0:T(8,128)(2,1)S(1)} %pad_maximum_fusion.1.refs_4_), channel_id=1, source_target_pairs={{0,2},{1,3},{2,0},{3,1},{4,6},{5,7},{6,4},{7,5},{8,10},{9,11},{10,... | collective-permute-start | bytes 589832 | tf_op jit(solution)/shard_map/ppermute | solution.py:314
  57.4 11.3 %collective-permute-start.3 = (bf16[768,128]{1,0:T(8,128)(2,1)S(1)}, bf16[768,128]{1,0:T(8,128)(2,1)S(1)}, u32[]{:S(2)}, u32[]{:S(2)}) collective-permute-start(bf16[768,128]{1,0:T(8,128)(2,1)S(1)} %pad_maximum_fusion.1.refs_4_), channel_id=1, source_target_pairs={{0,1},{1,2},{2,3},{3,0},{4,5},{5,6},{6,7},{7,4},{8,9},{9,10},{10,1... | collective-permute-start | bytes 589832 | tf_op jit(solution)/shard_map/ppermute | solution.py:314
  70.2 26.6 %copy-start.1 = (bf16[512,512]{1,0:T(8,128)(2,1)S(1)}, bf16[512,512]{1,0:T(8,128)(2,1)}, u32[]{:S(2)}) copy-start(bf16[512,512]{1,0:T(8,128)(2,1)} %constant.7.clone.a_ref) | copy-start | bytes 1572868
  70.2 26.6 %copy-start.4 = (bf16[256,256]{1,0:T(8,128)(2,1)S(1)}, bf16[256,256]{1,0:T(8,128)(2,1)}, u32[]{:S(2)}) copy-start(bf16[256,256]{1,0:T(8,128)(2,1)} %constant.8.clone.b_ref) | copy-start | bytes 393220
